TPU v7x, 768 devices: a whole 4x8x12 slice. The times are simulated.
768 devices in a mesh: pipe: 12 (over z), expert: 16 (over y, x_hi), tensor: 4 (over x_lo, core).
Axes of the slice: x: 4 (x_hi: 2, x_lo: 2; x = x_hi * 2 + x_lo), y: 8, z: 12, core: 2. Of those that a mesh axis runs over, the one named last changes fastest.
Arguments:
- inputs_prev: bfloat16 [12, 2048, 3584], P('pipe', 'expert', 'tensor'), may hold values from -6 to 6
- cotangent_next: bfloat16 [12, 2048, 3584], P('pipe', 'expert', 'tensor'), may hold values from -6 to 6
- saved_input: bfloat16 [12, 2048, 3584], P('pipe', 'expert', 'tensor'), may hold values from -6 to 6
- expert_ids: int32 [2, 12, 2048, 8], P(None, 'pipe', 'expert'), may hold values from 0 to 255, as said below
- keep_mask: int32 [2, 12, 2048, 8], P(None, 'pipe', 'expert'), may hold values from 0 to 1, as said below
- slot_pos: int32 [2, 12, 2048, 8], P(None, 'pipe', 'expert'), may hold values from 0 to 3, as said below
- weight_q: int32 [2, 12, 2048, 8], P(None, 'pipe', 'expert'), may hold values from 1 to 4095
- gate_routed: bfloat16 [12, 16, 3584, 512], P('pipe', 'expert', None, 'tensor'), may hold values from -0.09375 to 0.09375
- up_routed: bfloat16 [12, 16, 3584, 512], P('pipe', 'expert', None, 'tensor'), may hold values from -0.09375 to 0.09375
- down_routed: bfloat16 [12, 16, 512, 3584], P('pipe', 'expert', 'tensor'), may hold values from -0.1875 to 0.1875
- gate_shared: bfloat16 [12, 3584, 1024], P('pipe', None, 'tensor'), may hold values from -0.09375 to 0.09375
- up_shared: bfloat16 [12, 3584, 1024], P('pipe', None, 'tensor'), may hold values from -0.09375 to 0.09375
- down_shared: bfloat16 [12, 1024, 3584], P('pipe', 'tensor'), may hold values from -0.1875 to 0.1875
Outputs:
- out_act: bfloat16 [12, 2048, 3584], P('pipe', 'expert', 'tensor')
- in_grad: bfloat16 [12, 2048, 3584], P('pipe', 'expert', 'tensor')
Inputs may be any that keep to these rules, and one draw needn't show every extreme that they name: `expert_ids`: each row names 8 different experts; in every section and micro-batch one expert below 8 is named by every row. `keep_mask`: 1 only where the expert named is below 8; in one block of 128 rows no expert has more than 4 kept choices, and in every section and micro-batch one expert has exactly 4 in every block. `slot_pos`: kept choices of one block naming the same expert hold different slots; 0 where keep_mask is 0.
All inputs are finite; a program needn't handle non-finite values.
Results may differ from a plain program's by a relative error of at most 0.005.
Values may be sent and summed in bfloat16 or wider, within the bound.
No kernel may reach another device: no remote copies, remote signals or barrier semaphores. Data moves between devices by JAX's collectives and lax.ppermute only.
A program may use at most 64 MiB of HBM per device.

v0:
```python
import jax
import jax.numpy as jnp
from jax import lax
from jax.sharding import PartitionSpec as P


def passed_along(block, axis, distance):
    devices = range(lax.axis_size(axis))
    route = [((i - distance) % len(devices), i) for i in devices]
    return lax.ppermute(block, axis, route)


def swish(values):
    return values * jax.nn.sigmoid(values)


def swish_slope(values):
    logistic = jax.nn.sigmoid(values)
    return logistic * (1.0 + values * (1.0 - logistic))


def contract_last(left, right):
    return lax.dot_general(
        left, right, (((1,), (1,)), ((), ())), preferred_element_type=jnp.float32
    )


def slot_plan(choice_ids, kept_flags, slot_index, weight_levels, experts_here, capacity):
    total_slots = experts_here * capacity
    target = jnp.where(kept_flags > 0, choice_ids * capacity + slot_index, total_slots).reshape(-1)
    source = jnp.broadcast_to(
        jnp.arange(choice_ids.shape[0], dtype=jnp.int32)[:, None], choice_ids.shape
    ).reshape(-1)
    slot_token = jnp.zeros((total_slots,), jnp.int32).at[target].set(source, mode="drop")
    levels = (weight_levels.astype(jnp.float32) / 4096.0).reshape(-1)
    slot_weight = jnp.zeros((total_slots,), jnp.float32).at[target].set(levels, mode="drop")
    slot_live = jnp.zeros((total_slots,), jnp.float32).at[target].set(1.0, mode="drop")
    return (slot_token, slot_weight, slot_live)


def section_link(values, offset):
    return passed_along(values, "pipe", offset)


def build_parcels(
    values_in, values_saved, values_cot, plan_forward, plan_backward, experts_here, capacity
):
    token_f, weight_f, live_f = plan_forward
    token_b, weight_b, live_b = plan_backward
    rows_in = jnp.where(live_f[:, None] > 0, values_in[token_f], jnp.zeros((), values_in.dtype))
    rows_saved = jnp.where(
        live_b[:, None] > 0, values_saved[token_b], jnp.zeros((), values_saved.dtype)
    )
    rows_cot = (weight_b[:, None] * values_cot[token_b].astype(jnp.float32)).astype(jnp.bfloat16)

    def doubled(rows):
        columns = rows.shape[-1]
        lined = rows.reshape(experts_here, 1, capacity, columns)
        spread = jnp.broadcast_to(lined, (experts_here, 2, capacity, columns))
        return spread.reshape(2 * experts_here, capacity, columns)

    return (doubled(rows_in), doubled(rows_saved), doubled(rows_cot))


def expert_local(rows_in, rows_saved, rows_cot, gate_w, up_w, down_w):
    gate_pre = jnp.dot(rows_in, gate_w, preferred_element_type=jnp.float32)
    up_pre = jnp.dot(rows_in, up_w, preferred_element_type=jnp.float32)
    hidden = (swish(gate_pre) * up_pre).astype(jnp.bfloat16)
    result = jnp.dot(hidden, down_w, preferred_element_type=jnp.float32).astype(jnp.bfloat16)
    gate_back = jnp.dot(rows_saved, gate_w, preferred_element_type=jnp.float32)
    up_back = jnp.dot(rows_saved, up_w, preferred_element_type=jnp.float32)
    grad_hidden = contract_last(rows_cot, down_w)
    grad_gate = (grad_hidden * up_back * swish_slope(gate_back)).astype(jnp.bfloat16)
    grad_up = (grad_hidden * swish(gate_back)).astype(jnp.bfloat16)
    grad_rows = (contract_last(grad_gate, gate_w) + contract_last(grad_up, up_w)).astype(
        jnp.bfloat16
    )
    return (result, grad_rows)


def shared_pass(full_in, full_saved, full_cot, gate_w, up_w, down_w):
    gate_pre = jnp.dot(full_in, gate_w, preferred_element_type=jnp.float32)
    up_pre = jnp.dot(full_in, up_w, preferred_element_type=jnp.float32)
    hidden = (swish(gate_pre) * up_pre).astype(jnp.bfloat16)
    shared_out = jnp.dot(hidden, down_w, preferred_element_type=jnp.float32)
    gate_back = jnp.dot(full_saved, gate_w, preferred_element_type=jnp.float32)
    up_back = jnp.dot(full_saved, up_w, preferred_element_type=jnp.float32)
    grad_hidden = contract_last(full_cot, down_w)
    grad_gate = (grad_hidden * up_back * swish_slope(gate_back)).astype(jnp.bfloat16)
    grad_up = (grad_hidden * swish(gate_back)).astype(jnp.bfloat16)
    shared_grad = contract_last(grad_gate, gate_w) + contract_last(grad_up, up_w)
    return (shared_out, shared_grad)


def local(
    inputs_prev,
    cotangent_next,
    saved_input,
    expert_ids,
    keep_mask,
    slot_pos,
    weight_q,
    gate_routed,
    up_routed,
    down_routed,
    gate_shared,
    up_shared,
    down_shared,
):
    capacity = inputs_prev.shape[1] // 32
    experts_here = lax.axis_size("expert") // 2
    forward_in = section_link(inputs_prev[0], 1)
    backward_in = section_link(cotangent_next[0], -1)
    saved_rows = saved_input[0]
    plan_forward = slot_plan(
        expert_ids[0, 0], keep_mask[0, 0], slot_pos[0, 0], weight_q[0, 0], experts_here, capacity
    )
    plan_backward = slot_plan(
        expert_ids[1, 0], keep_mask[1, 0], slot_pos[1, 0], weight_q[1, 0], experts_here, capacity
    )
    gate_w = gate_routed[0, 0]
    up_w = up_routed[0, 0]
    down_w = down_routed[0, 0]
    full_in, full_saved, full_cot = (
        lax.all_gather(forward_in, "tensor", axis=1, tiled=True),
        lax.all_gather(saved_rows, "tensor", axis=1, tiled=True),
        lax.all_gather(backward_in, "tensor", axis=1, tiled=True),
    )
    parcel_in, parcel_saved, parcel_cot = build_parcels(
        full_in, full_saved, full_cot, plan_forward, plan_backward, experts_here, capacity
    )
    pieces = (
        lax.all_to_all(parcel_in, "expert", split_axis=0, concat_axis=0, tiled=True),
        lax.all_to_all(parcel_saved, "expert", split_axis=0, concat_axis=0, tiled=True),
        lax.all_to_all(parcel_cot, "expert", split_axis=0, concat_axis=0, tiled=True),
    )
    row_shape = pieces[0].shape
    feature_count = row_shape[2]
    result, grad_rows = expert_local(
        pieces[0].reshape(-1, feature_count),
        pieces[1].reshape(-1, feature_count),
        pieces[2].reshape(-1, feature_count),
        gate_w,
        up_w,
        down_w,
    )
    returned = (
        lax.all_to_all(
            result.reshape(row_shape), "expert", split_axis=0, concat_axis=0, tiled=True
        ),
        lax.all_to_all(
            grad_rows.reshape(row_shape), "expert", split_axis=0, concat_axis=0, tiled=True
        ),
    )
    back_out, back_grad = returned
    feature_count = full_in.shape[1]
    merged_out = (
        back_out.astype(jnp.float32)
        .reshape(experts_here, 2, capacity, feature_count)
        .sum(axis=1)
        .reshape(experts_here * capacity, feature_count)
    )
    merged_grad = (
        back_grad.astype(jnp.float32)
        .reshape(experts_here, 2, capacity, feature_count)
        .sum(axis=1)
        .reshape(experts_here * capacity, feature_count)
    )
    token_f, weight_f, live_f = plan_forward
    token_b, weight_b, live_b = plan_backward
    routed_out = (
        jnp.zeros(full_in.shape, jnp.float32).at[token_f].add(weight_f[:, None] * merged_out)
    )
    routed_grad = (
        jnp.zeros(full_in.shape, jnp.float32).at[token_b].add(live_b[:, None] * merged_grad)
    )
    shared_out, shared_grad = shared_pass(
        full_in, full_saved, full_cot, gate_shared[0], up_shared[0], down_shared[0]
    )
    summed_out, summed_grad = (
        lax.psum_scatter(routed_out + shared_out, "tensor", scatter_dimension=1, tiled=True),
        lax.psum_scatter(routed_grad + shared_grad, "tensor", scatter_dimension=1, tiled=True),
    )
    return (summed_out.astype(jnp.bfloat16)[None], summed_grad.astype(jnp.bfloat16)[None])


def solution(mesh):
    return jax.shard_map(
        local,
        mesh=mesh,
        in_specs=(
            P("pipe", "expert", "tensor"),
            P("pipe", "expert", "tensor"),
            P("pipe", "expert", "tensor"),
            P(None, "pipe", "expert", None),
            P(None, "pipe", "expert", None),
            P(None, "pipe", "expert", None),
            P(None, "pipe", "expert", None),
            P("pipe", "expert", None, "tensor"),
            P("pipe", "expert", None, "tensor"),
            P("pipe", "expert", "tensor", None),
            P("pipe", None, "tensor"),
            P("pipe", None, "tensor"),
            P("pipe", "tensor", None),
        ),
        out_specs=(P("pipe", "expert", "tensor"), P("pipe", "expert", "tensor")),
        check_vma=False,
    )
```

profile of v0, /device:TPU:1, one launch (start us, length us, event | category | flops | bytes accessed | tf_op | source)
XLA Modules:
  0.0 243.5 jit_solution(269399242853236374)
XLA Ops:
  8.4 4.3 %scatter_custom_fusion.4 = s32[32]{0:T(128)S(1)} fusion(s32[1024]{0:T(1024)S(1)} %bitcast.98, s32[1024]{0:T(1024)S(1)} %reshape.298, s32[]{:T(128)} %constant.9.clone.1), kind=kCustom, calls=%fused_computation.109 | custom fusion | bytes 132 | tf_op jit(solution)/shard_map/scatter | solution.py:34
  12.7 18.1 %all-gather = bf16[1,128,3584]{2,1,0:T(8,128)(2,1)S(1)} all-gather(bf16[1,128,896]{2,1,0:T(8,128)(2,1)} %param.15), channel_id=2, replica_groups=mesh['pipe'=12,'expert'=16,'tensor'=4] {'tensor'}, dimensions={2}, use_global_device_ids=true | all-gather | bytes 1146880 | tf_op jit(solution)/shard_map/all_gather | solution.py:126
  31.6 4.3 %scatter_custom_fusion.5 = f32[32]{0:T(128)S(1)} fusion(s32[1024]{0:T(1024)S(1)} %bitcast.99, f32[1024]{0:T(1024)S(1)} %broadcast.165, f32[]{:T(128)} %constant.13.clone.1), kind=kCustom, calls=%fused_computation.102 | custom fusion | bytes 132 | tf_op jit(solution)/shard_map/scatter | solution.py:37
  37.1 3.6 %all-to-all-start.3 = ((bf16[16,4,3584]{2,1,0:T(4,128)(2,1)}), bf16[16,4,3584]{2,1,0:T(4,128)(2,1)S(1)}, u32[]{:S(2)}, u32[]{:S(2)}) async-start(bf16[16,4,3584]{2,1,0:T(4,128)(2,1)} %bitcast.92), calls=%async_computation.4 | async-start | bytes 917504 | tf_op jit(solution)/shard_map/all_to_all | solution.py:134
  40.7 12.6 %collective-permute-start.1 = (bf16[128,896]{1,0:T(8,128)(2,1)}, bf16[128,896]{1,0:T(8,128)(2,1)S(1)}, u32[]{:S(2)}, u32[]{:S(2)}) collective-permute-start(bf16[128,896]{1,0:T(8,128)(2,1)} %bitcast.101), channel_id=1, source_target_pairs={{64,0},{128,64},{192,128},{256,192},{320,256},{384,320},{448,384},... | collective-permute-start | bytes 688136 | tf_op jit(solution)/shard_map/ppermute | solution.py:10
  53.3 1.9 collective-permute-start
  55.4 4.3 %scatter_custom_fusion = s32[32]{0:T(128)S(1)} fusion(s32[1024]{0:T(1024)S(1)} %bitcast.95, s32[1024]{0:T(1024)S(1)} %reshape.298, s32[]{:T(128)} %constant.9.clone.1), kind=kCustom, calls=%fused_computation.111 | custom fusion | bytes 132 | tf_op jit(solution)/shard_map/scatter | solution.py:34
  59.8 4.3 %scatter_custom_fusion.2 = f32[32]{0:T(128)S(1)} fusion(s32[1024]{0:T(1024)S(1)} %bitcast.96, f32[1024]{0:T(1024)S(1)} %broadcast.165, f32[]{:T(128)} %constant.13.clone.1), kind=kCustom, calls=%fused_computation.105 | custom fusion | bytes 132 | tf_op jit(solution)/shard_map/scatter | solution.py:37
  64.3 4.3 %scatter_custom_fusion.6 = f32[32]{0:T(128)S(1)} fusion(s32[1024]{0:T(1024)S(1)} %bitcast.100, f32[1024]{0:T(1024)S(1)} %reshape.314, f32[]{:T(128)} %constant.13.clone.1), kind=kCustom, calls=%fused_computation.100 | custom fusion | bytes 132 | tf_op jit(solution)/shard_map/scatter | solution.py:36
  68.8 9.9 %all_gather.10 = bf16[128,3584]{1,0:T(8,128)(2,1)} all-gather(bf16[128,896]{1,0:T(8,128)(2,1)S(1)} %collective-permute-done.1), channel_id=1, replica_groups=mesh['pipe'=12,'expert'=16,'tensor'=4] {'tensor'}, dimensions={1}, use_global_device_ids=true | all-gather | bytes 1146880 | tf_op jit(solution)/shard_map/all_gather | solution.py:127
  78.6 2.2 gather_fusion.1
  83.9 9.4 %all-to-all-start.2 = ((bf16[16,4,3584]{2,1,0:T(4,128)(2,1)}), bf16[16,4,3584]{2,1,0:T(4,128)(2,1)}, u32[]{:S(2)}, u32[]{:S(2)}) async-start(bf16[16,4,3584]{2,1,0:T(4,128)(2,1)} %bitcast.93), calls=%async_computation.3 | async-start | bytes 917504 | tf_op jit(solution)/shard_map/all_to_all | solution.py:135
  93.4 1.9 fusion.12
  97.9 12.0 %all-to-all-done.2 = bf16[16,4,3584]{2,1,0:T(4,128)(2,1)} async-done(((bf16[16,4,3584]{2,1,0:T(4,128)(2,1)}), bf16[16,4,3584]{2,1,0:T(4,128)(2,1)}, u32[]{:S(2)}, u32[]{:S(2)}) %all-to-all-start.2) | async-done | bytes 458784 | tf_op jit(solution)/shard_map/all_to_all | solution.py:135
  109.9 1.9 reshape.226
  113.6 3.1 %fusion.30 = f32[64,3584]{1,0:T(8,128)} fusion(f32[64,128]{1,0:T(8,128)S(1)} %fusion.31, bf16[64,3584]{1,0:T(8,128)(2,1)S(1)} %reshape.228, bf16[1,1,3584,128]{3,2,1,0:T(8,128)(2,1)} %param.21, bf16[1,1,3584,128]{3,2,1,0:T(8,128)(2,1)} %param.20, f32[64,128]{1,0:T(8,128)S(1)} %fusion.40), kind=kOutput, calls=%fused_computation.38 | convolution fusion | flops 117522432 | bytes 3276800 | tf_op jit(solution)/shard_map/dot_general | solution.py:23
  119.5 4.0 %all-to-all-start.4 = ((bf16[16,4,3584]{2,1,0:T(4,128)(2,1)}), bf16[16,4,3584]{2,1,0:T(4,128)(2,1)S(1)}, u32[]{:S(2)}, u32[]{:S(2)}) async-start(bf16[16,4,3584]{2,1,0:T(4,128)(2,1)} %reshape.229), calls=%async_computation.5 | async-start | bytes 917504 | tf_op jit(solution)/shard_map/all_to_all | solution.py:151
  123.8 2.5 %fusion.1 = f32[128,256]{1,0:T(8,128)S(1)} fusion(bf16[128,3584]{1,0:T(8,128)(2,1)} %all_gather.10, bf16[1,256,3584]{2,1,0:T(8,128)(2,1)} %param.25), kind=kOutput, calls=%fused_computation.15 | convolution fusion | flops 234881024 | bytes 2883584 | tf_op jit(solution)/shard_map/dot_general | solution.py:23
  126.3 4.1 %fusion.10 = f32[128,3584]{1,0:T(8,128)} fusion(bf16[1,3584,256]{2,1,0:T(8,128)(2,1)} %param.23, f32[128,256]{1,0:T(8,128)S(1)} %fusion.1, bf16[1,3584,256]{2,1,0:T(8,128)(2,1)S(1)} %copy-done, f32[128,256]{1,0:T(8,128)S(1)} %fusion.12, bf16[1,128,3584]{2,1,0:T(8,128)(2,1)S(1)} %all-gather), kind=kOutput, calls=%fused_computation.24 | convolution fusion | flops 470089728 | bytes 6684672 | tf_op jit(solution)/shard_map/dot_general | solution.py:23
  130.4 3.5 %convolution_add_fusion = f32[128,3584]{1,0:T(8,128)} fusion(f32[128,3584]{1,0:T(8,128)} %fusion.10, bf16[1,3584,256]{2,1,0:T(8,128)(2,1)S(1)} %copy-done, f32[128,256]{1,0:T(8,128)S(1)} %fusion.1, f32[128,256]{1,0:T(8,128)S(1)} %fusion.12), kind=kOutput, calls=%fused_computation.11 | convolution fusion | flops 235536384 | bytes 5767168 | tf_op jit(solution)/shard_map/dot_general | solution.py:23
  133.9 4.7 %all-to-all-done.4 = bf16[16,4,3584]{2,1,0:T(4,128)(2,1)S(1)} async-done(((bf16[16,4,3584]{2,1,0:T(4,128)(2,1)}), bf16[16,4,3584]{2,1,0:T(4,128)(2,1)S(1)}, u32[]{:S(2)}, u32[]{:S(2)}) %all-to-all-start.4) | async-done | bytes 458784 | tf_op jit(solution)/shard_map/all_to_all | solution.py:151
  139.0 4.0 %scatter_custom_fusion.7 = f32[128,3584]{1,0:T(8,128)} fusion(f32[128,3584]{1,0:T(8,128)} %convolution_add_fusion, s32[32]{0:T(128)S(1)} %compare_select_fusion.2, f32[32,3584]{1,0:T(8,128)S(1)} %reshape.232, f32[32]{0:T(128)S(1)} %scatter_custom_fusion.5), kind=kCustom, calls=%fused_computation.52 | custom fusion | flops 229376 | bytes 2294272 | tf_op jit(solution)/shard_map/scatter-add | solution.py:175
  143.0 11.5 %all_gather.9 = bf16[128,3584]{1,0:T(8,128)(2,1)S(1)} all-gather(bf16[128,896]{1,0:T(8,128)(2,1)} %collective-permute-done), channel_id=1, replica_groups=mesh['pipe'=12,'expert'=16,'tensor'=4] {'tensor'}, dimensions={1}, use_global_device_ids=true | all-gather | bytes 1146880 | tf_op jit(solution)/shard_map/all_gather | solution.py:125
  155.6 20.1 %all_to_all.25 = bf16[16,4,3584]{2,1,0:T(4,128)(2,1)} all-to-all(bf16[16,4,3584]{2,1,0:T(4,128)(2,1)S(1)} %bitcast.94), channel_id=1, replica_groups=mesh['pipe'=12,'expert'=16,'tensor'=4] {'expert'}, dimensions={0} | all-to-all | bytes 917504 | tf_op jit(solution)/shard_map/all_to_all | solution.py:133
  178.3 2.8 %convolution_convert_fusion = bf16[64,3584]{1,0:T(8,128)(2,1)} fusion(bf16[64,3584]{1,0:T(8,128)(2,1)S(1)} %reshape.220, bf16[1,1,128,3584]{3,2,1,0:T(8,128)(2,1)} %param.22, bf16[1,1,3584,128]{3,2,1,0:T(8,128)(2,1)} %param.21, f32[64,128]{1,0:T(8,128)S(1)} %fusion.42), kind=kOutput, calls=%fused_computation.13 | convolution fusion | flops 117719040 | bytes 2785280 | tf_op jit(solution)/shard_map/dot_general | solution.py:69
  181.1 1.9 reshape.221
  183.0 4.0 %all-to-all-start.1 = ((bf16[16,4,3584]{2,1,0:T(4,128)(2,1)}), bf16[16,4,3584]{2,1,0:T(4,128)(2,1)S(1)}, u32[]{:S(2)}, u32[]{:S(2)}) async-start(bf16[16,4,3584]{2,1,0:T(4,128)(2,1)} %reshape.221), calls=%async_computation.1 | async-start | bytes 917504 | tf_op jit(solution)/shard_map/all_to_all | solution.py:148
  187.3 4.3 %scatter_custom_fusion.1 = f32[32]{0:T(128)S(1)} fusion(s32[1024]{0:T(1024)S(1)} %bitcast.97, f32[1024]{0:T(1024)S(1)} %reshape.274, f32[]{:T(128)} %constant.13.clone.1), kind=kCustom, calls=%fused_computation.107 | custom fusion | bytes 132 | tf_op jit(solution)/shard_map/scatter | solution.py:36
  192.0 4.5 %fusion.3 = f32[128,3584]{1,0:T(8,128)} fusion(bf16[1,256,3584]{2,1,0:T(8,128)(2,1)} %param.25, f32[128,256]{1,0:T(8,128)S(1)} %fusion.8, bf16[128,3584]{1,0:T(8,128)(2,1)S(1)} %all_gather.9, bf16[1,3584,256]{2,1,0:T(8,128)(2,1)} %param.23), kind=kOutput, calls=%fused_computation.17 | convolution fusion | flops 469958656 | bytes 6553600 | tf_op jit(solution)/shard_map/dot_general | solution.py:85
  196.5 5.6 %all-to-all-done.1 = bf16[16,4,3584]{2,1,0:T(4,128)(2,1)S(1)} async-done(((bf16[16,4,3584]{2,1,0:T(4,128)(2,1)}), bf16[16,4,3584]{2,1,0:T(4,128)(2,1)S(1)}, u32[]{:S(2)}, u32[]{:S(2)}) %all-to-all-start.1) | async-done | bytes 458784 | tf_op jit(solution)/shard_map/all_to_all | solution.py:148
  202.6 4.0 %scatter_custom_fusion.3 = f32[128,3584]{1,0:T(8,128)} fusion(f32[128,3584]{1,0:T(8,128)} %fusion.3, s32[32]{0:T(128)S(1)} %compare_select_fusion.3, f32[32,3584]{1,0:T(8,128)S(1)} %reshape.224, f32[32]{0:T(128)S(1)} %scatter_custom_fusion.1), kind=kCustom, calls=%fused_computation.55 | custom fusion | flops 229376 | bytes 2294272 | tf_op jit(solution)/shard_map/scatter-add | solution.py:172
  208.3 26.7 %reduce-scatter.3.cloned.1.call-done = f32[128,896]{1,0:T(8,128)} async-done(((f32[128,3584]{1,0:T(8,128)}), f32[128,896]{1,0:T(8,128)}) %reduce-scatter.3.cloned.1.call-update) | async-done | bytes 458768 | tf_op jit(solution)/shard_map/reduce_scatter | solution.py:181
  (63 shorter events, 22.8 us)
Async XLA Ops:
  7.2 119.1 %copy-start = (bf16[1,3584,256]{2,1,0:T(8,128)(2,1)S(1)}, bf16[1,3584,256]{2,1,0:T(8,128)(2,1)}, u32[]{:S(2)}) copy-start(bf16[1,3584,256]{2,1,0:T(8,128)(2,1)} %param.24) | copy-start | bytes 5505028
  30.9 24.4 %copy-start.2 = (s32[2,1,128,8]{2,3,1,0:T(8,128)S(1)}, s32[2,1,128,8]{2,3,1,0:T(8,128)}, u32[]{:S(2)}) copy-start(s32[2,1,128,8]{2,3,1,0:T(8,128)} %param.19) | copy-start | bytes 24580
  37.1 45.8 %all-to-all-start.3 = ((bf16[16,4,3584]{2,1,0:T(4,128)(2,1)}), bf16[16,4,3584]{2,1,0:T(4,128)(2,1)S(1)}, u32[]{:S(2)}, u32[]{:S(2)}) async-start(bf16[16,4,3584]{2,1,0:T(4,128)(2,1)} %bitcast.92), calls=%async_computation.4 | async-start | bytes 917504 | tf_op jit(solution)/shard_map/all_to_all | solution.py:134
  40.7 28.1 %collective-permute-start.1 = (bf16[128,896]{1,0:T(8,128)(2,1)}, bf16[128,896]{1,0:T(8,128)(2,1)S(1)}, u32[]{:S(2)}, u32[]{:S(2)}) collective-permute-start(bf16[128,896]{1,0:T(8,128)(2,1)} %bitcast.101), channel_id=1, source_target_pairs={{64,0},{128,64},{192,128},{256,192},{320,256},{384,320},{448,384},... | collective-permute-start | bytes 688136 | tf_op jit(solution)/shard_map/ppermute | solution.py:10
  53.3 89.7 %collective-permute-start = (bf16[128,896]{1,0:T(8,128)(2,1)}, bf16[128,896]{1,0:T(8,128)(2,1)}, u32[]{:S(2)}, u32[]{:S(2)}) collective-permute-start(bf16[128,896]{1,0:T(8,128)(2,1)} %bitcast.102), channel_id=1, source_target_pairs={{704,0},{0,64},{64,128},{128,192},{192,256},{256,320},{320,384},{3... | collective-permute-start | bytes 688136 | tf_op jit(solution)/shard_map/ppermute | solution.py:10
  83.0 10.4 %copy-start.1 = (bf16[16,4,3584]{2,1,0:T(4,128)(2,1)}, bf16[16,4,3584]{2,1,0:T(4,128)(2,1)S(1)}, u32[]{:S(2)}) copy-start(bf16[16,4,3584]{2,1,0:T(4,128)(2,1)S(1)} %all-to-all-done.3) | copy-start | bytes 1376260
  83.9 26.0 %all-to-all-start.2 = ((bf16[16,4,3584]{2,1,0:T(4,128)(2,1)}), bf16[16,4,3584]{2,1,0:T(4,128)(2,1)}, u32[]{:S(2)}, u32[]{:S(2)}) async-start(bf16[16,4,3584]{2,1,0:T(4,128)(2,1)} %bitcast.93), calls=%async_computation.3 | async-start | bytes 917504 | tf_op jit(solution)/shard_map/all_to_all | solution.py:135
  119.5 19.0 %all-to-all-start.4 = ((bf16[16,4,3584]{2,1,0:T(4,128)(2,1)}), bf16[16,4,3584]{2,1,0:T(4,128)(2,1)S(1)}, u32[]{:S(2)}, u32[]{:S(2)}) async-start(bf16[16,4,3584]{2,1,0:T(4,128)(2,1)} %reshape.229), calls=%async_computation.5 | async-start | bytes 917504 | tf_op jit(solution)/shard_map/all_to_all | solution.py:151
  123.5 83.0 %reduce-scatter.5.cloned.1.call-start = ((), (), s32[]{:S(2)}) async-start(), calls=%async_computation.8 | async-start | bytes 2293760 | tf_op jit(solution)/shard_map/reduce_scatter | solution.py:182
  183.0 19.1 %all-to-all-start.1 = ((bf16[16,4,3584]{2,1,0:T(4,128)(2,1)}), bf16[16,4,3584]{2,1,0:T(4,128)(2,1)S(1)}, u32[]{:S(2)}, u32[]{:S(2)}) async-start(bf16[16,4,3584]{2,1,0:T(4,128)(2,1)} %reshape.221), calls=%async_computation.1 | async-start | bytes 917504 | tf_op jit(solution)/shard_map/all_to_all | solution.py:148
  187.1 47.9 %reduce-scatter.3.cloned.1.call-start = ((), (), s32[]{:S(2)}) async-start(), calls=%async_computation.7 | async-start | bytes 2293760 | tf_op jit(solution)/shard_map/reduce_scatter | solution.py:181
Sparse Core Ops, SparseCore 0:
  143.1 33.2 reduce-scatter.4
  206.7 28.2 reduce-scatter.2
where the time goes:
time: 245 us; the launch traced here: 244 us
  blocking collectives  59.7 us (24%)
  waiting for transfers between devices  49 us (20%)
  local copies, waits for them, and re-layouts  40.9 us (17%)
  starting transfers between devices  35.8 us (15%)
  matrix products  29.4 us (12%)
  other arithmetic  14.4 us (6%)
  between operations  14.4 us (6%)
    reduce_scatter x1, waiting for transfers between devices, local(): lax.psum_scatter(routed_out + shared_out, 'tensor', scatter_dimension=1,...  26.7 us
    all_to_all x1, blocking collectives, local(): lax.all_to_all(parcel_in, 'expert', split_axis=0, concat_axis=0, tiled=True)  20.1 us
    all_gather x1, blocking collectives, local(): lax.all_gather(saved_rows, 'tensor', axis=1, tiled=True)  18.1 us
    dot_general x6, matrix products, contract_last(): lax.dot_general(left, right, (((1,), (1,)), ((), ())), preferred_element_...  16.9 us
    ppermute x2, starting transfers between devices, passed_along(): return lax.ppermute(block, axis, route)  14.5 us
    all_to_all x1, waiting for transfers between devices, local(): lax.all_to_all(parcel_cot, 'expert', split_axis=0, concat_axis=0, tiled=T...  12 us
    all_gather x1, blocking collectives, local(): lax.all_gather(forward_in, 'tensor', axis=1, tiled=True)  11.5 us
    all_gather x1, blocking collectives, local(): lax.all_gather(backward_in, 'tensor', axis=1, tiled=True)  9.87 us
  transfers between devices with their start and end apart: 8, of which 4 were waited for; matrix products, arithmetic and copies ran while one was open for 29% of the time, Pallas kernels for 0%

commit v1 on v0

v1 whole, which is shorter than its diff:
```python
import jax
import jax.numpy as jnp
from jax import lax
from jax.sharding import Mesh, PartitionSpec as P

BF = jnp.bfloat16
F32 = jnp.float32
CAP = 4
RING = ("xh", "xl", "core")


def shifted(block, axis, distance):
    n = lax.axis_size(axis)
    return lax.ppermute(block, axis, [((i - distance) % n, i) for i in range(n)])


def swish_and_slope(v):
    s = jax.nn.sigmoid(v)
    return v * s, s * (1.0 + v * (1.0 - s))


def dot(a, b):
    return jnp.dot(a, b, preferred_element_type=F32)


def contract_last(left, right):
    return lax.dot_general(left, right, (((1,), (1,)), ((), ())), preferred_element_type=F32)


def slot_select(ids, keep, slot, weight_q, slots):
    target = jnp.where(keep > 0, ids * CAP + slot, slots).T
    hit = target[None] == lax.broadcasted_iota(jnp.int32, (slots, 1, 1), 0)
    weight = (weight_q.astype(F32) / 4096.0).T
    one = jnp.sum(jnp.where(hit, 1.0, 0.0), axis=1)
    return one, jnp.sum(jnp.where(hit, weight[None], 0.0), axis=1)


def spread(block, axis):
    return lax.all_to_all(jnp.broadcast_to(block[None], (2, *block.shape)), axis, 0, 0, tiled=True)


def local(inputs_prev, cotangent_next, saved_input, expert_ids, keep_mask, slot_pos, weight_q,
          gate_routed, up_routed, down_routed, gate_shared, up_shared, down_shared):
    tokens, shard = inputs_prev.shape[1:]
    experts = lax.axis_size("y")
    slots = experts * CAP
    saved = saved_input[0]
    fwd = shifted(inputs_prev[0], "pipe", 1)
    cot = shifted(cotangent_next[0], "pipe", -1)
    one_f, w_f = slot_select(expert_ids[0, 0], keep_mask[0, 0], slot_pos[0, 0], weight_q[0, 0], slots)
    one_b, w_b = slot_select(expert_ids[1, 0], keep_mask[1, 0], slot_pos[1, 0], weight_q[1, 0], slots)

    rows_f = dot(one_f.astype(BF), fwd).astype(BF)
    rows_s = dot(one_b.astype(BF), saved).astype(BF)
    rows_c = (jnp.sum(w_b, axis=1, keepdims=True) * dot(one_b.astype(BF), cot)).astype(BF)
    parcel = jnp.stack([r.reshape(experts, CAP, shard) for r in (rows_f, rows_s, rows_c)], axis=1)
    parcel = lax.all_to_all(parcel, "y", 0, 0, tiled=True)
    parcel = parcel.transpose(1, 0, 2, 3).reshape(3 * slots, shard)
    ring = lax.axis_size("xh") * 4
    got = lax.all_to_all(jnp.broadcast_to(parcel[None], (ring, *parcel.shape)), RING, 0, 0, tiled=True)
    got = got.reshape(2, 4, 3, slots, shard).transpose(2, 0, 3, 1, 4).reshape(3, 2 * slots, 4 * shard)

    def full(v):
        a = spread(v, "xl")
        b = spread(a, "core")
        return b.transpose(2, 1, 0, 3).reshape(tokens, 4 * shard)

    full_s = full(saved)
    full_f = full(fwd)
    full_c = full(cot)

    def compute(x, s, c, gate, up, down):
        n = x.shape[0]
        both = jnp.concatenate([x, s], axis=0)
        a = dot(both, gate)
        b = dot(both, up)
        dh = contract_last(c, down)
        act, slope = swish_and_slope(a)
        hidden = (act[:n] * b[:n]).astype(BF)
        gg = (dh * b[n:] * slope[n:]).astype(BF)
        gu = (dh * act[n:]).astype(BF)
        out = dot(hidden, down).astype(BF)
        grad = (contract_last(gg, gate) + contract_last(gu, up)).astype(BF)
        return out, grad

    out_r, grad_r = compute(got[0], got[1], got[2], gate_routed[0, 0], up_routed[0, 0], down_routed[0, 0])
    both = jnp.stack([out_r, grad_r]).reshape(2, 2, slots, 4, shard).transpose(1, 3, 0, 2, 4)
    both = lax.all_to_all(both.reshape(ring, 2 * slots, shard), RING, 0, 0, tiled=True)
    both = jnp.sum(both.astype(F32), axis=0).reshape(2, experts, CAP, shard).transpose(1, 0, 2, 3)
    both = lax.all_to_all(both.astype(BF), "y", 0, 0, tiled=True)
    both = both.transpose(1, 0, 2, 3).reshape(2, slots, shard).astype(F32)

    out_s, grad_s = compute(full_f, full_s, full_c, gate_shared[0], up_shared[0], down_shared[0])
    part = jnp.stack([out_s, grad_s]).reshape(2, tokens, 2, 2, shard).transpose(3, 2, 0, 1, 4)
    part = lax.all_to_all(part, "core", 0, 0, tiled=True)
    part = (part[0].astype(F32) + part[1].astype(F32)).astype(BF)
    part = lax.all_to_all(part, "xl", 0, 0, tiled=True)
    part = part[0].astype(F32) + part[1].astype(F32)

    def merge(weights, rows):
        return lax.dot_general(weights, rows, (((0,), (0,)), ((), ())), precision=lax.Precision.HIGHEST,
                               preferred_element_type=F32)

    out = part[0] + merge(w_f, both[0])
    grad = part[1] + merge(one_b, both[1])
    return out.astype(BF)[None], grad.astype(BF)[None]


def solution(mesh):
    pipe, expert, tensor = mesh.devices.shape
    fine = Mesh(mesh.devices.reshape(pipe, expert // 2, 2, 2, tensor // 2), ("pipe", "y", "xh", "xl", "core"))
    e, t = ("y", "xh"), ("xl", "core")
    act = P("pipe", e, t)
    table = P(None, "pipe", e, None)
    return jax.shard_map(
        local,
        mesh=fine,
        in_specs=(act, act, act, table, table, table, table,
                  P("pipe", e, None, t), P("pipe", e, None, t), P("pipe", e, t, None),
                  P("pipe", None, t), P("pipe", None, t), P("pipe", t, None)),
        out_specs=(act, act),
        check_vma=False,
    )
```

time: 245 us -> 182 us (0.74)
  blocking collectives: 59.7 us -> 6.13 us
  starting transfers between devices: 35.8 us -> 67.7 us
  between operations: 14.4 us -> 1.15 us
  local copies, waits for them, and re-layouts: 40.9 us -> 29.8 us
  matrix products: 29.4 us -> 19.9 us
  other arithmetic: 14.4 us -> 9.22 us
  waiting for transfers between devices: 49 us -> 46.1 us
    all_gather x3 -> x0, blocking collectives: 39.5 us -> none  [the longest x1 18.1 us: local(): lax.all_gather(saved_rows, 'tensor', axis=1, tiled=True)]
    all_to_all x4 -> x11, starting transfers between devices: 21 us -> 50.5 us  [the longest x5 21.4 us: spread(): lax.all_to_all(jnp.broadcast_to(block[None], (2, *block.shape)), axis, 0,...]
    reduce_scatter x2 -> x0, waiting for transfers between devices: 26.7 us -> none  [the longest x1 26.7 us: local(): lax.psum_scatter(routed_out + shared_out, 'tensor', scatter_dimension=1,...]
    scatter x6 -> x0, local copies, waits for them, and re-layouts: 25.8 us -> none  [the longest x2 8.61 us: slot_plan(): jnp.zeros((total_slots,), jnp.int32).at[target].set(source, mode='drop')]
    all_to_all x4 -> x11, waiting for transfers between devices: 22.3 us -> 46.1 us  [the longest x5 14.6 us: spread(): lax.all_to_all(jnp.broadcast_to(block[None], (2, *block.shape)), axis, 0,...]
    all_to_all x1, blocking collectives: 20.1 us -> 6.13 us  [spread(): lax.all_to_all(jnp.broadcast_to(block[None], (2, *block.shape)), axis, 0,...]
    another operation x1 -> x11, local copies, waits for them, and re-layouts: 0.01 us -> 11.9 us  [the longest x4 10.1 us: local(): jnp.stack([out_s, grad_s]).reshape(2, tokens, 2, 2, shard)]
    dot_general x6, matrix products: 16.9 us -> 6.26 us  [contract_last(): lax.dot_general(left, right, (((1,), (1,)), ((), ())), preferred_element_...]
  transfers between devices with their start and end apart: 8 -> 13, of which waited for: 4 -> 8; matrix products, arithmetic and copies ran while one was open for 29% -> 26% of each run, Pallas kernels for 0% -> 0%
where the time goes in v1:
time: 182 us; the launch traced here: 180 us
  starting transfers between devices  67.7 us (37%)
  waiting for transfers between devices  46.1 us (25%)
  local copies, waits for them, and re-layouts  29.8 us (16%)
  matrix products  19.9 us (11%)
  other arithmetic  9.22 us (5%)
  blocking collectives  6.13 us (3%)
    all_to_all x5, starting transfers between devices, spread(): lax.all_to_all(jnp.broadcast_to(block[None], (2, *block.shape)), axis, 0,...  21.4 us
    ppermute x2, starting transfers between devices, shifted(): lax.ppermute(block, axis, [((i - distance) % n, i) for i in range(n)])  17.2 us
    all_to_all x5, waiting for transfers between devices, spread(): lax.all_to_all(jnp.broadcast_to(block[None], (2, *block.shape)), axis, 0,...  14.6 us
    all_to_all x1, waiting for transfers between devices, local(): lax.all_to_all(both.reshape(ring, 2 * slots, shard), RING, 0, 0, tiled=True)  11 us
    another operation x4, local copies, waits for them, and re-layouts, local(): jnp.stack([out_s, grad_s]).reshape(2, tokens, 2, 2, shard)  10.1 us
    dot_general x9, matrix products, dot(): return jnp.dot(a, b, preferred_element_type=F32)  9.38 us
    all_to_all x1, waiting for transfers between devices, local(): part = lax.all_to_all(part, 'xl', 0, 0, tiled=True)  9.25 us
    all_to_all x1, starting transfers between devices, local(): parcel = lax.all_to_all(parcel, 'y', 0, 0, tiled=True)  6.82 us
  transfers between devices with their start and end apart: 13, of which 8 were waited for; matrix products, arithmetic and copies ran while one was open for 26% of the time, Pallas kernels for 0%

profile of v1, /device:TPU:1, one launch (start us, length us, event | category | flops | bytes accessed | tf_op | source)
XLA Modules:
  0.0 179.9 jit_solution(11732039109703114572)
XLA Ops:
  0.7 15.3 %collective-permute-start.1 = (bf16[128,896]{1,0:T(8,128)(2,1)}, bf16[128,896]{1,0:T(8,128)(2,1)S(1)}, u32[]{:S(2)}, u32[]{:S(2)}) collective-permute-start(bf16[128,896]{1,0:T(8,128)(2,1)} %bitcast.137), channel_id=1, source_target_pairs={{64,0},{128,64},{192,128},{256,192},{320,256},{384,320},{448,384},... | collective-permute-start | bytes 688136 | tf_op jit(solution)/shard_map/ppermute | solution.py:14
  16.0 1.9 %collective-permute-start = (bf16[128,896]{1,0:T(8,128)(2,1)}, bf16[128,896]{1,0:T(8,128)(2,1)S(1)}, u32[]{:S(2)}, u32[]{:S(2)}) collective-permute-start(bf16[128,896]{1,0:T(8,128)(2,1)} %bitcast.136), channel_id=1, source_target_pairs={{704,0},{0,64},{64,128},{128,192},{192,256},{256,320},{320,384},{3... | collective-permute-start | bytes 688136 | tf_op jit(solution)/shard_map/ppermute | solution.py:14
  19.8 3.5 %all-to-all-start.2 = ((bf16[2,128,896]{1,2,0:T(8,128)(2,1)}), bf16[2,128,896]{1,2,0:T(8,128)(2,1)S(1)}, u32[]{:S(2)}, u32[]{:S(2)}) async-start(bf16[2,128,896]{1,2,0:T(8,128)(2,1)} %broadcast_in_dim.89), calls=%async_computation.2 | async-start | bytes 917504 | tf_op jit(solution)/shard_map/all_to_all | solution.py:39
  25.2 4.5 %all-to-all-done.2 = bf16[2,128,896]{1,2,0:T(8,128)(2,1)S(1)} async-done(((bf16[2,128,896]{1,2,0:T(8,128)(2,1)}), bf16[2,128,896]{1,2,0:T(8,128)(2,1)S(1)}, u32[]{:S(2)}, u32[]{:S(2)}) %all-to-all-start.2) | async-done | bytes 458784 | tf_op jit(solution)/shard_map/all_to_all | solution.py:39
  30.7 5.4 %all-to-all-start.3 = ((bf16[2,2,128,896]{2,3,1,0:T(8,128)(2,1)}), bf16[2,2,128,896]{2,3,1,0:T(8,128)(2,1)S(1)}, u32[]{:S(2)}, u32[]{:S(2)}) async-start(bf16[2,2,128,896]{2,3,1,0:T(8,128)(2,1)} %broadcast_in_dim.90), calls=%async_computation.3 | async-start | bytes 1835008 | tf_op jit(solution)/shard_map/all_to_all | solution.py:39
  38.6 3.5 %all-to-all-start = ((bf16[2,128,896]{1,2,0:T(8,128)(2,1)}), bf16[2,128,896]{1,2,0:T(8,128)(2,1)S(1)}, u32[]{:S(2)}, u32[]{:S(2)}) async-start(bf16[2,128,896]{1,2,0:T(8,128)(2,1)} %broadcast_in_dim.86), calls=%async_computation | async-start | bytes 917504 | tf_op jit(solution)/shard_map/all_to_all | solution.py:39
  43.1 5.9 %all-to-all-done = bf16[2,128,896]{1,2,0:T(8,128)(2,1)S(1)} async-done(((bf16[2,128,896]{1,2,0:T(8,128)(2,1)}), bf16[2,128,896]{1,2,0:T(8,128)(2,1)S(1)}, u32[]{:S(2)}, u32[]{:S(2)}) %all-to-all-start) | async-done | bytes 458784 | tf_op jit(solution)/shard_map/all_to_all | solution.py:39
  49.2 6.1 %all_to_all.60 = bf16[2,2,128,896]{2,3,1,0:T(8,128)(2,1)} all-to-all(bf16[2,2,128,896]{2,3,1,0:T(8,128)(2,1)S(1)} %broadcast_in_dim.87), channel_id=1, replica_groups=mesh['pipe'=12,'y'=8,'xh'=2,'xl'=2,'core'=2] {'core'}, dimensions={0} | all-to-all | bytes 1835008 | tf_op jit(solution)/shard_map/all_to_all | solution.py:39
  56.1 3.5 %all-to-all-start.4 = ((bf16[2,128,896]{1,2,0:T(8,128)(2,1)}), bf16[2,128,896]{1,2,0:T(8,128)(2,1)S(1)}, u32[]{:S(2)}, u32[]{:S(2)}) async-start(bf16[2,128,896]{1,2,0:T(8,128)(2,1)} %broadcast_in_dim.91), calls=%async_computation.4 | async-start | bytes 917504 | tf_op jit(solution)/shard_map/all_to_all | solution.py:39
  63.0 3.5 %all-to-all-done.4 = bf16[2,128,896]{1,2,0:T(8,128)(2,1)S(1)} async-done(((bf16[2,128,896]{1,2,0:T(8,128)(2,1)}), bf16[2,128,896]{1,2,0:T(8,128)(2,1)S(1)}, u32[]{:S(2)}, u32[]{:S(2)}) %all-to-all-start.4) | async-done | bytes 458784 | tf_op jit(solution)/shard_map/all_to_all | solution.py:39
  67.6 5.6 %all-to-all-start.5 = ((bf16[2,2,128,896]{2,3,1,0:T(8,128)(2,1)}), bf16[2,2,128,896]{2,3,1,0:T(8,128)(2,1)}, u32[]{:S(2)}, u32[]{:S(2)}) async-start(bf16[2,2,128,896]{2,3,1,0:T(8,128)(2,1)} %broadcast_in_dim.92), calls=%async_computation.5 | async-start | bytes 1835008 | tf_op jit(solution)/shard_map/all_to_all | solution.py:39
  76.2 6.8 %all-to-all-start.8 = ((bf16[8,3,4,896]{3,2,1,0:T(4,128)(2,1)}), bf16[8,3,4,896]{3,2,1,0:T(4,128)(2,1)S(1)}, u32[]{:S(2)}, u32[]{:S(2)}) async-start(bf16[8,3,4,896]{3,2,1,0:T(4,128)(2,1)} %pad_maximum_fusion.4), calls=%async_computation.8 | async-start | bytes 344064 | tf_op jit(solution)/shard_map/all_to_all | solution.py:57
  83.0 2.3 %copy.73 = bf16[2,2,128,896]{2,3,0,1:T(8,128)(2,1)} copy(bf16[2,2,128,896]{2,3,1,0:T(8,128)(2,1)} %all-to-all-done.5) | data formatting | bytes 1835008 | tf_op jit(solution)/shard_map/all_to_all | solution.py:39
  85.4 2.6 %fusion.6 = f32[256,256]{1,0:T(8,128)} fusion(bf16[1,3584,256]{2,1,0:T(8,128)(2,1)S(1)} %copy-done.8, bf16[128,3584]{0,1:T(8,128)(2,1)S(1)} %bitcast.126, bf16[128,3584]{0,1:T(8,128)(2,1)} %bitcast.128), kind=kOutput, calls=%fused_computation.12 | convolution fusion | flops 473432064 | bytes 3932160 | tf_op jit(solution)/shard_map/dot_general | solution.py:23
  87.9 4.6 %all-to-all-done.8 = bf16[8,3,4,896]{3,2,1,0:T(4,128)(2,1)S(1)} async-done(((bf16[8,3,4,896]{3,2,1,0:T(4,128)(2,1)}), bf16[8,3,4,896]{3,2,1,0:T(4,128)(2,1)S(1)}, u32[]{:S(2)}, u32[]{:S(2)}) %all-to-all-start.8) | async-done | bytes 172064 | tf_op jit(solution)/shard_map/all_to_all | solution.py:57
  93.9 5.7 %all-to-all-start.9 = ((bf16[8,96,896]{2,1,0:T(8,128)(2,1)}), bf16[8,96,896]{2,1,0:T(8,128)(2,1)S(1)}, u32[]{:S(2)}, u32[]{:S(2)}) async-start(bf16[8,96,896]{2,1,0:T(8,128)(2,1)} %broadcast_in_dim.99), calls=%async_computation.9 | async-start | bytes 2752512 | tf_op jit(solution)/shard_map/all_to_all | solution.py:60
  99.6 2.6 %fusion.2 = f32[128,256]{1,0:T(8,128)S(1)} fusion(bf16[128,3584]{0,1:T(8,128)(2,1)} %bitcast.118, bf16[1,256,3584]{2,1,0:T(8,128)(2,1)} %param.25), kind=kOutput, calls=%fused_computation.8 | convolution fusion | flops 234881024 | bytes 2883584 | tf_op jit(solution)/shard_map/dot_general | solution.py:27
  103.7 1.7 fusion
  105.4 3.2 %stack.22 = bf16[1,128,2,2,896]{4,3,2,1,0:T(2,128)(2,1)} reshape(bf16[128,3584]{1,0:T(8,128)(2,1)} %fusion) | data formatting | bytes 1835008 | tf_op jit(solution)/shard_map/stack | solution.py:94
  108.6 2.3 %copy.75 = bf16[1,128,2,2,896]{4,1,0,2,3:T(8,128)(2,1)} copy(bf16[1,128,2,2,896]{4,3,2,1,0:T(2,128)(2,1)} %stack.22) | data formatting | bytes 1835008 | tf_op jit(solution)/shard_map/stack | solution.py:94
  110.9 2.3 %convolution_convert_fusion = bf16[128,3584]{1,0:T(8,128)(2,1)} fusion(bf16[1,256,3584]{2,1,0:T(8,128)(2,1)S(1)} %copy-done.1, f32[256,256]{1,0:T(8,128)} %fusion.6, f32[256,256]{1,0:T(8,128)S(1)} %get-tuple-element.9), kind=kOutput, calls=%fused_computation.2 | convolution fusion | flops 235405312 | bytes 3014656 | tf_op jit(solution)/shard_map/dot_general | solution.py:23
  113.2 3.2 %stack.21 = bf16[1,128,2,2,896]{4,3,2,1,0:T(2,128)(2,1)} reshape(bf16[128,3584]{1,0:T(8,128)(2,1)} %convolution_convert_fusion) | data formatting | bytes 1835008 | tf_op jit(solution)/shard_map/stack | solution.py:94
  119.2 4.9 %all-to-all-start.6 = ((bf16[2,2,2,128,896]{4,3,2,1,0:T(8,128)(2,1)}), bf16[2,2,2,128,896]{4,3,2,1,0:T(8,128)(2,1)}, u32[]{:S(2)}, u32[]{:S(2)}) async-start(bf16[2,2,2,128,896]{4,3,2,1,0:T(8,128)(2,1)} %maximum_bitcast_fusion), calls=%async_computation.6 | async-start | bytes 3670016 | tf_op jit(solution)/shard_map/all_to_all | solution.py:95
  130.3 4.8 %all-to-all-start.10 = ((bf16[8,64,896]{2,1,0:T(8,128)(2,1)}), bf16[8,64,896]{2,1,0:T(8,128)(2,1)S(1)}, u32[]{:S(2)}, u32[]{:S(2)}) async-start(bf16[8,64,896]{2,1,0:T(8,128)(2,1)} %bitcast.117), calls=%async_computation.10 | async-start | bytes 1835008 | tf_op jit(solution)/shard_map/all_to_all | solution.py:88
  135.1 2.6 %fusion.17 = bf16[2,2,128,896]{3,2,1,0:T(8,128)(2,1)} fusion(bf16[2,2,2,128,896]{4,3,2,1,0:T(8,128)(2,1)} %all-to-all-done.6), kind=kLoop, calls=%fused_computation.29 | loop fusion | flops 1835008 | bytes 2752512 | tf_op jit(solution)/shard_map/convert_element_type | solution.py:96
  137.7 11.0 %all-to-all-done.10 = bf16[8,64,896]{2,1,0:T(8,128)(2,1)S(1)} async-done(((bf16[8,64,896]{2,1,0:T(8,128)(2,1)}), bf16[8,64,896]{2,1,0:T(8,128)(2,1)S(1)}, u32[]{:S(2)}, u32[]{:S(2)}) %all-to-all-start.10) | async-done | bytes 917536 | tf_op jit(solution)/shard_map/all_to_all | solution.py:88
  149.6 3.6 %all-to-all-start.7 = ((bf16[2,2,128,896]{3,2,1,0:T(8,128)(2,1)}), bf16[2,2,128,896]{3,2,1,0:T(8,128)(2,1)S(1)}, u32[]{:S(2)}, u32[]{:S(2)}) async-start(bf16[2,2,128,896]{3,2,1,0:T(8,128)(2,1)} %fusion.17), calls=%async_computation.7 | async-start | bytes 1835008 | tf_op jit(solution)/shard_map/all_to_all | solution.py:97
  155.3 9.3 %all-to-all-done.7 = bf16[2,2,128,896]{3,2,1,0:T(8,128)(2,1)S(1)} async-done(((bf16[2,2,128,896]{3,2,1,0:T(8,128)(2,1)}), bf16[2,2,128,896]{3,2,1,0:T(8,128)(2,1)S(1)}, u32[]{:S(2)}, u32[]{:S(2)}) %all-to-all-start.7) | async-done | bytes 917536 | tf_op jit(solution)/shard_map/all_to_all | solution.py:97
  164.5 3.4 %all-to-all-start.11 = ((bf16[8,2,4,896]{3,2,1,0:T(4,128)(2,1)}), bf16[8,2,4,896]{3,2,1,0:T(4,128)(2,1)S(1)}, u32[]{:S(2)}, u32[]{:S(2)}) async-start(bf16[8,2,4,896]{3,2,1,0:T(4,128)(2,1)} %copy.85), calls=%async_computation.11 | async-start | bytes 229376 | tf_op jit(solution)/shard_map/all_to_all | solution.py:90
  168.9 6.7 %all-to-all-done.11 = bf16[8,2,4,896]{3,2,1,0:T(4,128)(2,1)S(1)} async-done(((bf16[8,2,4,896]{3,2,1,0:T(4,128)(2,1)}), bf16[8,2,4,896]{3,2,1,0:T(4,128)(2,1)S(1)}, u32[]{:S(2)}, u32[]{:S(2)}) %all-to-all-start.11) | async-done | bytes 114720 | tf_op jit(solution)/shard_map/all_to_all | solution.py:90
  175.7 2.1 %fusion.14 = bf16[1,128,896]{2,1,0:T(8,128)(2,1)} fusion(f32[32,128]{1,0:T(8,128)S(1)} %get-tuple-element.4, bf16[32,896]{1,0:T(8,128)(2,1)S(1)} %squeeze.72, f32[1,2,128,896]{3,2,1,0:T(8,128)} %convert_add_fusion), kind=kOutput, calls=%fused_computation.23 | convolution fusion | flops 44269568 | bytes 761856 | tf_op jit(solution)/shard_map/dot_general | solution.py:101
  177.8 2.1 %fusion.15 = bf16[1,128,896]{2,1,0:T(8,128)(2,1)} fusion(f32[32,128]{1,0:T(8,128)S(1)} %copy-done.20, bf16[32,896]{1,0:T(8,128)(2,1)S(1)} %squeeze.70, f32[1,2,128,896]{3,2,1,0:T(8,128)} %convert_add_fusion), kind=kOutput, calls=%fused_computation.24 | convolution fusion | flops 44269568 | bytes 761856 | tf_op jit(solution)/shard_map/dot_general | solution.py:101
  (112 shorter events, 32.6 us)
Async XLA Ops:
  0.6 73.5 %copy-start = (bf16[1,3584,256]{2,1,0:T(8,128)(2,1)S(1)}, bf16[1,3584,256]{2,1,0:T(8,128)(2,1)}, u32[]{:S(2)}) copy-start(bf16[1,3584,256]{2,1,0:T(8,128)(2,1)} %param.23) | copy-start | bytes 5505028
  0.6 23.0 %copy-start.13 = (bf16[1,128,896]{2,1,0:T(8,128)(2,1)S(1)}, bf16[1,128,896]{2,1,0:T(8,128)(2,1)}, u32[]{:S(2)}) copy-start(bf16[1,128,896]{2,1,0:T(8,128)(2,1)} %param.15) | copy-start | bytes 688132
  0.7 22.6 %copy-start.21 = (s32[2,1,128,8]{2,3,1,0:T(8,128)S(1)}, s32[2,1,128,8]{2,3,1,0:T(8,128)}, u32[]{:S(2)}) copy-start(s32[2,1,128,8]{2,3,1,0:T(8,128)} %param.19) | copy-start | bytes 24580
  0.7 22.6 %copy-start.23 = (s32[2,1,128,8]{2,3,1,0:T(8,128)S(1)}, s32[2,1,128,8]{2,3,1,0:T(8,128)}, u32[]{:S(2)}) copy-start(s32[2,1,128,8]{2,3,1,0:T(8,128)} %param.16) | copy-start | bytes 24580
  0.7 22.6 %copy-start.24 = (s32[2,1,128,8]{2,3,1,0:T(8,128)S(1)}, s32[2,1,128,8]{2,3,1,0:T(8,128)}, u32[]{:S(2)}) copy-start(s32[2,1,128,8]{2,3,1,0:T(8,128)} %param.17) | copy-start | bytes 24580
  0.7 22.6 %copy-start.22 = (s32[2,1,128,8]{2,3,1,0:T(8,128)S(1)}, s32[2,1,128,8]{2,3,1,0:T(8,128)}, u32[]{:S(2)}) copy-start(s32[2,1,128,8]{2,3,1,0:T(8,128)} %param.18) | copy-start | bytes 24580
  0.7 35.6 %collective-permute-start.1 = (bf16[128,896]{1,0:T(8,128)(2,1)}, bf16[128,896]{1,0:T(8,128)(2,1)S(1)}, u32[]{:S(2)}, u32[]{:S(2)}) collective-permute-start(bf16[128,896]{1,0:T(8,128)(2,1)} %bitcast.137), channel_id=1, source_target_pairs={{64,0},{128,64},{192,128},{256,192},{320,256},{384,320},{448,384},... | collective-permute-start | bytes 688136 | tf_op jit(solution)/shard_map/ppermute | solution.py:14
  16.0 20.1 %collective-permute-start = (bf16[128,896]{1,0:T(8,128)(2,1)}, bf16[128,896]{1,0:T(8,128)(2,1)S(1)}, u32[]{:S(2)}, u32[]{:S(2)}) collective-permute-start(bf16[128,896]{1,0:T(8,128)(2,1)} %bitcast.136), channel_id=1, source_target_pairs={{704,0},{0,64},{64,128},{128,192},{192,256},{256,320},{320,384},{3... | collective-permute-start | bytes 688136 | tf_op jit(solution)/shard_map/ppermute | solution.py:14
  19.8 9.9 %all-to-all-start.2 = ((bf16[2,128,896]{1,2,0:T(8,128)(2,1)}), bf16[2,128,896]{1,2,0:T(8,128)(2,1)S(1)}, u32[]{:S(2)}, u32[]{:S(2)}) async-start(bf16[2,128,896]{1,2,0:T(8,128)(2,1)} %broadcast_in_dim.89), calls=%async_computation.2 | async-start | bytes 917504 | tf_op jit(solution)/shard_map/all_to_all | solution.py:39
  30.7 7.0 %all-to-all-start.3 = ((bf16[2,2,128,896]{2,3,1,0:T(8,128)(2,1)}), bf16[2,2,128,896]{2,3,1,0:T(8,128)(2,1)S(1)}, u32[]{:S(2)}, u32[]{:S(2)}) async-start(bf16[2,2,128,896]{2,3,1,0:T(8,128)(2,1)} %broadcast_in_dim.90), calls=%async_computation.3 | async-start | bytes 1835008 | tf_op jit(solution)/shard_map/all_to_all | solution.py:39
  36.3 2.3 %copy-start.14 = (bf16[128,896]{1,0:T(8,128)(2,1)}, bf16[128,896]{1,0:T(8,128)(2,1)S(1)}, u32[]{:S(2)}) copy-start(bf16[128,896]{1,0:T(8,128)(2,1)S(1)} %collective-permute-done.1) | copy-start | bytes 688132
  38.6 10.5 %all-to-all-start = ((bf16[2,128,896]{1,2,0:T(8,128)(2,1)}), bf16[2,128,896]{1,2,0:T(8,128)(2,1)S(1)}, u32[]{:S(2)}, u32[]{:S(2)}) async-start(bf16[2,128,896]{1,2,0:T(8,128)(2,1)} %broadcast_in_dim.86), calls=%async_computation | async-start | bytes 917504 | tf_op jit(solution)/shard_map/all_to_all | solution.py:39
  49.0 6.3 %copy-start.15 = (bf16[128,896]{0,1:T(8,128)(2,1)S(1)}, bf16[128,896]{0,1:T(8,128)(2,1)}, u32[]{:S(2)}) copy-start(bf16[128,896]{0,1:T(8,128)(2,1)} %copy.72) | copy-start | bytes 688132
  56.1 10.5 %all-to-all-start.4 = ((bf16[2,128,896]{1,2,0:T(8,128)(2,1)}), bf16[2,128,896]{1,2,0:T(8,128)(2,1)S(1)}, u32[]{:S(2)}, u32[]{:S(2)}) async-start(bf16[2,128,896]{1,2,0:T(8,128)(2,1)} %broadcast_in_dim.91), calls=%async_computation.4 | async-start | bytes 917504 | tf_op jit(solution)/shard_map/all_to_all | solution.py:39
  60.4 1.9 %copy-start.17 = (bf16[8,1,4,896]{3,2,0,1:T(4,128)(2,1)S(1)}, bf16[8,1,4,896]{3,2,0,1:T(4,128)(2,1)}, u32[]{:S(2)}) copy-start(bf16[8,1,4,896]{3,2,0,1:T(4,128)(2,1)} %stack_reshape.10) | copy-start | bytes 172036
  62.2 11.0 %copy-start.3 = (bf16[2,2,128,896]{2,3,1,0:T(8,128)(2,1)S(1)}, bf16[2,2,128,896]{2,3,1,0:T(8,128)(2,1)}, u32[]{:S(2)}) copy-start(bf16[2,2,128,896]{2,3,1,0:T(8,128)(2,1)} %all_to_all.60) | copy-start | bytes 2752516
  67.6 8.6 %all-to-all-start.5 = ((bf16[2,2,128,896]{2,3,1,0:T(8,128)(2,1)}), bf16[2,2,128,896]{2,3,1,0:T(8,128)(2,1)}, u32[]{:S(2)}, u32[]{:S(2)}) async-start(bf16[2,2,128,896]{2,3,1,0:T(8,128)(2,1)} %broadcast_in_dim.92), calls=%async_computation.5 | async-start | bytes 1835008 | tf_op jit(solution)/shard_map/all_to_all | solution.py:39
  73.2 1.5 copy-start.10
  74.7 10.6 %copy-start.11 = (bf16[128,2,2,896]{0,3,2,1:T(8,128)(2,1)S(1)}, bf16[128,2,2,896]{0,3,2,1:T(8,128)(2,1)}, u32[]{:S(2)}) copy-start(bf16[128,2,2,896]{0,3,2,1:T(8,128)(2,1)} %copy.71) | copy-start | bytes 2752516
  76.2 16.3 %all-to-all-start.8 = ((bf16[8,3,4,896]{3,2,1,0:T(4,128)(2,1)}), bf16[8,3,4,896]{3,2,1,0:T(4,128)(2,1)S(1)}, u32[]{:S(2)}, u32[]{:S(2)}) async-start(bf16[8,3,4,896]{3,2,1,0:T(4,128)(2,1)} %pad_maximum_fusion.4), calls=%async_computation.8 | async-start | bytes 344064 | tf_op jit(solution)/shard_map/all_to_all | solution.py:57
  83.0 2.3 %copy-start.8 = (bf16[1,3584,256]{2,1,0:T(8,128)(2,1)S(1)}, bf16[1,3584,256]{2,1,0:T(8,128)(2,1)}, u32[]{:S(2)}) copy-start(bf16[1,3584,256]{2,1,0:T(8,128)(2,1)} %param.24) | copy-start | bytes 5505028
  93.9 25.4 %all-to-all-start.9 = ((bf16[8,96,896]{2,1,0:T(8,128)(2,1)}), bf16[8,96,896]{2,1,0:T(8,128)(2,1)S(1)}, u32[]{:S(2)}, u32[]{:S(2)}) async-start(bf16[8,96,896]{2,1,0:T(8,128)(2,1)} %broadcast_in_dim.99), calls=%async_computation.9 | async-start | bytes 2752512 | tf_op jit(solution)/shard_map/all_to_all | solution.py:60
  99.6 2.6 %copy-start.16 = (f32[256,256]{1,0:T(8,128)S(1)}, f32[256,256]{1,0:T(8,128)}, u32[]{:S(2)}) copy-start(f32[256,256]{1,0:T(8,128)} %fusion.6) | copy-start | bytes 786436
  99.6 2.6 %copy-start.18 = (f32[256,256]{1,0:T(8,128)S(1)}, f32[256,256]{1,0:T(8,128)}, u32[]{:S(2)}) copy-start(f32[256,256]{1,0:T(8,128)} %get-tuple-element.10) | copy-start | bytes 786436
  99.6 2.6 %copy-start.19 = (f32[256,256]{1,0:T(8,128)S(1)}, f32[256,256]{1,0:T(8,128)}, u32[]{:S(2)}) copy-start(f32[256,256]{1,0:T(8,128)} %get-tuple-element.20) | copy-start | bytes 786436
  102.2 1.5 copy-start.9
  108.6 2.4 %copy-start.1 = (bf16[1,256,3584]{2,1,0:T(8,128)(2,1)S(1)}, bf16[1,256,3584]{2,1,0:T(8,128)(2,1)}, u32[]{:S(2)}) copy-start(bf16[1,256,3584]{2,1,0:T(8,128)(2,1)} %param.25) | copy-start | bytes 5505028
  119.2 11.1 %all-to-all-start.6 = ((bf16[2,2,2,128,896]{4,3,2,1,0:T(8,128)(2,1)}), bf16[2,2,2,128,896]{4,3,2,1,0:T(8,128)(2,1)}, u32[]{:S(2)}, u32[]{:S(2)}) async-start(bf16[2,2,2,128,896]{4,3,2,1,0:T(8,128)(2,1)} %maximum_bitcast_fusion), calls=%async_computation.6 | async-start | bytes 3670016 | tf_op jit(solution)/shard_map/all_to_all | solution.py:95
  130.3 18.4 %all-to-all-start.10 = ((bf16[8,64,896]{2,1,0:T(8,128)(2,1)}), bf16[8,64,896]{2,1,0:T(8,128)(2,1)S(1)}, u32[]{:S(2)}, u32[]{:S(2)}) async-start(bf16[8,64,896]{2,1,0:T(8,128)(2,1)} %bitcast.117), calls=%async_computation.10 | async-start | bytes 1835008 | tf_op jit(solution)/shard_map/all_to_all | solution.py:88
  149.6 14.9 %all-to-all-start.7 = ((bf16[2,2,128,896]{3,2,1,0:T(8,128)(2,1)}), bf16[2,2,128,896]{3,2,1,0:T(8,128)(2,1)S(1)}, u32[]{:S(2)}, u32[]{:S(2)}) async-start(bf16[2,2,128,896]{3,2,1,0:T(8,128)(2,1)} %fusion.17), calls=%async_computation.7 | async-start | bytes 1835008 | tf_op jit(solution)/shard_map/all_to_all | solution.py:97
  154.5 23.3 %copy-start.20 = (f32[32,128]{1,0:T(8,128)S(1)}, f32[32,128]{1,0:T(8,128)}, u32[]{:S(2)}) copy-start(f32[32,128]{1,0:T(8,128)} %get-tuple-element.3) | copy-start | bytes 49156
  164.5 11.1 %all-to-all-start.11 = ((bf16[8,2,4,896]{3,2,1,0:T(4,128)(2,1)}), bf16[8,2,4,896]{3,2,1,0:T(4,128)(2,1)S(1)}, u32[]{:S(2)}, u32[]{:S(2)}) async-start(bf16[8,2,4,896]{3,2,1,0:T(4,128)(2,1)} %copy.85), calls=%async_computation.11 | async-start | bytes 229376 | tf_op jit(solution)/shard_map/all_to_all | solution.py:90
  (6 other events, 7.0 us)

commit v2 on v1

v2 whole, which is shorter than its diff:
```python
import functools

import jax
import jax.numpy as jnp
from jax import lax
from jax.experimental import pallas as pl
from jax.experimental.pallas import tpu as pltpu
from jax.sharding import Mesh, PartitionSpec as P

BF = jnp.bfloat16
F32 = jnp.float32
I32 = jnp.int32
CAP = 4
PAD = 4 * CAP


def call(body, name, outs, grid=(1,), in_specs=None, out_specs=None, scratch=(), flops=0):
    spec = pltpu.PrefetchScalarGridSpec(
        num_scalar_prefetch=1, grid=grid, in_specs=in_specs, out_specs=out_specs, scratch_shapes=scratch
    )
    return pl.pallas_call(
        body, grid_spec=spec, out_shape=outs, name=name,
        cost_estimate=pl.CostEstimate(flops=flops, transcendentals=0, bytes_accessed=0),
        compiler_params=pltpu.CompilerParams(vmem_limit_bytes=48 * 2**20),
    )


def whole(shape):
    return pl.BlockSpec(shape, lambda j, s: (0,) * len(shape))


def shape_of(dtype, *dims):
    return jax.ShapeDtypeStruct(dims, dtype)


def shifted(block, axis, distance):
    n = lax.axis_size(axis)
    return lax.ppermute(block, axis, [((i - distance) % n, i) for i in range(n)])


def swapped(block, axis):
    return lax.ppermute(block, axis, [(0, 1), (1, 0)])


def dot(a, b):
    return jnp.dot(a, b, preferred_element_type=F32)


def contract_last(left, right):
    return lax.dot_general(left, right, (((1,), (1,)), ((), ())), preferred_element_type=F32)


def tables_body(s, ids, keep, slot, wq, sel_f, sel_s, sel_c, scale, add_hi, add_lo, add_b):
    tokens = ids.shape[2]
    row = lax.broadcasted_iota(I32, (tokens, 1), 0)
    arr = (row // CAP) % 4
    slot_id = (row // PAD) * CAP + row % CAP
    back = 8 * (tokens // PAD)
    row2 = lax.broadcasted_iota(I32, (back, 1), 0)
    dirn = (row2 // CAP) % 2
    slot2 = (row2 // 8) * CAP + row2 % CAP
    want_f = jnp.where(arr == 0, slot_id, -1)
    want_b = jnp.where((arr == 1) | (arr == 2), slot_id, -1)
    back_f = jnp.where(dirn == 0, slot2, -1)
    back_b = jnp.where(dirn == 1, slot2, -1)
    hit_f = jnp.zeros((tokens, tokens), F32)
    hit_b = jnp.zeros((tokens, tokens), F32)
    weight = jnp.zeros((tokens, tokens), F32)
    hi = jnp.zeros((back, tokens), F32)
    lo = jnp.zeros((back, tokens), F32)
    one = jnp.zeros((back, tokens), F32)
    target = jnp.where(keep[...] > 0, ids[...] * CAP + slot[...], -2)
    level = wq[...]
    for k in range(ids.shape[1]):
        tf = target[0, k : k + 1]
        tb = target[1, k : k + 1]
        lf = level[0, k : k + 1]
        lb = level[1, k : k + 1].astype(F32) * (1.0 / 4096.0)
        top = (lf // 64) * 64
        hit_f += jnp.where(tf == want_f, 1.0, 0.0)
        eq = tb == want_b
        hit_b += jnp.where(eq, 1.0, 0.0)
        weight += jnp.where(eq, lb, 0.0)
        eq = tf == back_f
        hi += jnp.where(eq, top.astype(F32) * (1.0 / 4096.0), 0.0)
        lo += jnp.where(eq, (lf - top).astype(F32) * (1.0 / 4096.0), 0.0)
        one += jnp.where(tb == back_b, 1.0, 0.0)
    sel_f[...] = hit_f.astype(BF)
    sel_s[...] = jnp.where(arr == 1, hit_b, 0.0).astype(BF)
    sel_c[...] = jnp.where(arr == 2, hit_b, 0.0).astype(BF)
    scale[...] = jnp.sum(weight, axis=1, keepdims=True)
    add_hi[...] = hi.T.astype(BF)
    add_lo[...] = lo.T.astype(BF)
    add_b[...] = one.T.astype(BF)


def parcel_body(s, sel_f, sel_s, sel_c, scale, fwd, saved, cot, out):
    rows = dot(sel_f[...], fwd[...]) + dot(sel_s[...], saved[...]) + scale[...] * dot(sel_c[...], cot[...])
    out[...] = rows.astype(BF)


def fan_body(s, got, out):
    n = got.shape[0]
    m = n * 3 // 4
    half = n // 2
    r = lax.broadcasted_iota(I32, (m, n), 0)
    c = lax.broadcasted_iota(I32, (m, n), 1)
    k = r - half
    source = jnp.where(r < half, (r // 8) * PAD + r % 8, (k // CAP) * PAD + 8 + k % CAP)
    rows = dot(jnp.where(c == source, 1.0, 0.0).astype(BF), got[...]).astype(BF)
    for i in range(out.shape[0]):
        out[i] = rows


def pack_body(s, gs, us, gr, ur, ds, dr, in_side, out_side):
    w = gs.shape[2]
    n = gr.shape[2]
    in_side[:, 0:w] = gs[0]
    in_side[:, w : 2 * w] = us[0]
    in_side[:, 2 * w : 2 * w + n] = gr[0]
    in_side[:, 2 * w + n : 2 * w + 2 * n] = ur[0]
    out_side[0 : ds.shape[0]] = ds[...]
    out_side[ds.shape[0] :] = dr[...]


def pre(acc, first, both, cot, gate, up, down, gate_o, up_o, down_o):
    n = both.shape[0]
    m = cot.shape[0]
    w = gate.shape[1]

    def put(r0, r1, c0, c1, v):
        @pl.when(first)
        def _():
            acc[r0:r1, c0:c1] = v

        @pl.when(jnp.logical_not(first))
        def _():
            acc[r0:r1, c0:c1] += v

    put(0, n, 0, w, dot(both, gate))
    put(0, n, w, 2 * w, dot(both, gate_o))
    put(n, 2 * n, 0, w, dot(both, up))
    put(n, 2 * n, w, 2 * w, dot(both, up_o))
    put(2 * n, 2 * n + m, 0, w, contract_last(cot, down))
    put(2 * n, 2 * n + m, w, 2 * w, contract_last(cot, down_o))


def joined(mine, other):
    w = mine.shape[1] // 2
    return jnp.concatenate([mine[:, :w] + other[:, w:], mine[:, w:] + other[:, :w]], axis=1)


def shared_pre_body(s, own_f, own_s, own_c, far_f, far_s, far_c, gate, up, down, gate_o, up_o, down_o, acc):
    j = pl.program_id(0)
    near = j == 0
    both = jnp.concatenate(
        [jnp.where(near, own_f[...], far_f[...]), jnp.where(near, own_s[...], far_s[...])], axis=0
    )
    cot = jnp.where(near, own_c[...], far_c[...])
    pre(acc, near, both, cot, gate[0], up[0], down[...], gate_o[...], up_o[...], down_o[...])


def shared_post_body(s, mine, other, gate, up, down, gate_o, up_o, down_o, send, keep, hid, gg, gu):
    j = pl.program_id(0)
    n = hid.shape[0]
    w = gate.shape[2]

    @pl.when(j == 0)
    def _():
        a_f = joined(mine[0:n], other[0:n])
        a_s = joined(mine[n : 2 * n], other[n : 2 * n])
        b_f = joined(mine[2 * n : 3 * n], other[2 * n : 3 * n])
        b_s = joined(mine[3 * n : 4 * n], other[3 * n : 4 * n])
        dh = joined(mine[4 * n : 5 * n], other[4 * n : 5 * n])
        hid[...] = (a_f * jax.nn.sigmoid(a_f) * b_f).astype(BF)
        sg = jax.nn.sigmoid(a_s)
        gg[...] = (dh * b_s * (sg * (1.0 + a_s * (1.0 - sg)))).astype(BF)
        gu[...] = (dh * (a_s * sg)).astype(BF)

    out = dot(hid[:, :w], down[...]) + dot(hid[:, w:], down_o[...])
    grad = (
        contract_last(gg[:, :w], gate[0]) + contract_last(gg[:, w:], gate_o[...])
        + contract_last(gu[:, :w], up[0]) + contract_last(gu[:, w:], up_o[...])
    )

    @pl.when(j == 0)
    def _():
        send[0] = out.astype(BF)
        send[1] = grad.astype(BF)

    @pl.when(j == 1)
    def _():
        keep[0] = out
        keep[1] = grad


def expert_pre_body(s, got, gate, up, down, gate_o, up_o, down_o, acc):
    j = pl.program_id(0)
    half = got.shape[2] * 2 // 3
    both = jnp.concatenate([got[0, 0, :half], got[1, 0, :half]], axis=0)
    cot = jnp.concatenate([got[0, 0, half:], got[1, 0, half:]], axis=0)
    pre(acc, j == 0, both, cot, gate[0], up[0], down[...], gate_o[...], up_o[...], down_o[...])


def expert_post_body(s, mine, other, gate, up, down, gate_o, up_o, down_o, out, hid, gg, gu):
    j = pl.program_id(0)
    n = hid.shape[0]
    m = n // 2
    w = gate.shape[2]

    @pl.when(j == 0)
    def _():
        a = joined(mine[0:n], other[0:n])
        b = joined(mine[n : 2 * n], other[n : 2 * n])
        dh = joined(mine[2 * n : 2 * n + m], other[2 * n : 2 * n + m])
        r = lax.broadcasted_iota(I32, (n, m), 0)
        c = lax.broadcasted_iota(I32, (n, m), 1)
        place = jnp.where(c == (r // 8) * CAP + r % CAP, 1.0, 0.0)
        dh = jnp.dot(place, dh, precision=lax.Precision.HIGHEST, preferred_element_type=F32)
        back = (lax.broadcasted_iota(I32, (n, 1), 0) // CAP) % 2 == 1
        sg = jax.nn.sigmoid(a)
        hid[...] = jnp.where(back, 0.0, a * sg * b).astype(BF)
        gg[...] = jnp.where(back, dh * b * (sg * (1.0 + a * (1.0 - sg))), 0.0).astype(BF)
        gu[...] = jnp.where(back, dh * (a * sg), 0.0).astype(BF)

    rows = (
        dot(hid[:, :w], down[...]) + dot(hid[:, w:], down_o[...])
        + contract_last(gg[:, :w], gate[0]) + contract_last(gg[:, w:], gate_o[...])
        + contract_last(gu[:, :w], up[0]) + contract_last(gu[:, w:], up_o[...])
    ).astype(BF)
    out[0, 0] = rows[:m]
    out[1, 0] = rows[m:]


def merge_body(s, back, keep, far, add_hi, add_lo, add_b, out, grad):
    rows = back[...]
    out[...] = (keep[0] + far[0].astype(F32) + (dot(add_hi[...], rows) + dot(add_lo[...], rows))).astype(BF)
    grad[...] = (keep[1] + far[1].astype(F32) + dot(add_b[...], rows)).astype(BF)


def local(inputs_prev, cotangent_next, saved_input, expert_ids, keep_mask, slot_pos, weight_q,
          gate_routed, up_routed, down_routed, gate_shared, up_shared, down_shared):
    tokens, shard = inputs_prev.shape[1:]
    experts = lax.axis_size("y")
    here = jnp.stack([lax.axis_index("xl"), lax.axis_index("core")]).astype(I32)
    saved = saved_input[0]
    gs = gate_shared[0].reshape(4, shard, -1)
    us = up_shared[0].reshape(4, shard, -1)
    ds = down_shared[0]
    gr = gate_routed[0, 0].reshape(4, shard, -1)
    ur = up_routed[0, 0].reshape(4, shard, -1)
    dr = down_routed[0, 0]
    fs = gs.shape[2]
    fe = gr.shape[2]

    fwd = shifted(inputs_prev[0], "pipe", 1)
    cot = shifted(cotangent_next[0], "pipe", -1)
    far_s = swapped(saved, "xl")

    def rows_at(n, which):
        return pl.BlockSpec((1, shard, n), lambda j, s: (which(j, s), 0, 0))

    def cols_at(n, which):
        return pl.BlockSpec((n, shard), lambda j, s: (0, which(j, s)))

    theirs = lambda j, s: 2 * j + 1 - s[1]
    in_side, out_side = call(
        pack_body, "pack",
        (shape_of(BF, 2 * shard, 2 * fs + 2 * fe), shape_of(BF, fs + fe, 2 * shard)), grid=(2,),
        in_specs=[rows_at(fs, theirs), rows_at(fs, theirs), rows_at(fe, theirs), rows_at(fe, theirs),
                  cols_at(fs, theirs), cols_at(fe, theirs)],
        out_specs=(pl.BlockSpec((shard, 2 * fs + 2 * fe), lambda j, s: (j, 0)),
                   pl.BlockSpec((fs + fe, shard), lambda j, s: (0, j))),
    )(here, gs, us, gr, ur, ds, dr)
    in_side = swapped(in_side, "core")
    out_side = swapped(out_side, "core")

    def turned(v):
        return v[:, 0].transpose(0, 2, 1)

    sq = shape_of(BF, tokens, tokens)
    tall = shape_of(BF, tokens, 8 * experts)
    tab = whole((2, expert_ids.shape[3], tokens))
    sel_f, sel_s, sel_c, scale, add_hi, add_lo, add_b = call(
        tables_body, "tables", (sq, sq, sq, shape_of(F32, tokens, 1), tall, tall, tall),
        in_specs=[tab] * 4,
        out_specs=(whole(sq.shape),) * 3 + (whole((tokens, 1)),) + (whole(tall.shape),) * 3,
    )(here, turned(expert_ids), turned(keep_mask), turned(slot_pos), turned(weight_q))

    act = whole((tokens, shard))
    parcel = call(
        parcel_body, "parcel", shape_of(BF, tokens, shard),
        in_specs=[whole(sq.shape)] * 3 + [whole((tokens, 1))] + [act] * 3, out_specs=act,
    )(here, sel_f, sel_s, sel_c, scale, fwd, saved, cot)
    parcel = lax.all_to_all(parcel.reshape(experts, PAD, shard), "y", 0, 0, tiled=True)
    rows = experts * 3 * CAP
    fan = call(
        fan_body, "fan", shape_of(BF, 4, rows, shard),
        in_specs=[act], out_specs=whole((4, rows, shard)),
    )(here, parcel.reshape(tokens, shard))
    got = lax.all_to_all(fan, ("xh", "xl"), 0, 0, tiled=True).reshape(2, 2, rows, shard)

    far_f = swapped(fwd, "xl")
    far_c = swapped(cot, "xl")

    def weight_specs(fw, block, at, mine):
        lane = block * 2
        return [rows_at(fw, mine), rows_at(fw, mine), cols_at(fw, mine),
                pl.BlockSpec((shard, fw), lambda j, s: (at(j, s), lane)),
                pl.BlockSpec((shard, fw), lambda j, s: (at(j, s), lane + 1)),
                pl.BlockSpec((fw, shard), lambda j, s: (lane, at(j, s)))]

    def near_first(j, s):
        return (s[0] + j) % 2

    def far_first(j, s):
        return (s[0] + 1 + j) % 2

    def straight(j, s):
        return j

    def own(at):
        return lambda j, s: 2 * at(j, s) + s[1]

    shared_w = (gs, us, ds, in_side, in_side, out_side)
    routed_w = (gr, ur, dr, in_side, in_side, out_side)

    z_s = call(
        shared_pre_body, "shared_pre", shape_of(F32, 5 * tokens, 2 * fs), grid=(2,),
        in_specs=[act] * 6 + weight_specs(fs, 0, near_first, own(near_first)),
        out_specs=whole((5 * tokens, 2 * fs)),
    )(here, fwd, saved, cot, far_f, far_s, far_c, *shared_w)
    z_s2 = swapped(z_s, "core")

    n_e = 2 * experts * 2 * CAP
    routed_specs = [rows_at(fe, own(straight)), rows_at(fe, own(straight)), cols_at(fe, own(straight)),
                    pl.BlockSpec((shard, fe), lambda j, s: (j, 2 * fs // fe)),
                    pl.BlockSpec((shard, fe), lambda j, s: (j, 2 * fs // fe + 1)),
                    pl.BlockSpec((fe, shard), lambda j, s: (fs // fe, j))]
    z_e = call(
        expert_pre_body, "expert_pre", shape_of(F32, 5 * n_e // 2, 2 * fe), grid=(2,),
        in_specs=[pl.BlockSpec((2, 1, rows, shard), lambda j, s: (0, j, 0, 0))] + routed_specs,
        out_specs=whole((5 * n_e // 2, 2 * fe)),
    )(here, got, *routed_w)
    z_e2 = swapped(z_e, "core")

    ret = call(
        expert_post_body, "expert_post", shape_of(BF, 2, 2, n_e // 2, shard), grid=(2,),
        in_specs=[whole(z_e.shape)] * 2 + routed_specs,
        out_specs=pl.BlockSpec((2, 1, n_e // 2, shard), lambda j, s: (0, j, 0, 0)),
        scratch=[pltpu.VMEM((n_e, 2 * fe), BF)] * 3,
    )(here, z_e, z_e2, *routed_w)
    ret = lax.all_to_all(ret.reshape(4, n_e // 2, shard), ("xh", "xl"), 0, 0, tiled=True)
    ret = jnp.sum(ret.astype(F32), axis=0).astype(BF)
    ret = lax.all_to_all(ret.reshape(experts, 2 * CAP, shard), "y", 0, 0, tiled=True)

    send, keep = call(
        shared_post_body, "shared_post", (shape_of(BF, 2, tokens, shard), shape_of(F32, 2, tokens, shard)), grid=(2,),
        in_specs=[whole(z_s.shape)] * 2 + weight_specs(fs, 0, far_first, own(far_first)),
        out_specs=(whole((2, tokens, shard)), whole((2, tokens, shard))),
        scratch=[pltpu.VMEM((tokens, 2 * fs), BF)] * 3,
    )(here, z_s, z_s2, *shared_w)
    far = swapped(send, "xl")

    out, grad = call(
        merge_body, "merge", (shape_of(BF, tokens, shard),) * 2,
        in_specs=[whole((8 * experts, shard)), whole(keep.shape), whole(far.shape)] + [whole(tall.shape)] * 3,
        out_specs=(act, act),
    )(here, ret.reshape(8 * experts, shard), keep, far, add_hi, add_lo, add_b)
    return out[None], grad[None]


def solution(mesh):
    pipe, expert, tensor = mesh.devices.shape
    fine = Mesh(mesh.devices.reshape(pipe, expert // 2, 2, 2, tensor // 2), ("pipe", "y", "xh", "xl", "core"))
    e, t = ("y", "xh"), ("xl", "core")
    act = P("pipe", e, t)
    table = P(None, "pipe", e, None)
    return jax.shard_map(
        local,
        mesh=fine,
        in_specs=(act, act, act, table, table, table, table,
                  P("pipe", e, None, t), P("pipe", e, None, t), P("pipe", e, t, None),
                  P("pipe", None, t), P("pipe", None, t), P("pipe", t, None)),
        out_specs=(act, act),
        check_vma=False,
    )
```

time: 182 us -> 124 us (0.68)
  waiting for transfers between devices: 46.1 us -> 1.75 us
  Pallas kernels: 0 us -> 32.2 us
  blocking collectives: 6.13 us -> 29.1 us
  local copies, waits for them, and re-layouts: 29.8 us -> 7.7 us
  matrix products: 19.9 us -> 0 us
  starting transfers between devices: 67.7 us -> 50.8 us
  other arithmetic: 9.22 us -> 0.15 us
    all_to_all x11 -> x2, waiting for transfers between devices: 46.1 us -> 0.01 us  [the longest x1 0.01 us: local(): lax.all_to_all(parcel.reshape(experts, PAD, shard), 'y', 0, 0, tiled=True)]
    all_to_all x11 -> x2, starting transfers between devices: 50.5 us -> 10.3 us  [the longest x1 6.83 us: local(): lax.all_to_all(parcel.reshape(experts, PAD, shard), 'y', 0, 0, tiled=True)]
    ppermute x0 -> x8, starting transfers between devices: none -> 33.3 us  [swapped(): return lax.ppermute(block, axis, [(0, 1), (1, 0)])]
    pallas_call x0 -> x9, Pallas kernels: none -> 32.2 us  [the longest x1 8.95 us: local(): call(shared_pre_body, 'shared_pre', shape_of(F32, 5 * tokens, 2 * fs), gr...]
    all_to_all x1 -> x2, blocking collectives: 6.13 us -> 29.1 us  [the longest x1 14.6 us: local(): lax.all_to_all(fan, ('xh', 'xl'), 0, 0, tiled=True)]
    dot_general x17 -> x0, matrix products: 19.9 us -> none  [the longest x9 9.38 us: dot(): return jnp.dot(a, b, preferred_element_type=F32)]
    another operation x11 -> x0, local copies, waits for them, and re-layouts: 11.9 us -> none  [the longest x4 10.1 us: local(): jnp.stack([out_s, grad_s]).reshape(2, tokens, 2, 2, shard)]
    ppermute x2, starting transfers between devices: 17.2 us -> 7.25 us  [shifted(): lax.ppermute(block, axis, [((i - distance) % n, i) for i in range(n)])]
  transfers between devices with their start and end apart: 13 -> 12, of which waited for: 8 -> 2; matrix products, arithmetic and copies ran while one was open for 26% -> 0% of each run, Pallas kernels for 0% -> 22%
where the time goes in v2:
time: 124 us; the launch traced here: 123 us
  starting transfers between devices  50.8 us (41%)
  Pallas kernels  32.2 us (26%)
  blocking collectives  29.1 us (23%)
  local copies, waits for them, and re-layouts  7.7 us (6%)
  waiting for transfers between devices  1.75 us (1%)
    ppermute x8, starting transfers between devices, swapped(): return lax.ppermute(block, axis, [(0, 1), (1, 0)])  33.3 us
    all_to_all x1, blocking collectives, local(): lax.all_to_all(fan, ('xh', 'xl'), 0, 0, tiled=True)  14.6 us
    all_to_all x1, blocking collectives, local(): lax.all_to_all(ret.reshape(experts, 2 * CAP, shard), 'y', 0, 0, tiled=True)  14.5 us
    pallas_call x1, Pallas kernels, local(): call(shared_pre_body, 'shared_pre', shape_of(F32, 5 * tokens, 2 * fs), gr...  8.95 us
    unnamed x36, local copies, waits for them, and re-layouts  7.7 us
    ppermute x2, starting transfers between devices, shifted(): lax.ppermute(block, axis, [((i - distance) % n, i) for i in range(n)])  7.25 us
    all_to_all x1, starting transfers between devices, local(): lax.all_to_all(parcel.reshape(experts, PAD, shard), 'y', 0, 0, tiled=True)  6.83 us
    pallas_call x1, Pallas kernels, local(): call(shared_post_body, 'shared_post', (shape_of(BF, 2, tokens, shard), sh...  5.2 us
  transfers between devices with their start and end apart: 12, of which 2 were waited for; matrix products, arithmetic and copies ran while one was open for 0% of the time, Pallas kernels for 22%

profile of v2, /device:TPU:1, one launch (start us, length us, event | category | flops | bytes accessed | tf_op | source)
XLA Modules:
  0.0 122.7 jit_solution(3644565090675654874)
XLA Ops:
  0.7 1.5 %copy-done = bf16[1,3584,256]{2,1,0:T(8,128)(2,1)S(1)} copy-done((bf16[1,3584,256]{2,1,0:T(8,128)(2,1)S(1)}, bf16[1,3584,256]{2,1,0:T(8,128)(2,1)}, u32[]{:S(2)}) %copy-start) | copy-done | bytes 1835032
  2.2 1.2 copy-done.2
  3.4 1.2 copy-done.4
  4.6 1.2 copy-done.6
  5.8 4.2 %pack.1 = (bf16[1792,768]{1,0:T(8,128)(2,1)}, bf16[384,1792]{1,0:T(8,128)(2,1)}) custom-call(s32[2]{0:T(128)S(1)} %pad_add_fusion.s, bf16[4,896,256]{2,1,0:T(8,128)(2,1)S(1)} %bitcast.32, bf16[4,896,256]{2,1,0:T(8,128)(2,1)} %bitcast.54, bf16[4,896,128]{2,1,0:T(8,128)(2,1)S(1)} %bitcast.34, bf16[4,896,128]{2,1,0:T(8,128)(2,1)S(1)} %bitcast.37, ...), custom_call_target="tpu_custom_call" | custom-call | tf_op jit(solution)/shard_map/pack/pallas_call | solution.py:267
  10.0 12.4 %collective-permute-start.2 = (bf16[1792,768]{1,0:T(8,128)(2,1)}, bf16[1792,768]{1,0:T(8,128)(2,1)}, u32[]{:S(2)}, u32[]{:S(2)}) collective-permute-start(bf16[1792,768]{1,0:T(8,128)(2,1)} %get-tuple-element.19), channel_id=1, source_target_pairs={{0,1},{1,0},{2,3},{3,2},{4,5},{5,4},{6,7},{7,6},{8,9},{9,8},{10,11... | collective-permute-start | bytes 8257544 | tf_op jit(solution)/shard_map/ppermute | solution.py:42
  22.4 1.9 %collective-permute-start.3 = (bf16[384,1792]{1,0:T(8,128)(2,1)}, bf16[384,1792]{1,0:T(8,128)(2,1)S(1)}, u32[]{:S(2)}, u32[]{:S(2)}) collective-permute-start(bf16[384,1792]{1,0:T(8,128)(2,1)} %get-tuple-element.20), channel_id=1, source_target_pairs={{0,1},{1,0},{2,3},{3,2},{4,5},{5,4},{6,7},{7,6},{8,9},{9,8},{10,11... | collective-permute-start | bytes 4128776 | tf_op jit(solution)/shard_map/ppermute | solution.py:42
  24.3 1.9 %collective-permute-start = (bf16[128,896]{1,0:T(8,128)(2,1)S(1)}, bf16[128,896]{1,0:T(8,128)(2,1)}, u32[]{:S(2)}, u32[]{:S(2)}) collective-permute-start(bf16[128,896]{1,0:T(8,128)(2,1)S(1)} %bitcast.61), channel_id=1, source_target_pairs={{704,0},{0,64},{64,128},{128,192},{192,256},{256,320},{320,384},{3... | collective-permute-start | bytes 688136 | tf_op jit(solution)/shard_map/ppermute | solution.py:38
  26.3 5.3 %collective-permute-start.1 = (bf16[128,896]{1,0:T(8,128)(2,1)S(1)}, bf16[128,896]{1,0:T(8,128)(2,1)}, u32[]{:S(2)}, u32[]{:S(2)}) collective-permute-start(bf16[128,896]{1,0:T(8,128)(2,1)S(1)} %bitcast.62), channel_id=1, source_target_pairs={{64,0},{128,64},{192,128},{256,192},{320,256},{384,320},{448,384},... | collective-permute-start | bytes 688136 | tf_op jit(solution)/shard_map/ppermute | solution.py:38
  31.6 3.1 %collective-permute-start.6 = (bf16[128,896]{1,0:T(8,128)(2,1)S(1)}, bf16[128,896]{1,0:T(8,128)(2,1)}, u32[]{:S(2)}, u32[]{:S(2)}) collective-permute-start(bf16[128,896]{1,0:T(8,128)(2,1)S(1)} %bitcast.45), channel_id=1, source_target_pairs={{0,2},{2,0},{1,3},{3,1},{4,6},{6,4},{5,7},{7,5},{8,10},{10,8},{9,1... | collective-permute-start | bytes 688136 | tf_op jit(solution)/shard_map/ppermute | solution.py:42
  34.7 0.5 collective-permute-done.fwd.own_f
  35.2 3.1 %collective-permute-start.5 = (bf16[128,896]{1,0:T(8,128)(2,1)}, bf16[128,896]{1,0:T(8,128)(2,1)}, u32[]{:S(2)}, u32[]{:S(2)}) collective-permute-start(bf16[128,896]{1,0:T(8,128)(2,1)} %collective-permute-done.fwd.own_f), channel_id=1, source_target_pairs={{0,2},{2,0},{1,3},{3,1},{4,6},{6,4},{5,7},{7,5},{8,10},{10,8},{9,1... | collective-permute-start | bytes 688136 | tf_op jit(solution)/shard_map/ppermute | solution.py:42
  38.4 2.2 %collective-permute-start.7 = (bf16[128,896]{1,0:T(8,128)(2,1)}, bf16[128,896]{1,0:T(8,128)(2,1)}, u32[]{:S(2)}, u32[]{:S(2)}) collective-permute-start(bf16[128,896]{1,0:T(8,128)(2,1)} %collective-permute-done.1.cot.own_c), channel_id=1, source_target_pairs={{0,2},{2,0},{1,3},{3,1},{4,6},{6,4},{5,7},{7,5},{8,10},{10,8},{9,1... | collective-permute-start | bytes 688136 | tf_op jit(solution)/shard_map/ppermute | solution.py:42
  40.6 0.9 tables.1
  41.4 1.9 %parcel.1 = bf16[128,896]{1,0:T(8,128)(2,1)S(1)} custom-call(s32[2]{0:T(128)S(1)} %pad_add_fusion.s, bf16[128,128]{1,0:T(8,128)(2,1)S(1)} %get-tuple-element.15.sel_f, bf16[128,128]{1,0:T(8,128)(2,1)S(1)} %get-tuple-element.16.sel_s, bf16[128,128]{1,0:T(8,128)(2,1)S(1)} %get-tuple-element.17.sel_c, f32[128,1]{1,0:T(8,128)S(1)} %get-tuple-element.18.scale, ...), custom_call_target="tpu_custom_call" | custom-call | tf_op jit(solution)/shard_map/parcel/pallas_call | solution.py:291
  43.4 0.7 copy-done.11
  44.0 6.8 %all-to-all-start = ((bf16[8,16,896]{2,1,0:T(8,128)(2,1)}), bf16[8,16,896]{2,1,0:T(8,128)(2,1)}, u32[]{:S(2)}, u32[]{:S(2)}) async-start(bf16[8,16,896]{2,1,0:T(8,128)(2,1)} %bitcast.48), calls=%async_computation | async-start | bytes 458752 | tf_op jit(solution)/shard_map/all_to_all | solution.py:295
  50.9 9.0 %shared_pre.1.mine = f32[640,512]{1,0:T(8,128)} custom-call(s32[2]{0:T(128)S(1)} %pad_add_fusion.s, bf16[128,896]{1,0:T(8,128)(2,1)} %collective-permute-done.fwd.own_f, bf16[128,896]{1,0:T(8,128)(2,1)S(1)} %bitcast.47, bf16[128,896]{1,0:T(8,128)(2,1)} %collective-permute-done.1.cot.own_c, bf16[128,896]{1,0:T(8,128)(2,1)} %collective-permute-done.5.far_f, ...), custom_call_target="tpu_custom_call" | custom-call | tf_op jit(solution)/shard_map/shared_pre/pallas_call | solution.py:328
  59.9 3.9 %collective-permute-start.8 = (f32[640,512]{1,0:T(8,128)}, f32[640,512]{1,0:T(8,128)}, u32[]{:S(2)}, u32[]{:S(2)}) collective-permute-start(f32[640,512]{1,0:T(8,128)} %shared_pre.1.mine), channel_id=1, source_target_pairs={{0,1},{1,0},{2,3},{3,2},{4,5},{5,4},{6,7},{7,6},{8,9},{9,8},{10,11... | collective-permute-start | bytes 3932168 | tf_op jit(solution)/shard_map/ppermute | solution.py:42
  63.9 1.7 %fan.1 = bf16[4,96,896]{2,1,0:T(8,128)(2,1)S(1)} custom-call(s32[2]{0:T(128)S(1)} %pad_add_fusion.s, bf16[128,896]{1,0:T(8,128)(2,1)} %bitcast.14.got), custom_call_target="tpu_custom_call" | custom-call | tf_op jit(solution)/shard_map/fan/pallas_call | solution.py:297
  65.5 14.6 %all_to_all.20 = bf16[4,96,896]{2,1,0:T(8,128)(2,1)S(1)} all-to-all(bf16[4,96,896]{2,1,0:T(8,128)(2,1)S(1)} %fan.1), channel_id=1, replica_groups=mesh['pipe'=12,'y'=8,'xh'=2,'xl'=2,'core'=2] {'xh','xl'}, dimensions={0} | all-to-all | bytes 1376256 | tf_op jit(solution)/shard_map/all_to_all | solution.py:301
  80.2 1.2 copy-done.7
  81.3 4.7 %expert_pre.1.mine = f32[320,256]{1,0:T(8,128)S(1)} custom-call(s32[2]{0:T(128)S(1)} %pad_add_fusion.s, bf16[2,2,96,896]{3,2,1,0:T(8,128)(2,1)S(1)} %bitcast.43, bf16[4,896,128]{2,1,0:T(8,128)(2,1)S(1)} %bitcast.35, bf16[4,896,128]{2,1,0:T(8,128)(2,1)S(1)} %bitcast.38, bf16[128,3584]{1,0:T(8,128)(2,1)S(1)} %bitcast.41, ...), custom_call_target="tpu_custom_call" | custom-call | tf_op jit(solution)/shard_map/expert_pre/pallas_call | solution.py:340
  86.1 3.3 %collective-permute-start.4 = (f32[320,256]{1,0:T(8,128)S(1)}, f32[320,256]{1,0:T(8,128)S(1)}, u32[]{:S(2)}, u32[]{:S(2)}) collective-permute-start(f32[320,256]{1,0:T(8,128)S(1)} %expert_pre.1.mine), channel_id=1, source_target_pairs={{0,1},{1,0},{2,3},{3,2},{4,5},{5,4},{6,7},{7,6},{8,9},{9,8},{10,11... | collective-permute-start | bytes 983048 | tf_op jit(solution)/shard_map/ppermute | solution.py:42
  89.4 1.2 %collective-permute-done.4.other = f32[320,256]{1,0:T(8,128)S(1)} collective-permute-done((f32[320,256]{1,0:T(8,128)S(1)}, f32[320,256]{1,0:T(8,128)S(1)}, u32[]{:S(2)}, u32[]{:S(2)}) %collective-permute-start.4) | collective-permute-done | bytes 327712 | tf_op jit(solution)/shard_map/ppermute | solution.py:42
  90.6 3.1 %expert_post.1 = bf16[2,2,64,896]{3,2,1,0:T(8,128)(2,1)S(1)} custom-call(s32[2]{0:T(128)S(1)} %pad_add_fusion.s, f32[320,256]{1,0:T(8,128)S(1)} %expert_pre.1.mine, f32[320,256]{1,0:T(8,128)S(1)} %collective-permute-done.4.other, bf16[4,896,128]{2,1,0:T(8,128)(2,1)S(1)} %bitcast.36, bf16[4,896,128]{2,1,0:T(8,128)(2,1)S(1)} %bitcast.39, ...), custom_call_target="tpu_custom_call" | custom-call | tf_op jit(solution)/shard_map/expert_post/pallas_call | solution.py:347
  93.7 0.8 copy-done.9
  94.5 3.5 %all-to-all-start.2 = ((bf16[4,64,896]{2,1,0:T(8,128)(2,1)}), bf16[4,64,896]{2,1,0:T(8,128)(2,1)S(1)}, u32[]{:S(2)}, u32[]{:S(2)}) async-start(bf16[4,64,896]{2,1,0:T(8,128)(2,1)} %bitcast.44), calls=%async_computation.2 | async-start | bytes 917504 | tf_op jit(solution)/shard_map/all_to_all | solution.py:353
  98.0 5.2 %shared_post.1 = (bf16[2,128,896]{2,1,0:T(8,128)(2,1)S(1)}, f32[2,128,896]{2,1,0:T(8,128)S(1)}) custom-call(s32[2]{0:T(128)S(1)} %pad_add_fusion.s, f32[640,512]{1,0:T(8,128)} %shared_pre.1.mine, f32[640,512]{1,0:T(8,128)} %collective-permute-done.8.other, bf16[4,896,256]{2,1,0:T(8,128)(2,1)} %bitcast.31, bf16[4,896,256]{2,1,0:T(8,128)(2,1)} %bitcast.56, ...), custom_call_target="tpu_custom_call" | custom-call | tf_op jit(solution)/shard_map/shared_post/pallas_call | solution.py:357
  103.2 3.3 %collective-permute-start.9 = (bf16[2,128,896]{2,1,0:T(8,128)(2,1)S(1)}, bf16[2,128,896]{2,1,0:T(8,128)(2,1)S(1)}, u32[]{:S(2)}, u32[]{:S(2)}) collective-permute-start(bf16[2,128,896]{2,1,0:T(8,128)(2,1)S(1)} %get-tuple-element.22), channel_id=1, source_target_pairs={{0,2},{2,0},{1,3},{3,1},{4,6},{6,4},{5,7},{7,5},{8,10},{10,8},{9,1... | collective-permute-start | bytes 1376264 | tf_op jit(solution)/shard_map/ppermute | solution.py:42
  106.6 14.5 %all_to_all.21 = bf16[8,8,896]{2,1,0:T(8,128)(2,1)S(1)} all-to-all(bf16[8,8,896]{2,1,0:T(8,128)(2,1)S(1)} %bitcast.60), channel_id=1, replica_groups=mesh['pipe'=12,'y'=8,'xh'=2,'xl'=2,'core'=2] {'y'}, dimensions={0} | all-to-all | bytes 229376 | tf_op jit(solution)/shard_map/all_to_all | solution.py:355
  121.1 1.6 %merge.1 = (bf16[128,896]{1,0:T(8,128)(2,1)}, bf16[128,896]{1,0:T(8,128)(2,1)}) custom-call(s32[2]{0:T(128)S(1)} %pad_add_fusion.s, bf16[64,896]{1,0:T(8,128)(2,1)S(1)} %bitcast.49, f32[2,128,896]{2,1,0:T(8,128)S(1)} %get-tuple-element.21.keep, bf16[2,128,896]{2,1,0:T(8,128)(2,1)S(1)} %collective-permute-done.9.far, ...), custom_call_target="tpu_custom_call" | custom-call | tf_op jit(solution)/shard_map/merge/pallas_call | solution.py:365
  (41 shorter events, 0.2 us)
Async XLA Ops:
  0.7 1.5 %copy-start = (bf16[1,3584,256]{2,1,0:T(8,128)(2,1)S(1)}, bf16[1,3584,256]{2,1,0:T(8,128)(2,1)}, u32[]{:S(2)}) copy-start(bf16[1,3584,256]{2,1,0:T(8,128)(2,1)} %param.23) | copy-start | bytes 5505028
  2.2 1.2 copy-start.2
  3.4 1.2 copy-start.4
  4.6 1.2 copy-start.6
  5.7 18.6 %copy-start.16 = (bf16[1,128,896]{2,1,0:T(8,128)(2,1)S(1)}, bf16[1,128,896]{2,1,0:T(8,128)(2,1)}, u32[]{:S(2)}) copy-start(bf16[1,128,896]{2,1,0:T(8,128)(2,1)} %param.13) | copy-start | bytes 688132
  5.8 20.5 %copy-start.17 = (bf16[1,128,896]{2,1,0:T(8,128)(2,1)S(1)}, bf16[1,128,896]{2,1,0:T(8,128)(2,1)}, u32[]{:S(2)}) copy-start(bf16[1,128,896]{2,1,0:T(8,128)(2,1)} %param.14) | copy-start | bytes 688132
  5.8 25.8 %copy-start.10 = (bf16[1,128,896]{2,1,0:T(8,128)(2,1)S(1)}, bf16[1,128,896]{2,1,0:T(8,128)(2,1)}, u32[]{:S(2)}) copy-start(bf16[1,128,896]{2,1,0:T(8,128)(2,1)} %param.15) | copy-start | bytes 688132
  5.8 34.8 %copy-start.12 = (s32[2,1,128,8]{2,3,1,0:T(8,128)S(1)}, s32[2,1,128,8]{2,3,1,0:T(8,128)}, u32[]{:S(2)}) copy-start(s32[2,1,128,8]{2,3,1,0:T(8,128)} %param.16) | copy-start | bytes 24580
  5.8 34.8 %copy-start.13 = (s32[2,1,128,8]{2,3,1,0:T(8,128)S(1)}, s32[2,1,128,8]{2,3,1,0:T(8,128)}, u32[]{:S(2)}) copy-start(s32[2,1,128,8]{2,3,1,0:T(8,128)} %param.17) | copy-start | bytes 24580
  5.8 34.8 %copy-start.14 = (s32[2,1,128,8]{2,3,1,0:T(8,128)S(1)}, s32[2,1,128,8]{2,3,1,0:T(8,128)}, u32[]{:S(2)}) copy-start(s32[2,1,128,8]{2,3,1,0:T(8,128)} %param.18) | copy-start | bytes 24580
  5.8 34.8 %copy-start.15 = (s32[2,1,128,8]{2,3,1,0:T(8,128)S(1)}, s32[2,1,128,8]{2,3,1,0:T(8,128)}, u32[]{:S(2)}) copy-start(s32[2,1,128,8]{2,3,1,0:T(8,128)} %param.19) | copy-start | bytes 24580
  5.8 45.1 %copy-start.1 = (bf16[1,3584,256]{2,1,0:T(8,128)(2,1)S(1)}, bf16[1,3584,256]{2,1,0:T(8,128)(2,1)}, u32[]{:S(2)}) copy-start(bf16[1,3584,256]{2,1,0:T(8,128)(2,1)} %param.23) | copy-start | bytes 5505028
  10.0 40.9 %collective-permute-start.2 = (bf16[1792,768]{1,0:T(8,128)(2,1)}, bf16[1792,768]{1,0:T(8,128)(2,1)}, u32[]{:S(2)}, u32[]{:S(2)}) collective-permute-start(bf16[1792,768]{1,0:T(8,128)(2,1)} %get-tuple-element.19), channel_id=1, source_target_pairs={{0,1},{1,0},{2,3},{3,2},{4,5},{5,4},{6,7},{7,6},{8,9},{9,8},{10,11... | collective-permute-start | bytes 8257544 | tf_op jit(solution)/shard_map/ppermute | solution.py:42
  22.4 28.5 %collective-permute-start.3 = (bf16[384,1792]{1,0:T(8,128)(2,1)}, bf16[384,1792]{1,0:T(8,128)(2,1)S(1)}, u32[]{:S(2)}, u32[]{:S(2)}) collective-permute-start(bf16[384,1792]{1,0:T(8,128)(2,1)} %get-tuple-element.20), channel_id=1, source_target_pairs={{0,1},{1,0},{2,3},{3,2},{4,5},{5,4},{6,7},{7,6},{8,9},{9,8},{10,11... | collective-permute-start | bytes 4128776 | tf_op jit(solution)/shard_map/ppermute | solution.py:42
  24.3 10.9 %collective-permute-start = (bf16[128,896]{1,0:T(8,128)(2,1)S(1)}, bf16[128,896]{1,0:T(8,128)(2,1)}, u32[]{:S(2)}, u32[]{:S(2)}) collective-permute-start(bf16[128,896]{1,0:T(8,128)(2,1)S(1)} %bitcast.61), channel_id=1, source_target_pairs={{704,0},{0,64},{64,128},{128,192},{192,256},{256,320},{320,384},{3... | collective-permute-start | bytes 688136 | tf_op jit(solution)/shard_map/ppermute | solution.py:38
  26.3 12.1 %collective-permute-start.1 = (bf16[128,896]{1,0:T(8,128)(2,1)S(1)}, bf16[128,896]{1,0:T(8,128)(2,1)}, u32[]{:S(2)}, u32[]{:S(2)}) collective-permute-start(bf16[128,896]{1,0:T(8,128)(2,1)S(1)} %bitcast.62), channel_id=1, source_target_pairs={{64,0},{128,64},{192,128},{256,192},{320,256},{384,320},{448,384},... | collective-permute-start | bytes 688136 | tf_op jit(solution)/shard_map/ppermute | solution.py:38
  31.6 19.3 %collective-permute-start.6 = (bf16[128,896]{1,0:T(8,128)(2,1)S(1)}, bf16[128,896]{1,0:T(8,128)(2,1)}, u32[]{:S(2)}, u32[]{:S(2)}) collective-permute-start(bf16[128,896]{1,0:T(8,128)(2,1)S(1)} %bitcast.45), channel_id=1, source_target_pairs={{0,2},{2,0},{1,3},{3,1},{4,6},{6,4},{5,7},{7,5},{8,10},{10,8},{9,1... | collective-permute-start | bytes 688136 | tf_op jit(solution)/shard_map/ppermute | solution.py:42
  35.2 15.7 %collective-permute-start.5 = (bf16[128,896]{1,0:T(8,128)(2,1)}, bf16[128,896]{1,0:T(8,128)(2,1)}, u32[]{:S(2)}, u32[]{:S(2)}) collective-permute-start(bf16[128,896]{1,0:T(8,128)(2,1)} %collective-permute-done.fwd.own_f), channel_id=1, source_target_pairs={{0,2},{2,0},{1,3},{3,1},{4,6},{6,4},{5,7},{7,5},{8,10},{10,8},{9,1... | collective-permute-start | bytes 688136 | tf_op jit(solution)/shard_map/ppermute | solution.py:42
  38.4 12.5 %collective-permute-start.7 = (bf16[128,896]{1,0:T(8,128)(2,1)}, bf16[128,896]{1,0:T(8,128)(2,1)}, u32[]{:S(2)}, u32[]{:S(2)}) collective-permute-start(bf16[128,896]{1,0:T(8,128)(2,1)} %collective-permute-done.1.cot.own_c), channel_id=1, source_target_pairs={{0,2},{2,0},{1,3},{3,1},{4,6},{6,4},{5,7},{7,5},{8,10},{10,8},{9,1... | collective-permute-start | bytes 688136 | tf_op jit(solution)/shard_map/ppermute | solution.py:42
  43.4 0.7 copy-start.11
  44.0 19.8 %all-to-all-start = ((bf16[8,16,896]{2,1,0:T(8,128)(2,1)}), bf16[8,16,896]{2,1,0:T(8,128)(2,1)}, u32[]{:S(2)}, u32[]{:S(2)}) async-start(bf16[8,16,896]{2,1,0:T(8,128)(2,1)} %bitcast.48), calls=%async_computation | async-start | bytes 458752 | tf_op jit(solution)/shard_map/all_to_all | solution.py:295
  59.9 20.3 %copy-start.3 = (bf16[1,1,3584,128]{3,2,1,0:T(8,128)(2,1)S(1)}, bf16[1,1,3584,128]{3,2,1,0:T(8,128)(2,1)}, u32[]{:S(2)}) copy-start(bf16[1,1,3584,128]{3,2,1,0:T(8,128)(2,1)} %param.20) | copy-start | bytes 2752516
  59.9 20.3 %copy-start.5 = (bf16[1,1,3584,128]{3,2,1,0:T(8,128)(2,1)S(1)}, bf16[1,1,3584,128]{3,2,1,0:T(8,128)(2,1)}, u32[]{:S(2)}) copy-start(bf16[1,1,3584,128]{3,2,1,0:T(8,128)(2,1)} %param.21) | copy-start | bytes 2752516
  59.9 38.1 %collective-permute-start.8 = (f32[640,512]{1,0:T(8,128)}, f32[640,512]{1,0:T(8,128)}, u32[]{:S(2)}, u32[]{:S(2)}) collective-permute-start(f32[640,512]{1,0:T(8,128)} %shared_pre.1.mine), channel_id=1, source_target_pairs={{0,1},{1,0},{2,3},{3,2},{4,5},{5,4},{6,7},{7,6},{8,9},{9,8},{10,11... | collective-permute-start | bytes 3932168 | tf_op jit(solution)/shard_map/ppermute | solution.py:42
  80.2 1.2 copy-start.7
  81.3 9.3 %copy-start.8 = (bf16[1,1,128,3584]{3,2,1,0:T(8,128)(2,1)S(1)}, bf16[1,1,128,3584]{3,2,1,0:T(8,128)(2,1)}, u32[]{:S(2)}) copy-start(bf16[1,1,128,3584]{3,2,1,0:T(8,128)(2,1)} %param.22) | copy-start | bytes 2752516
  86.1 4.6 %collective-permute-start.4 = (f32[320,256]{1,0:T(8,128)S(1)}, f32[320,256]{1,0:T(8,128)S(1)}, u32[]{:S(2)}, u32[]{:S(2)}) collective-permute-start(f32[320,256]{1,0:T(8,128)S(1)} %expert_pre.1.mine), channel_id=1, source_target_pairs={{0,1},{1,0},{2,3},{3,2},{4,5},{5,4},{6,7},{7,6},{8,9},{9,8},{10,11... | collective-permute-start | bytes 983048 | tf_op jit(solution)/shard_map/ppermute | solution.py:42
  93.7 0.8 copy-start.9
  94.5 12.0 %all-to-all-start.2 = ((bf16[4,64,896]{2,1,0:T(8,128)(2,1)}), bf16[4,64,896]{2,1,0:T(8,128)(2,1)S(1)}, u32[]{:S(2)}, u32[]{:S(2)}) async-start(bf16[4,64,896]{2,1,0:T(8,128)(2,1)} %bitcast.44), calls=%async_computation.2 | async-start | bytes 917504 | tf_op jit(solution)/shard_map/all_to_all | solution.py:353
  103.2 17.9 %collective-permute-start.9 = (bf16[2,128,896]{2,1,0:T(8,128)(2,1)S(1)}, bf16[2,128,896]{2,1,0:T(8,128)(2,1)S(1)}, u32[]{:S(2)}, u32[]{:S(2)}) collective-permute-start(bf16[2,128,896]{2,1,0:T(8,128)(2,1)S(1)} %get-tuple-element.22), channel_id=1, source_target_pairs={{0,2},{2,0},{1,3},{3,1},{4,6},{6,4},{5,7},{7,5},{8,10},{10,8},{9,1... | collective-permute-start | bytes 1376264 | tf_op jit(solution)/shard_map/ppermute | solution.py:42

commit v3 on v2

v3 whole, which is shorter than its diff:
```python
import jax
import jax.numpy as jnp
from jax import lax
from jax.experimental import pallas as pl
from jax.experimental.pallas import tpu as pltpu
from jax.sharding import Mesh, PartitionSpec as P


BF = jnp.bfloat16
F32 = jnp.float32
I32 = jnp.int32
CAP = 4
PAD = 4 * CAP


def call(body, outs, grid=(1,), in_specs=None, out_specs=None, scratch=(), flops=0):
    spec = pltpu.PrefetchScalarGridSpec(
        num_scalar_prefetch=1, grid=grid, in_specs=in_specs, out_specs=out_specs, scratch_shapes=scratch
    )
    return pl.pallas_call(
        body, grid_spec=spec, out_shape=outs,
        cost_estimate=pl.CostEstimate(flops=flops, transcendentals=0, bytes_accessed=0),
        compiler_params=pltpu.CompilerParams(vmem_limit_bytes=20 * 2**20),
    )


def whole(shape):
    return pl.BlockSpec(shape, lambda j, s: (0,) * len(shape))


hbm = pl.BlockSpec(memory_space=pltpu.HBM)
anywhere = pl.BlockSpec(memory_space=pl.ANY)


def shape_of(dtype, *dims):
    return jax.ShapeDtypeStruct(dims, dtype)


def shifted(block, axis, distance):
    n = lax.axis_size(axis)
    return lax.ppermute(block, axis, [((i - distance) % n, i) for i in range(n)])


def swapped(block, axis):
    return lax.ppermute(block, axis, [(0, 1), (1, 0)])


def dot(a, b):
    return jnp.dot(a, b, preferred_element_type=F32)


def contract_last(left, right):
    return lax.dot_general(left, right, (((1,), (1,)), ((), ())), preferred_element_type=F32)


def tables_body(s, ids, keep, slot, wq, sel_f, sel_s, sel_c, scale):
    tokens = ids.shape[2]
    row = lax.broadcasted_iota(I32, (tokens, 1), 0)
    arr = (row // CAP) % 4
    slot_id = (row // PAD) * CAP + row % CAP
    want_f = jnp.where(arr == 0, slot_id, -1)
    want_b = jnp.where((arr == 1) | (arr == 2), slot_id, -1)
    hit_f = jnp.zeros((tokens, tokens), F32)
    hit_b = jnp.zeros((tokens, tokens), F32)
    weight = jnp.zeros((tokens, tokens), F32)
    target = jnp.where(keep[...] > 0, ids[...] * CAP + slot[...], -2)
    level = wq[1].astype(F32) * (1.0 / 4096.0)
    for k in range(ids.shape[1]):
        hit_f += jnp.where(target[0, k : k + 1] == want_f, 1.0, 0.0)
        eq = target[1, k : k + 1] == want_b
        hit_b += jnp.where(eq, 1.0, 0.0)
        weight += jnp.where(eq, level[k : k + 1], 0.0)
    sel_f[...] = hit_f.astype(BF)
    sel_s[...] = jnp.where(arr == 1, hit_b, 0.0).astype(BF)
    sel_c[...] = jnp.where(arr == 2, hit_b, 0.0).astype(BF)
    scale[...] = jnp.sum(weight, axis=1, keepdims=True)


def adders_body(s, ids, keep, slot, wq, add_hi, add_lo, add_b):
    tokens = ids.shape[2]
    back = add_b.shape[1]
    row = lax.broadcasted_iota(I32, (back, 1), 0)
    dirn = (row // CAP) % 2
    slot_id = (row // 8) * CAP + row % CAP
    back_f = jnp.where(dirn == 0, slot_id, -1)
    back_b = jnp.where(dirn == 1, slot_id, -1)
    hi = jnp.zeros((back, tokens), F32)
    lo = jnp.zeros((back, tokens), F32)
    one = jnp.zeros((back, tokens), F32)
    target = jnp.where(keep[...] > 0, ids[...] * CAP + slot[...], -2)
    level = wq[0]
    top = (level // 64) * 64
    high = top.astype(F32) * (1.0 / 4096.0)
    low = (level - top).astype(F32) * (1.0 / 4096.0)
    for k in range(ids.shape[1]):
        eq = target[0, k : k + 1] == back_f
        hi += jnp.where(eq, high[k : k + 1], 0.0)
        lo += jnp.where(eq, low[k : k + 1], 0.0)
        one += jnp.where(target[1, k : k + 1] == back_b, 1.0, 0.0)
    add_hi[...] = hi.T.astype(BF)
    add_lo[...] = lo.T.astype(BF)
    add_b[...] = one.T.astype(BF)


def parcel_body(s, sel_f, sel_s, sel_c, scale, fwd, saved, cot, out, pair):
    rows = dot(sel_f[...], fwd[...]) + dot(sel_s[...], saved[...]) + scale[...] * dot(sel_c[...], cot[...])
    out[...] = rows.astype(BF)
    pair[0] = fwd[...]
    pair[1] = cot[...]


def fan_body(s, got, out):
    n = got.shape[0]
    m = n * 3 // 4
    half = n // 2
    r = lax.broadcasted_iota(I32, (m, n), 0)
    c = lax.broadcasted_iota(I32, (m, n), 1)
    k = r - half
    source = jnp.where(r < half, (r // 8) * PAD + r % 8, (k // CAP) * PAD + 8 + k % CAP)
    rows = dot(jnp.where(c == source, 1.0, 0.0).astype(BF), got[...]).astype(BF)
    for i in range(out.shape[0]):
        out[i] = rows


def run(copies, sems):
    handles = [pltpu.make_async_copy(src, dst, sems.at[i]) for i, (src, dst) in enumerate(copies)]
    for h in handles:
        h.start()

    def wait(lo, hi):
        for h in handles[lo:hi]:
            h.wait()

    return wait


def pack_body(s, gs, us, gr, ur, ds, dr, box, hold, sems):
    w = gs.shape[2]
    n = gr.shape[2]
    f = gs.shape[1]
    wait = []
    for x in range(2):
        t = 2 * x + 1 - s[1]
        cols = pl.ds(pl.multiple_of(t * f, 128), f)
        h = hold.at[x]
        wait.append(run([
            (gs.at[t], h.at[0:f, 0:w]),
            (us.at[t], h.at[0:f, w : 2 * w]),
            (gr.at[t], h.at[0:f, 2 * w : 2 * w + n]),
            (ur.at[t], h.at[0:f, 2 * w + n : 2 * w + 2 * n]),
            (dr.at[:, cols], h.at[f : f + n]),
            (ds.at[:, cols], h.at[f + n :]),
        ], sems.at[7 * x :]))
    done = []
    for x in range(2):
        wait[x](0, 6)
        done.append(run([(hold.at[x], box.at[x])], sems.at[7 * x + 6 :]))
    for x in range(2):
        done[x](0, 1)


def weight_copies(s, order, gate, up, down, box, lane, row, g, u, d):
    f, w = gate.shape[1:]
    gates, ups, downs = [], [], []
    for i, x in enumerate(order):
        t = 2 * x + s[1]
        rows = slice(i * f, i * f + f)
        body = box.at[x, 0:f]
        gates += [(gate.at[t], g.at[rows, 0:w]), (body.at[:, lane : lane + w], g.at[rows, w : 2 * w])]
        ups += [(up.at[t], u.at[rows, 0:w]), (body.at[:, lane + w : lane + 2 * w], u.at[rows, w : 2 * w])]
        downs += [(down.at[:, pl.ds(pl.multiple_of(t * f, 128), f)], d.at[0:w, rows]),
                  (box.at[x, row : row + w], d.at[w : 2 * w, rows])]
    return gates, ups, downs


def joined(mine, other):
    w = mine.shape[1] // 2
    return jnp.concatenate([mine[:, :w] + other[:, w:], mine[:, w:] + other[:, :w]], axis=1)


def pre(wait, n_x, both, cot, g, u, d, acc):
    n = both.shape[0]
    wait(0, n_x + 4)
    acc[0:n] = dot(both[...], g[...])
    wait(n_x + 4, n_x + 8)
    acc[n : 2 * n] = dot(both[...], u[...])
    wait(n_x + 8, n_x + 12)
    acc[2 * n :] = contract_last(cot[...], d[...])


def shared_pre_body(s, fwd, saved, cot, far, far_s, gate, up, down, box, acc, x, g, u, d, sems):
    n, f = fwd.shape
    near, away = slice(0, f), slice(f, 2 * f)
    xs = [(fwd, x.at[0:n, near]), (saved, x.at[n : 2 * n, near]), (cot, x.at[2 * n :, near]),
          (far.at[0], x.at[0:n, away]), (far_s, x.at[n : 2 * n, away]), (far.at[1], x.at[2 * n :, away])]
    ws = weight_copies(s, (s[0], 1 - s[0]), gate, up, down, box, 0, f + gate.shape[2] // 2, g, u, d)
    wait = run(xs + ws[0] + ws[1] + ws[2], sems)
    pre(wait, len(xs), x.at[0 : 2 * n], x.at[2 * n :], g, u, d, acc)


def shared_post_body(s, mine, other, gate, up, down, gate_o, up_o, down_o, send, keep, hid, gg, gu):
    j = pl.program_id(0)
    n = hid.shape[0]
    w = gate.shape[2]

    @pl.when(j == 0)
    def _():
        a_f = joined(mine[0:n], other[0:n])
        a_s = joined(mine[n : 2 * n], other[n : 2 * n])
        b_f = joined(mine[2 * n : 3 * n], other[2 * n : 3 * n])
        b_s = joined(mine[3 * n : 4 * n], other[3 * n : 4 * n])
        dh = joined(mine[4 * n : 5 * n], other[4 * n : 5 * n])
        hid[...] = (a_f * jax.nn.sigmoid(a_f) * b_f).astype(BF)
        sg = jax.nn.sigmoid(a_s)
        gg[...] = (dh * b_s * (sg * (1.0 + a_s * (1.0 - sg)))).astype(BF)
        gu[...] = (dh * (a_s * sg)).astype(BF)

    out = dot(hid[:, :w], down[...]) + dot(hid[:, w:], down_o[0])
    grad = (
        contract_last(gg[:, :w], gate[0]) + contract_last(gg[:, w:], gate_o[0])
        + contract_last(gu[:, :w], up[0]) + contract_last(gu[:, w:], up_o[0])
    )

    @pl.when(j == 0)
    def _():
        send[0] = out.astype(BF)
        send[1] = grad.astype(BF)

    @pl.when(j == 1)
    def _():
        keep[0] = out
        keep[1] = grad


def expert_pre_body(s, got, gate, up, down, box, acc, both, cot, g, u, d, sems):
    n, f = both.shape[0] // 2, got.shape[3]
    m = cot.shape[0] // 2
    xs = []
    for h in range(2):
        for x in range(2):
            cols = slice(x * f, x * f + f)
            xs += [(got.at[h, x, 0:n], both.at[h * n : h * n + n, cols]),
                   (got.at[h, x, n:], cot.at[h * m : h * m + m, cols])]
    w = gate.shape[2]
    ws = weight_copies(s, (0, 1), gate, up, down, box, 4 * w, f, g, u, d)
    wait = run(xs + ws[0] + ws[1] + ws[2], sems)
    pre(wait, len(xs), both, cot, g, u, d, acc)


def expert_post_body(s, mine, other, gate, up, down, gate_o, up_o, down_o, out, hid, gg, gu):
    j = pl.program_id(0)
    n = hid.shape[0]
    m = n // 2
    w = gate.shape[2]

    @pl.when(j == 0)
    def _():
        a = joined(mine[0:n], other[0:n])
        b = joined(mine[n : 2 * n], other[n : 2 * n])
        dh = joined(mine[2 * n : 2 * n + m], other[2 * n : 2 * n + m])
        r = lax.broadcasted_iota(I32, (n, m), 0)
        c = lax.broadcasted_iota(I32, (n, m), 1)
        place = jnp.where(c == (r // 8) * CAP + r % CAP, 1.0, 0.0)
        dh = jnp.dot(place, dh, precision=lax.Precision.HIGHEST, preferred_element_type=F32)
        back = (lax.broadcasted_iota(I32, (n, 1), 0) // CAP) % 2 == 1
        sg = jax.nn.sigmoid(a)
        hid[...] = jnp.where(back, 0.0, a * sg * b).astype(BF)
        gg[...] = jnp.where(back, dh * b * (sg * (1.0 + a * (1.0 - sg))), 0.0).astype(BF)
        gu[...] = jnp.where(back, dh * (a * sg), 0.0).astype(BF)

    rows = (
        dot(hid[:, :w], down[...]) + dot(hid[:, w:], down_o[0])
        + contract_last(gg[:, :w], gate[0]) + contract_last(gg[:, w:], gate_o[0])
        + contract_last(gu[:, :w], up[0]) + contract_last(gu[:, w:], up_o[0])
    ).astype(BF)
    out[0, 0] = rows[:m]
    out[1, 0] = rows[m:]


def sum_body(s, parts, out):
    p = parts[...].astype(F32)
    out[...] = ((p[0] + p[1]) + (p[2] + p[3])).astype(BF)


def merge_body(s, back, keep, far, add_hi, add_lo, add_b, out, grad):
    rows = back[...]
    out[...] = (keep[0] + far[0].astype(F32) + (dot(add_hi[...], rows) + dot(add_lo[...], rows))).astype(BF)
    grad[...] = (keep[1] + far[1].astype(F32) + dot(add_b[...], rows)).astype(BF)


def local(inputs_prev, cotangent_next, saved_input, expert_ids, keep_mask, slot_pos, weight_q,
          gate_routed, up_routed, down_routed, gate_shared, up_shared, down_shared):
    tokens, shard = inputs_prev.shape[1:]
    experts = lax.axis_size("y")
    here = jnp.stack([lax.axis_index("xl"), lax.axis_index("core")]).astype(I32)
    saved = saved_input[0]
    gs = gate_shared[0].reshape(4, shard, -1)
    us = up_shared[0].reshape(4, shard, -1)
    ds = down_shared[0]
    gr = gate_routed[0, 0].reshape(4, shard, -1)
    ur = up_routed[0, 0].reshape(4, shard, -1)
    dr = down_routed[0, 0]
    gs, us, ds, gr, ur, dr = [pltpu.with_memory_space_constraint(w, pltpu.HBM) for w in (gs, us, ds, gr, ur, dr)]
    fs = gs.shape[2]
    fe = gr.shape[2]

    fwd = shifted(inputs_prev[0], "pipe", 1)
    cot = shifted(cotangent_next[0], "pipe", -1)
    far_s = swapped(saved, "xl")

    def rows_at(n, which):
        return pl.BlockSpec((1, shard, n), lambda j, s: (which(j, s), 0, 0))

    def cols_at(n, which):
        return pl.BlockSpec((n, shard), lambda j, s: (0, which(j, s)))

    height = shard + fe + fs
    box = call(
        pack_body, pltpu.HBM((2, height, shard), BF), in_specs=[hbm] * 6, out_specs=hbm,
        scratch=[pltpu.VMEM((2, height, shard), BF), pltpu.SemaphoreType.DMA((14,))],
    )(here, gs, us, gr, ur, ds, dr)
    box = swapped(box, "core")

    def turned(v):
        return pltpu.with_memory_space_constraint(v[:, 0].transpose(0, 2, 1), pltpu.HBM)

    sq = shape_of(BF, tokens, tokens)
    tall = shape_of(BF, tokens, 8 * experts)
    tab = whole((2, expert_ids.shape[3], tokens))
    plan = [turned(v) for v in (expert_ids, keep_mask, slot_pos, weight_q)]
    sel_f, sel_s, sel_c, scale = call(
        tables_body, (sq, sq, sq, shape_of(F32, tokens, 1)),
        in_specs=[tab] * 4, out_specs=(whole(sq.shape),) * 3 + (whole((tokens, 1)),),
    )(here, *plan)
    add_hi, add_lo, add_b = call(
        adders_body, (tall, tall, tall), in_specs=[tab] * 4, out_specs=(whole(tall.shape),) * 3,
    )(here, *plan)

    act = whole((tokens, shard))
    parcel, pair = call(
        parcel_body, (pltpu.HBM((tokens, shard), BF), pltpu.HBM((2, tokens, shard), BF)),
        in_specs=[whole(sq.shape)] * 3 + [whole((tokens, 1))] + [act] * 3, out_specs=(act, whole((2, tokens, shard))),
    )(here, sel_f, sel_s, sel_c, scale, fwd, saved, cot)
    parcel = lax.all_to_all(parcel.reshape(experts, PAD, shard), "y", 0, 0, tiled=True)
    rows = experts * 3 * CAP
    fan = call(
        fan_body, pltpu.HBM((4, rows, shard), BF),
        in_specs=[act], out_specs=whole((4, rows, shard)),
    )(here, parcel.reshape(tokens, shard))
    got = lax.all_to_all(fan, ("xh", "xl"), 0, 0, tiled=True).reshape(2, 2, rows, shard)

    far_fc = swapped(pair, "xl")

    def buffers(w):
        return [pltpu.VMEM((2 * shard, 2 * w), BF)] * 2 + [pltpu.VMEM((2 * w, 2 * shard), BF)]

    def weight_specs(w, lane, row, at):
        mine = lambda j, s: 2 * at(j, s) + s[1]
        return [rows_at(w, mine), rows_at(w, mine), cols_at(w, mine),
                pl.BlockSpec((1, shard, w), lambda j, s: (at(j, s), 0, lane)),
                pl.BlockSpec((1, shard, w), lambda j, s: (at(j, s), 0, lane + 1)),
                pl.BlockSpec((1, w, shard), lambda j, s: (at(j, s), row, 0))]

    far_first = lambda j, s: (s[0] + 1 + j) % 2
    straight = lambda j, s: j

    def sems(n):
        return [pltpu.SemaphoreType.DMA((n,))]

    shared_w = (gs, us, ds, box)
    shared_w2 = (gs, us, ds, box, box, box)
    routed_w = (gr, ur, dr, box)
    routed_w2 = (gr, ur, dr, box, box, box)
    z_shape = (5 * tokens, 2 * fs)
    z_s = call(
        shared_pre_body, shape_of(F32, *z_shape),
        in_specs=[anywhere] * 5 + [hbm] * 3 + [anywhere], out_specs=whole(z_shape),
        scratch=[pltpu.VMEM((3 * tokens, 2 * shard), BF)] + buffers(fs) + sems(18),
    )(here, fwd, saved, cot, far_fc, far_s, *shared_w)
    z_s2 = swapped(z_s, "core")

    n_e = 2 * experts * 2 * CAP
    ze_shape = (5 * n_e // 2, 2 * fe)
    z_e = call(
        expert_pre_body, shape_of(F32, *ze_shape),
        in_specs=[anywhere] + [hbm] * 3 + [anywhere], out_specs=whole(ze_shape),
        scratch=[pltpu.VMEM((n_e, 2 * shard), BF), pltpu.VMEM((n_e // 2, 2 * shard), BF)] + buffers(fe) + sems(20),
    )(here, got, *routed_w)
    z_e2 = swapped(z_e, "core")

    ret = call(
        expert_post_body, pltpu.HBM((2, 2, n_e // 2, shard), BF), grid=(2,),
        in_specs=[whole(ze_shape)] * 2 + weight_specs(fe, 2 * fs // fe, shard // fe, straight),
        out_specs=pl.BlockSpec((2, 1, n_e // 2, shard), lambda j, s: (0, j, 0, 0)),
        scratch=[pltpu.VMEM((n_e, 2 * fe), BF)] * 3,
    )(here, z_e, z_e2, *routed_w2)
    ret = lax.all_to_all(ret.reshape(4, n_e // 2, shard), ("xh", "xl"), 0, 0, tiled=True)
    ret = call(
        sum_body, pltpu.HBM((n_e // 2, shard), BF),
        in_specs=[whole((4, n_e // 2, shard))], out_specs=whole((n_e // 2, shard)),
    )(here, ret)
    ret = lax.all_to_all(ret.reshape(experts, 2 * CAP, shard), "y", 0, 0, tiled=True)

    send, keep = call(
        shared_post_body, (pltpu.HBM((2, tokens, shard), BF), pltpu.HBM((2, tokens, shard), F32)), grid=(2,),
        in_specs=[whole(z_shape)] * 2 + weight_specs(fs, 0, (shard + fe) // fs, far_first),
        out_specs=(whole((2, tokens, shard)),) * 2,
        scratch=[pltpu.VMEM((tokens, 2 * fs), BF)] * 3,
    )(here, z_s, z_s2, *shared_w2)
    far = swapped(send, "xl")

    keep = pltpu.with_memory_space_constraint(keep, pltpu.HBM)
    out, grad = call(
        merge_body, (shape_of(BF, tokens, shard),) * 2,
        in_specs=[whole((8 * experts, shard)), whole(keep.shape), whole(far.shape)] + [whole(tall.shape)] * 3,
        out_specs=(act, act),
    )(here, ret.reshape(8 * experts, shard), keep, far, add_hi, add_lo, add_b)
    return out[None], grad[None]


def solution(mesh):
    pipe, expert, tensor = mesh.devices.shape
    fine = Mesh(mesh.devices.reshape(pipe, expert // 2, 2, 2, tensor // 2), ("pipe", "y", "xh", "xl", "core"))
    e, t = ("y", "xh"), ("xl", "core")
    act = P("pipe", e, t)
    table = P(None, "pipe", e, None)

    def step(*args):
        return local(*args)

    step = jax.shard_map(
        step,
        mesh=fine,
        in_specs=(act, act, act, table, table, table, table,
                  P("pipe", e, None, t), P("pipe", e, None, t), P("pipe", e, t, None),
                  P("pipe", None, t), P("pipe", None, t), P("pipe", t, None)),
        out_specs=(act, act),
        check_vma=False,
    )


    return step
```

time: 124 us -> 118 us (0.952)
  waiting for transfers between devices: 1.75 us -> 17.1 us
  blocking collectives: 29.1 us -> 14.8 us
  local copies, waits for them, and re-layouts: 7.7 us -> 0.01 us
  starting transfers between devices: 50.8 us -> 52.3 us
    all_to_all x1 -> x0, blocking collectives: 14.5 us -> none  [local(): lax.all_to_all(ret.reshape(experts, 2 * CAP, shard), 'y', 0, 0, tiled=True)]
    unnamed x36 -> x6, local copies, waits for them, and re-layouts: 7.7 us -> 0.01 us
    all_to_all x0 -> x1, starting transfers between devices: none -> 6.83 us  [local(): lax.all_to_all(ret.reshape(experts, 2 * CAP, shard), 'y', 0, 0, tiled=True)]
    all_to_all x0 -> x1, waiting for transfers between devices: none -> 6.38 us  [local(): lax.all_to_all(ret.reshape(experts, 2 * CAP, shard), 'y', 0, 0, tiled=True)]
    ppermute x8 -> x6, waiting for transfers between devices: 1.25 us -> 7.35 us  [swapped(): return lax.ppermute(block, axis, [(0, 1), (1, 0)])]
    ppermute x8 -> x6, starting transfers between devices: 33.3 us -> 27.9 us  [swapped(): return lax.ppermute(block, axis, [(0, 1), (1, 0)])]
    ppermute x2, waiting for transfers between devices: 0.5 us -> 3.41 us  [shifted(): lax.ppermute(block, axis, [((i - distance) % n, i) for i in range(n)])]
    pallas_call x9 -> x11, Pallas kernels: 32.2 us -> 31.8 us  [the longest x1 5.53 us: local(): call(shared_post_body, (pltpu.HBM((2, tokens, shard), BF), pltpu.HBM((2,...]
  transfers between devices with their start and end apart: 12 -> 11, of which waited for: 2 -> 5; matrix products, arithmetic and copies ran while one was open for 0% -> 0% of each run, Pallas kernels for 22% -> 21%
where the time goes in v3:
time: 118 us; the launch traced here: 117 us
  starting transfers between devices  52.3 us (44%)
  Pallas kernels  31.8 us (27%)
  waiting for transfers between devices  17.1 us (14%)
  blocking collectives  14.8 us (13%)
    ppermute x6, starting transfers between devices, swapped(): return lax.ppermute(block, axis, [(0, 1), (1, 0)])  27.9 us
    all_to_all x1, blocking collectives, local(): lax.all_to_all(fan, ('xh', 'xl'), 0, 0, tiled=True)  14.8 us
    ppermute x6, waiting for transfers between devices, swapped(): return lax.ppermute(block, axis, [(0, 1), (1, 0)])  7.35 us
    ppermute x2, starting transfers between devices, shifted(): lax.ppermute(block, axis, [((i - distance) % n, i) for i in range(n)])  7.24 us
    all_to_all x1, starting transfers between devices, local(): lax.all_to_all(parcel.reshape(experts, PAD, shard), 'y', 0, 0, tiled=True)  6.83 us
    all_to_all x1, starting transfers between devices, local(): lax.all_to_all(ret.reshape(experts, 2 * CAP, shard), 'y', 0, 0, tiled=True)  6.83 us
    all_to_all x1, waiting for transfers between devices, local(): lax.all_to_all(ret.reshape(experts, 2 * CAP, shard), 'y', 0, 0, tiled=True)  6.38 us
    pallas_call x1, Pallas kernels, local(): call(shared_post_body, (pltpu.HBM((2, tokens, shard), BF), pltpu.HBM((2,...  5.53 us
  transfers between devices with their start and end apart: 11, of which 5 were waited for; matrix products, arithmetic and copies ran while one was open for 0% of the time, Pallas kernels for 21%

profile of v3, /device:TPU:1, one launch (start us, length us, event | category | flops | bytes accessed | tf_op | source)
XLA Modules:
  0.0 116.9 jit_solution(2774131513711165666)
XLA Ops:
  0.6 0.1 pad_add_fusion.s
  0.7 4.3 %shard_map.143 = bf16[2,1280,896]{2,1,0:T(8,128)(2,1)} custom-call(s32[2]{0:T(128)S(1)} %pad_add_fusion.s, bf16[4,896,256]{2,1,0:T(8,128)(2,1)} %bitcast.37, bf16[4,896,256]{2,1,0:T(8,128)(2,1)} %bitcast.40, bf16[4,896,128]{2,1,0:T(8,128)(2,1)} %bitcast.46, bf16[4,896,128]{2,1,0:T(8,128)(2,1)} %bitcast.49, bf16[256,3584]{1,0:T(8,128)(2,1)} %bitcast.43, ...), custom_call_target="tpu_custom_call" | custom-call | tf_op jit(solution)/shard_map/pallas_call | solution.py:318
  5.0 12.4 %collective-permute-start.2 = (bf16[2,1280,896]{2,1,0:T(8,128)(2,1)}, bf16[2,1280,896]{2,1,0:T(8,128)(2,1)}, u32[]{:S(2)}, u32[]{:S(2)}) collective-permute-start(bf16[2,1280,896]{2,1,0:T(8,128)(2,1)} %shard_map.143), channel_id=1, source_target_pairs={{0,1},{1,0},{2,3},{3,2},{4,5},{5,4},{6,7},{7,6},{8,9},{9,8},{10,11... | collective-permute-start | bytes 13762568 | tf_op jit(solution)/shard_map/ppermute | solution.py:45
  17.4 1.9 %collective-permute-start = (bf16[128,896]{1,0:T(8,128)(2,1)S(1)}, bf16[128,896]{1,0:T(8,128)(2,1)S(1)}, u32[]{:S(2)}, u32[]{:S(2)}) collective-permute-start(bf16[128,896]{1,0:T(8,128)(2,1)S(1)} %bitcast.66), channel_id=1, source_target_pairs={{704,0},{0,64},{64,128},{128,192},{192,256},{256,320},{320,384},{3... | collective-permute-start | bytes 688136 | tf_op jit(solution)/shard_map/ppermute | solution.py:41
  19.4 5.3 %collective-permute-start.1 = (bf16[128,896]{1,0:T(8,128)(2,1)S(1)}, bf16[128,896]{1,0:T(8,128)(2,1)S(1)}, u32[]{:S(2)}, u32[]{:S(2)}) collective-permute-start(bf16[128,896]{1,0:T(8,128)(2,1)S(1)} %bitcast.67), channel_id=1, source_target_pairs={{64,0},{128,64},{192,128},{256,192},{320,256},{384,320},{448,384},... | collective-permute-start | bytes 688136 | tf_op jit(solution)/shard_map/ppermute | solution.py:41
  24.7 1.5 %shard_map.140 = (bf16[128,128]{1,0:T(8,128)(2,1)S(1)}, bf16[128,128]{1,0:T(8,128)(2,1)S(1)}, bf16[128,128]{1,0:T(8,128)(2,1)S(1)}, f32[128,1]{1,0:T(8,128)S(1)}) custom-call(s32[2]{0:T(128)S(1)} %pad_add_fusion.s, s32[2,8,128]{2,1,0:T(8,128)} %bitcast.58, s32[2,8,128]{2,1,0:T(8,128)} %bitcast.60, s32[2,8,128]{2,1,0:T(8,128)} %bitcast.62, s32[2,8,128]{2,1,0:T(8,128)} %bitcast.64), custom_call_target="tpu_custom_call" | custom-call | tf_op jit(solution)/shard_map/pallas_call | solution.py:331
  26.2 2.5 %collective-permute-done.fwd = bf16[128,896]{1,0:T(8,128)(2,1)S(1)} collective-permute-done((bf16[128,896]{1,0:T(8,128)(2,1)S(1)}, bf16[128,896]{1,0:T(8,128)(2,1)S(1)}, u32[]{:S(2)}, u32[]{:S(2)}) %collective-permute-start) | collective-permute-done | bytes 229408 | tf_op jit(solution)/shard_map/ppermute | solution.py:41
  28.7 0.9 collective-permute-done.1.cot
  29.6 1.7 %shard_map.141 = (bf16[128,896]{1,0:T(8,128)(2,1)}, bf16[2,128,896]{2,1,0:T(8,128)(2,1)}) custom-call(s32[2]{0:T(128)S(1)} %pad_add_fusion.s, bf16[128,128]{1,0:T(8,128)(2,1)S(1)} %get-tuple-element.15.sel_f, bf16[128,128]{1,0:T(8,128)(2,1)S(1)} %get-tuple-element.16.sel_s, bf16[128,128]{1,0:T(8,128)(2,1)S(1)} %get-tuple-element.17.sel_c, ...), custom_call_target="tpu_custom_call" | custom-call | tf_op jit(solution)/shard_map/pallas_call | solution.py:340
  31.3 3.1 %collective-permute-start.4 = (bf16[2,128,896]{2,1,0:T(8,128)(2,1)}, bf16[2,128,896]{2,1,0:T(8,128)(2,1)S(1)}, u32[]{:S(2)}, u32[]{:S(2)}) collective-permute-start(bf16[2,128,896]{2,1,0:T(8,128)(2,1)} %get-tuple-element.20), channel_id=1, source_target_pairs={{0,2},{2,0},{1,3},{3,1},{4,6},{6,4},{5,7},{7,5},{8,10},{10,8},{9,1... | collective-permute-start | bytes 1376264 | tf_op jit(solution)/shard_map/ppermute | solution.py:45
  34.4 2.2 %collective-permute-start.5 = (bf16[128,896]{1,0:T(8,128)(2,1)S(1)}, bf16[128,896]{1,0:T(8,128)(2,1)S(1)}, u32[]{:S(2)}, u32[]{:S(2)}) collective-permute-start(bf16[128,896]{1,0:T(8,128)(2,1)S(1)} %bitcast.34), channel_id=1, source_target_pairs={{0,2},{2,0},{1,3},{3,1},{4,6},{6,4},{5,7},{7,5},{8,10},{10,8},{9,1... | collective-permute-start | bytes 688136 | tf_op jit(solution)/shard_map/ppermute | solution.py:45
  36.6 6.8 %all-to-all-start = ((bf16[8,16,896]{2,1,0:T(8,128)(2,1)}), bf16[8,16,896]{2,1,0:T(8,128)(2,1)S(1)}, u32[]{:S(2)}, u32[]{:S(2)}) async-start(bf16[8,16,896]{2,1,0:T(8,128)(2,1)} %bitcast.57), calls=%async_computation | async-start | bytes 458752 | tf_op jit(solution)/shard_map/all_to_all | solution.py:344
  43.4 6.1 %collective-permute-done.5.far_s = bf16[128,896]{1,0:T(8,128)(2,1)S(1)} collective-permute-done((bf16[128,896]{1,0:T(8,128)(2,1)S(1)}, bf16[128,896]{1,0:T(8,128)(2,1)S(1)}, u32[]{:S(2)}, u32[]{:S(2)}) %collective-permute-start.5) | collective-permute-done | bytes 229408 | tf_op jit(solution)/shard_map/ppermute | solution.py:45
  49.5 0.0 collective-permute-done.4.far
  49.5 0.0 collective-permute-done.2.box.gate_o.up_o.down_o
  49.5 4.3 %shard_map.147.mine = f32[640,512]{1,0:T(8,128)S(1)} custom-call(s32[2]{0:T(128)S(1)} %pad_add_fusion.s, bf16[128,896]{1,0:T(8,128)(2,1)S(1)} %collective-permute-done.fwd, bf16[128,896]{1,0:T(8,128)(2,1)S(1)} %bitcast.35, bf16[128,896]{1,0:T(8,128)(2,1)S(1)} %collective-permute-done.1.cot, bf16[2,128,896]{2,1,0:T(8,128)(2,1)S(1)} %collective-permute-done.4.far, ...), custom_call_target="tpu_custom_call" | custom-call | tf_op jit(solution)/shard_map/pallas_call | solution.py:375
  53.8 3.6 %collective-permute-start.6 = (f32[640,512]{1,0:T(8,128)S(1)}, f32[640,512]{1,0:T(8,128)S(1)}, u32[]{:S(2)}, u32[]{:S(2)}) collective-permute-start(f32[640,512]{1,0:T(8,128)S(1)} %shard_map.147.mine), channel_id=1, source_target_pairs={{0,1},{1,0},{2,3},{3,2},{4,5},{5,4},{6,7},{7,6},{8,9},{9,8},{10,11... | collective-permute-start | bytes 3932168 | tf_op jit(solution)/shard_map/ppermute | solution.py:45
  57.5 0.0 all-to-all-done
  57.5 1.6 %shard_map.142 = bf16[4,96,896]{2,1,0:T(8,128)(2,1)} custom-call(s32[2]{0:T(128)S(1)} %pad_add_fusion.s, bf16[128,896]{1,0:T(8,128)(2,1)S(1)} %bitcast.32), custom_call_target="tpu_custom_call" | custom-call | tf_op jit(solution)/shard_map/pallas_call | solution.py:346
  59.1 14.8 %all_to_all.20 = bf16[4,96,896]{2,1,0:T(8,128)(2,1)S(1)} all-to-all(bf16[4,96,896]{2,1,0:T(8,128)(2,1)} %shard_map.142), channel_id=1, replica_groups=mesh['pipe'=12,'y'=8,'xh'=2,'xl'=2,'core'=2] {'xh','xl'}, dimensions={0} | all-to-all | bytes 1376256 | tf_op jit(solution)/shard_map/all_to_all | solution.py:350
  73.9 3.3 %shard_map.144.mine = f32[320,256]{1,0:T(8,128)S(1)} custom-call(s32[2]{0:T(128)S(1)} %pad_add_fusion.s, bf16[2,2,96,896]{3,2,1,0:T(8,128)(2,1)S(1)} %bitcast.31, bf16[4,896,128]{2,1,0:T(8,128)(2,1)} %bitcast.47, bf16[4,896,128]{2,1,0:T(8,128)(2,1)} %bitcast.50, bf16[128,3584]{1,0:T(8,128)(2,1)} %bitcast.53, ...), custom_call_target="tpu_custom_call" | custom-call | tf_op jit(solution)/shard_map/pallas_call | solution.py:384
  77.2 3.3 %collective-permute-start.3 = (f32[320,256]{1,0:T(8,128)S(1)}, f32[320,256]{1,0:T(8,128)S(1)}, u32[]{:S(2)}, u32[]{:S(2)}) collective-permute-start(f32[320,256]{1,0:T(8,128)S(1)} %shard_map.144.mine), channel_id=1, source_target_pairs={{0,1},{1,0},{2,3},{3,2},{4,5},{5,4},{6,7},{7,6},{8,9},{9,8},{10,11... | collective-permute-start | bytes 983048 | tf_op jit(solution)/shard_map/ppermute | solution.py:45
  80.5 1.2 %collective-permute-done.3.other = f32[320,256]{1,0:T(8,128)S(1)} collective-permute-done((f32[320,256]{1,0:T(8,128)S(1)}, f32[320,256]{1,0:T(8,128)S(1)}, u32[]{:S(2)}, u32[]{:S(2)}) %collective-permute-start.3) | collective-permute-done | bytes 327712 | tf_op jit(solution)/shard_map/ppermute | solution.py:45
  81.8 4.2 %shard_map.145 = bf16[2,2,64,896]{3,2,1,0:T(8,128)(2,1)} custom-call(s32[2]{0:T(128)S(1)} %pad_add_fusion.s, f32[320,256]{1,0:T(8,128)S(1)} %shard_map.144.mine, f32[320,256]{1,0:T(8,128)S(1)} %collective-permute-done.3.other, bf16[4,896,128]{2,1,0:T(8,128)(2,1)} %bitcast.48, bf16[4,896,128]{2,1,0:T(8,128)(2,1)} %bitcast.51, bf16[128,3584]{1,0:T(8,128)(2,1)} %bitcast.54, ...), custom_call_target="tpu_custom_call" | custom-call | tf_op jit(solution)/shard_map/pallas_call | solution.py:391
  85.9 3.5 %all-to-all-start.2 = ((bf16[4,64,896]{2,1,0:T(8,128)(2,1)}), bf16[4,64,896]{2,1,0:T(8,128)(2,1)S(1)}, u32[]{:S(2)}, u32[]{:S(2)}) async-start(bf16[4,64,896]{2,1,0:T(8,128)(2,1)} %bitcast.55), calls=%async_computation.2 | async-start | bytes 917504 | tf_op jit(solution)/shard_map/all_to_all | solution.py:397
  89.4 5.5 %shard_map.148 = (bf16[2,128,896]{2,1,0:T(8,128)(2,1)}, f32[2,128,896]{2,1,0:T(8,128)}) custom-call(s32[2]{0:T(128)S(1)} %pad_add_fusion.s, f32[640,512]{1,0:T(8,128)S(1)} %shard_map.147.mine, f32[640,512]{1,0:T(8,128)S(1)} %collective-permute-done.6.other, bf16[4,896,256]{2,1,0:T(8,128)(2,1)} %bitcast.39, bf16[4,896,256]{2,1,0:T(8,128)(2,1)} %bitcast.42, ...), custom_call_target="tpu_custom_call" | custom-call | tf_op jit(solution)/shard_map/pallas_call | solution.py:404
  94.9 3.3 %collective-permute-start.7 = (bf16[2,128,896]{2,1,0:T(8,128)(2,1)}, bf16[2,128,896]{2,1,0:T(8,128)(2,1)S(1)}, u32[]{:S(2)}, u32[]{:S(2)}) collective-permute-start(bf16[2,128,896]{2,1,0:T(8,128)(2,1)} %get-tuple-element.22), channel_id=1, source_target_pairs={{0,2},{2,0},{1,3},{3,1},{4,6},{6,4},{5,7},{7,5},{8,10},{10,8},{9,1... | collective-permute-start | bytes 1376264 | tf_op jit(solution)/shard_map/ppermute | solution.py:45
  98.2 1.2 %shard_map.146 = bf16[64,896]{1,0:T(8,128)(2,1)} custom-call(s32[2]{0:T(128)S(1)} %pad_add_fusion.s, bf16[4,64,896]{2,1,0:T(8,128)(2,1)S(1)} %all-to-all-done.2.parts), custom_call_target="tpu_custom_call" | custom-call | tf_op jit(solution)/shard_map/pallas_call | solution.py:398
  99.5 6.8 %all-to-all-start.3 = ((bf16[8,8,896]{2,1,0:T(8,128)(2,1)}), bf16[8,8,896]{2,1,0:T(8,128)(2,1)S(1)}, u32[]{:S(2)}, u32[]{:S(2)}) async-start(bf16[8,8,896]{2,1,0:T(8,128)(2,1)} %bitcast.56), calls=%async_computation.3 | async-start | bytes 229376 | tf_op jit(solution)/shard_map/all_to_all | solution.py:402
  106.3 1.5 %shard_map.149 = (bf16[128,64]{1,0:T(8,128)(2,1)S(1)}, bf16[128,64]{1,0:T(8,128)(2,1)S(1)}, bf16[128,64]{1,0:T(8,128)(2,1)S(1)}) custom-call(s32[2]{0:T(128)S(1)} %pad_add_fusion.s, s32[2,8,128]{2,1,0:T(8,128)} %bitcast.59, s32[2,8,128]{2,1,0:T(8,128)} %bitcast.61, s32[2,8,128]{2,1,0:T(8,128)} %bitcast.63, s32[2,8,128]{2,1,0:T(8,128)} %bitcast.65), custom_call_target="tpu_custom_call" | custom-call | tf_op jit(solution)/shard_map/pallas_call | solution.py:335
  107.8 6.4 %all-to-all-done.3 = bf16[8,8,896]{2,1,0:T(8,128)(2,1)S(1)} async-done(((bf16[8,8,896]{2,1,0:T(8,128)(2,1)}), bf16[8,8,896]{2,1,0:T(8,128)(2,1)S(1)}, u32[]{:S(2)}, u32[]{:S(2)}) %all-to-all-start.3) | async-done | bytes 114720 | tf_op jit(solution)/shard_map/all_to_all | solution.py:402
  114.2 2.8 %shard_map.150 = (bf16[128,896]{1,0:T(8,128)(2,1)}, bf16[128,896]{1,0:T(8,128)(2,1)}) custom-call(s32[2]{0:T(128)S(1)} %pad_add_fusion.s, bf16[64,896]{1,0:T(8,128)(2,1)S(1)} %bitcast.36, f32[2,128,896]{2,1,0:T(8,128)} %get-tuple-element.21.keep, bf16[2,128,896]{2,1,0:T(8,128)(2,1)S(1)} %collective-permute-done.7.far, ...), custom_call_target="tpu_custom_call" | custom-call | tf_op jit(solution)/shard_map/pallas_call | solution.py:413
  (9 shorter events, 0.0 us)
Async XLA Ops:
  0.7 16.7 %copy-start.1 = (bf16[1,128,896]{2,1,0:T(8,128)(2,1)S(1)}, bf16[1,128,896]{2,1,0:T(8,128)(2,1)}, u32[]{:S(2)}) copy-start(bf16[1,128,896]{2,1,0:T(8,128)(2,1)} %param.13) | copy-start | bytes 688132
  0.7 18.6 %copy-start.2 = (bf16[1,128,896]{2,1,0:T(8,128)(2,1)S(1)}, bf16[1,128,896]{2,1,0:T(8,128)(2,1)}, u32[]{:S(2)}) copy-start(bf16[1,128,896]{2,1,0:T(8,128)(2,1)} %param.14) | copy-start | bytes 688132
  0.7 28.9 %copy-start = (bf16[1,128,896]{2,1,0:T(8,128)(2,1)S(1)}, bf16[1,128,896]{2,1,0:T(8,128)(2,1)}, u32[]{:S(2)}) copy-start(bf16[1,128,896]{2,1,0:T(8,128)(2,1)} %param.15) | copy-start | bytes 688132
  5.0 44.5 %collective-permute-start.2 = (bf16[2,1280,896]{2,1,0:T(8,128)(2,1)}, bf16[2,1280,896]{2,1,0:T(8,128)(2,1)}, u32[]{:S(2)}, u32[]{:S(2)}) collective-permute-start(bf16[2,1280,896]{2,1,0:T(8,128)(2,1)} %shard_map.143), channel_id=1, source_target_pairs={{0,1},{1,0},{2,3},{3,2},{4,5},{5,4},{6,7},{7,6},{8,9},{9,8},{10,11... | collective-permute-start | bytes 13762568 | tf_op jit(solution)/shard_map/ppermute | solution.py:45
  17.4 11.3 %collective-permute-start = (bf16[128,896]{1,0:T(8,128)(2,1)S(1)}, bf16[128,896]{1,0:T(8,128)(2,1)S(1)}, u32[]{:S(2)}, u32[]{:S(2)}) collective-permute-start(bf16[128,896]{1,0:T(8,128)(2,1)S(1)} %bitcast.66), channel_id=1, source_target_pairs={{704,0},{0,64},{64,128},{128,192},{192,256},{256,320},{320,384},{3... | collective-permute-start | bytes 688136 | tf_op jit(solution)/shard_map/ppermute | solution.py:41
  19.4 10.3 %collective-permute-start.1 = (bf16[128,896]{1,0:T(8,128)(2,1)S(1)}, bf16[128,896]{1,0:T(8,128)(2,1)S(1)}, u32[]{:S(2)}, u32[]{:S(2)}) collective-permute-start(bf16[128,896]{1,0:T(8,128)(2,1)S(1)} %bitcast.67), channel_id=1, source_target_pairs={{64,0},{128,64},{192,128},{256,192},{320,256},{384,320},{448,384},... | collective-permute-start | bytes 688136 | tf_op jit(solution)/shard_map/ppermute | solution.py:41
  31.3 18.2 %collective-permute-start.4 = (bf16[2,128,896]{2,1,0:T(8,128)(2,1)}, bf16[2,128,896]{2,1,0:T(8,128)(2,1)S(1)}, u32[]{:S(2)}, u32[]{:S(2)}) collective-permute-start(bf16[2,128,896]{2,1,0:T(8,128)(2,1)} %get-tuple-element.20), channel_id=1, source_target_pairs={{0,2},{2,0},{1,3},{3,1},{4,6},{6,4},{5,7},{7,5},{8,10},{10,8},{9,1... | collective-permute-start | bytes 1376264 | tf_op jit(solution)/shard_map/ppermute | solution.py:45
  34.4 15.1 %collective-permute-start.5 = (bf16[128,896]{1,0:T(8,128)(2,1)S(1)}, bf16[128,896]{1,0:T(8,128)(2,1)S(1)}, u32[]{:S(2)}, u32[]{:S(2)}) collective-permute-start(bf16[128,896]{1,0:T(8,128)(2,1)S(1)} %bitcast.34), channel_id=1, source_target_pairs={{0,2},{2,0},{1,3},{3,1},{4,6},{6,4},{5,7},{7,5},{8,10},{10,8},{9,1... | collective-permute-start | bytes 688136 | tf_op jit(solution)/shard_map/ppermute | solution.py:45
  36.6 20.9 %all-to-all-start = ((bf16[8,16,896]{2,1,0:T(8,128)(2,1)}), bf16[8,16,896]{2,1,0:T(8,128)(2,1)S(1)}, u32[]{:S(2)}, u32[]{:S(2)}) async-start(bf16[8,16,896]{2,1,0:T(8,128)(2,1)} %bitcast.57), calls=%async_computation | async-start | bytes 458752 | tf_op jit(solution)/shard_map/all_to_all | solution.py:344
  53.8 35.6 %collective-permute-start.6 = (f32[640,512]{1,0:T(8,128)S(1)}, f32[640,512]{1,0:T(8,128)S(1)}, u32[]{:S(2)}, u32[]{:S(2)}) collective-permute-start(f32[640,512]{1,0:T(8,128)S(1)} %shard_map.147.mine), channel_id=1, source_target_pairs={{0,1},{1,0},{2,3},{3,2},{4,5},{5,4},{6,7},{7,6},{8,9},{9,8},{10,11... | collective-permute-start | bytes 3932168 | tf_op jit(solution)/shard_map/ppermute | solution.py:45
  77.2 4.6 %collective-permute-start.3 = (f32[320,256]{1,0:T(8,128)S(1)}, f32[320,256]{1,0:T(8,128)S(1)}, u32[]{:S(2)}, u32[]{:S(2)}) collective-permute-start(f32[320,256]{1,0:T(8,128)S(1)} %shard_map.144.mine), channel_id=1, source_target_pairs={{0,1},{1,0},{2,3},{3,2},{4,5},{5,4},{6,7},{7,6},{8,9},{9,8},{10,11... | collective-permute-start | bytes 983048 | tf_op jit(solution)/shard_map/ppermute | solution.py:45
  85.9 12.3 %all-to-all-start.2 = ((bf16[4,64,896]{2,1,0:T(8,128)(2,1)}), bf16[4,64,896]{2,1,0:T(8,128)(2,1)S(1)}, u32[]{:S(2)}, u32[]{:S(2)}) async-start(bf16[4,64,896]{2,1,0:T(8,128)(2,1)} %bitcast.55), calls=%async_computation.2 | async-start | bytes 917504 | tf_op jit(solution)/shard_map/all_to_all | solution.py:397
  94.9 19.3 %collective-permute-start.7 = (bf16[2,128,896]{2,1,0:T(8,128)(2,1)}, bf16[2,128,896]{2,1,0:T(8,128)(2,1)S(1)}, u32[]{:S(2)}, u32[]{:S(2)}) collective-permute-start(bf16[2,128,896]{2,1,0:T(8,128)(2,1)} %get-tuple-element.22), channel_id=1, source_target_pairs={{0,2},{2,0},{1,3},{3,1},{4,6},{6,4},{5,7},{7,5},{8,10},{10,8},{9,1... | collective-permute-start | bytes 1376264 | tf_op jit(solution)/shard_map/ppermute | solution.py:45
  99.5 14.7 %all-to-all-start.3 = ((bf16[8,8,896]{2,1,0:T(8,128)(2,1)}), bf16[8,8,896]{2,1,0:T(8,128)(2,1)S(1)}, u32[]{:S(2)}, u32[]{:S(2)}) async-start(bf16[8,8,896]{2,1,0:T(8,128)(2,1)} %bitcast.56), calls=%async_computation.3 | async-start | bytes 229376 | tf_op jit(solution)/shard_map/all_to_all | solution.py:402

commit v4 on v3

--- a/solution.py
+++ b/solution.py
@@ -13,12 +13,12 @@
 PAD = 4 * CAP
 
 
-def call(body, outs, grid=(1,), in_specs=None, out_specs=None, scratch=(), flops=0):
+def call(body, outs, grid=(1,), in_specs=None, out_specs=None, scratch=(), flops=0, aliases={}):
     spec = pltpu.PrefetchScalarGridSpec(
         num_scalar_prefetch=1, grid=grid, in_specs=in_specs, out_specs=out_specs, scratch_shapes=scratch
     )
     return pl.pallas_call(
-        body, grid_spec=spec, out_shape=outs,
+        body, grid_spec=spec, out_shape=outs, input_output_aliases=aliases,
         cost_estimate=pl.CostEstimate(flops=flops, transcendentals=0, bytes_accessed=0),
         compiler_params=pltpu.CompilerParams(vmem_limit_bytes=20 * 2**20),
     )
@@ -53,7 +53,7 @@
     return lax.dot_general(left, right, (((1,), (1,)), ((), ())), preferred_element_type=F32)
 
 
-def tables_body(s, ids, keep, slot, wq, sel_f, sel_s, sel_c, scale):
+def make_tables(ids, keep, slot, wq, sel, scale):
     tokens = ids.shape[2]
     row = lax.broadcasted_iota(I32, (tokens, 1), 0)
     arr = (row // CAP) % 4
@@ -70,10 +70,10 @@
         eq = target[1, k : k + 1] == want_b
         hit_b += jnp.where(eq, 1.0, 0.0)
         weight += jnp.where(eq, level[k : k + 1], 0.0)
-    sel_f[...] = hit_f.astype(BF)
-    sel_s[...] = jnp.where(arr == 1, hit_b, 0.0).astype(BF)
-    sel_c[...] = jnp.where(arr == 2, hit_b, 0.0).astype(BF)
-    scale[...] = jnp.sum(weight, axis=1, keepdims=True)
+    sel[0] = hit_f.astype(BF)
+    sel[1] = jnp.where(arr == 1, hit_b, 0.0).astype(BF)
+    sel[2] = jnp.where(arr == 2, hit_b, 0.0).astype(BF)
+    scale[...] = jnp.broadcast_to(jnp.sum(weight, axis=1, keepdims=True), scale.shape)
 
 
 def adders_body(s, ids, keep, slot, wq, add_hi, add_lo, add_b):
@@ -102,8 +102,8 @@
     add_b[...] = one.T.astype(BF)
 
 
-def parcel_body(s, sel_f, sel_s, sel_c, scale, fwd, saved, cot, out, pair):
-    rows = dot(sel_f[...], fwd[...]) + dot(sel_s[...], saved[...]) + scale[...] * dot(sel_c[...], cot[...])
+def parcel_body(s, sel, scale, fwd, saved, cot, out, pair):
+    rows = dot(sel[0], fwd[...]) + dot(sel[1], saved[...]) + scale[:, 0:1] * dot(sel[2], cot[...])
     out[...] = rows.astype(BF)
     pair[0] = fwd[...]
     pair[1] = cot[...]
@@ -134,10 +134,11 @@
     return wait
 
 
-def pack_body(s, gs, us, gr, ur, ds, dr, box, hold, sems):
+def prep(gs, us, gr, ur, ds, dr, plan, box, sel, scale, hold, ints, sel_v, scale_v, sems, s):
     w = gs.shape[2]
     n = gr.shape[2]
     f = gs.shape[1]
+    ready = run([(v, ints.at[i]) for i, v in enumerate(plan)], sems.at[14:18])
     wait = []
     for x in range(2):
         t = 2 * x + 1 - s[1]
@@ -150,13 +151,28 @@
             (ur.at[t], h.at[0:f, 2 * w + n : 2 * w + 2 * n]),
             (dr.at[:, cols], h.at[f : f + n]),
             (ds.at[:, cols], h.at[f + n :]),
-        ], sems.at[7 * x :]))
-    done = []
+        ], sems.at[7 * x : 7 * x + 6]))
+    ready(0, 4)
+    make_tables(*[ints.at[i] for i in range(4)], sel_v, scale_v)
+    done = [run([(sel_v, sel), (scale_v, scale)], sems.at[18:20])]
     for x in range(2):
         wait[x](0, 6)
-        done.append(run([(hold.at[x], box.at[x])], sems.at[7 * x + 6 :]))
-    for x in range(2):
-        done[x](0, 1)
+        done.append(run([(hold.at[x], box.at[x])], sems.at[7 * x + 6 : 7 * x + 7]))
+    done[0](0, 2)
+    done[1](0, 1)
+    done[2](0, 1)
+
+
+def prep_first_body(s, *refs):
+    @pl.when(s[2] == 0)
+    def _():
+        prep(*refs[:6], refs[6:10], *refs[10:], s)
+
+
+def prep_rest_body(s, *refs):
+    @pl.when(s[2] != 0)
+    def _():
+        prep(*refs[:6], refs[6:10], *refs[13:], s)
 
 
 def weight_copies(s, order, gate, up, down, box, lane, row, g, u, d):
@@ -198,38 +214,33 @@
     pre(wait, len(xs), x.at[0 : 2 * n], x.at[2 * n :], g, u, d, acc)
 
 
-def shared_post_body(s, mine, other, gate, up, down, gate_o, up_o, down_o, send, keep, hid, gg, gu):
-    j = pl.program_id(0)
-    n = hid.shape[0]
+def shared_back(hid, gg, gu, gate, up, down, gate_o, up_o, down_o):
     w = gate.shape[2]
-
-    @pl.when(j == 0)
-    def _():
-        a_f = joined(mine[0:n], other[0:n])
-        a_s = joined(mine[n : 2 * n], other[n : 2 * n])
-        b_f = joined(mine[2 * n : 3 * n], other[2 * n : 3 * n])
-        b_s = joined(mine[3 * n : 4 * n], other[3 * n : 4 * n])
-        dh = joined(mine[4 * n : 5 * n], other[4 * n : 5 * n])
-        hid[...] = (a_f * jax.nn.sigmoid(a_f) * b_f).astype(BF)
-        sg = jax.nn.sigmoid(a_s)
-        gg[...] = (dh * b_s * (sg * (1.0 + a_s * (1.0 - sg)))).astype(BF)
-        gu[...] = (dh * (a_s * sg)).astype(BF)
-
     out = dot(hid[:, :w], down[...]) + dot(hid[:, w:], down_o[0])
     grad = (
         contract_last(gg[:, :w], gate[0]) + contract_last(gg[:, w:], gate_o[0])
         + contract_last(gu[:, :w], up[0]) + contract_last(gu[:, w:], up_o[0])
     )
-
-    @pl.when(j == 0)
-    def _():
-        send[0] = out.astype(BF)
-        send[1] = grad.astype(BF)
-
-    @pl.when(j == 1)
-    def _():
-        keep[0] = out
-        keep[1] = grad
+    return out, grad
+
+
+def shared_send_body(s, mine, other, gate, up, down, gate_o, up_o, down_o, send, hid_out, gg_out, gu_out):
+    n = send.shape[1]
+    a_f, a_s, b_f, b_s, dh = [joined(mine[i * n : i * n + n], other[i * n : i * n + n]) for i in range(5)]
+    hid = (a_f * jax.nn.sigmoid(a_f) * b_f).astype(BF)
+    sg = jax.nn.sigmoid(a_s)
+    gg = (dh * b_s * (sg * (1.0 + a_s * (1.0 - sg)))).astype(BF)
+    gu = (dh * (a_s * sg)).astype(BF)
+    hid_out[...] = hid
+    gg_out[...] = gg
+    gu_out[...] = gu
+    out, grad = shared_back(hid, gg, gu, gate, up, down, gate_o, up_o, down_o)
+    send[0] = out.astype(BF)
+    send[1] = grad.astype(BF)
+
+
+def shared_keep_body(s, hid, gg, gu, gate, up, down, gate_o, up_o, down_o, keep):
+    keep[0], keep[1] = shared_back(hid[...], gg[...], gu[...], gate, up, down, gate_o, up_o, down_o)
 
 
 def expert_pre_body(s, got, gate, up, down, box, acc, both, cot, g, u, d, sems):
@@ -292,7 +303,7 @@
           gate_routed, up_routed, down_routed, gate_shared, up_shared, down_shared):
     tokens, shard = inputs_prev.shape[1:]
     experts = lax.axis_size("y")
-    here = jnp.stack([lax.axis_index("xl"), lax.axis_index("core")]).astype(I32)
+    here = jnp.stack([lax.axis_index("xl"), lax.axis_index("core"), lax.axis_index("pipe")]).astype(I32)
     saved = saved_input[0]
     gs = gate_shared[0].reshape(4, shard, -1)
     us = up_shared[0].reshape(4, shard, -1)
@@ -315,23 +326,25 @@
         return pl.BlockSpec((n, shard), lambda j, s: (0, which(j, s)))
 
     height = shard + fe + fs
-    box = call(
-        pack_body, pltpu.HBM((2, height, shard), BF), in_specs=[hbm] * 6, out_specs=hbm,
-        scratch=[pltpu.VMEM((2, height, shard), BF), pltpu.SemaphoreType.DMA((14,))],
-    )(here, gs, us, gr, ur, ds, dr)
-    box = swapped(box, "core")
 
     def turned(v):
         return pltpu.with_memory_space_constraint(v[:, 0].transpose(0, 2, 1), pltpu.HBM)
 
-    sq = shape_of(BF, tokens, tokens)
+    plan = [turned(v) for v in (expert_ids, keep_mask, slot_pos, weight_q)]
+    sq = (tokens, tokens)
     tall = shape_of(BF, tokens, 8 * experts)
     tab = whole((2, expert_ids.shape[3], tokens))
-    plan = [turned(v) for v in (expert_ids, keep_mask, slot_pos, weight_q)]
-    sel_f, sel_s, sel_c, scale = call(
-        tables_body, (sq, sq, sq, shape_of(F32, tokens, 1)),
-        in_specs=[tab] * 4, out_specs=(whole(sq.shape),) * 3 + (whole((tokens, 1)),),
-    )(here, *plan)
+    made = (pltpu.HBM((2, height, shard), BF), pltpu.HBM((3, *sq), BF), pltpu.HBM(sq, F32))
+    room = [pltpu.VMEM((2, height, shard), BF), pltpu.VMEM((4, 2, expert_ids.shape[3], tokens), I32),
+            pltpu.VMEM((3, *sq), BF), pltpu.VMEM(sq, F32), pltpu.SemaphoreType.DMA((20,))]
+    given = (gs, us, gr, ur, ds, dr, *plan)
+    first = call(prep_first_body, made, in_specs=[hbm] * 10, out_specs=(hbm,) * 3, scratch=room)(here, *given)
+    box, sel, scale = call(
+        prep_rest_body, made, in_specs=[hbm] * 13, out_specs=(hbm,) * 3, scratch=room,
+        aliases={11: 0, 12: 1, 13: 2},
+    )(here, *given, *first)
+    box = swapped(box, "core")
+
     add_hi, add_lo, add_b = call(
         adders_body, (tall, tall, tall), in_specs=[tab] * 4, out_specs=(whole(tall.shape),) * 3,
     )(here, *plan)
@@ -339,8 +352,8 @@
     act = whole((tokens, shard))
     parcel, pair = call(
         parcel_body, (pltpu.HBM((tokens, shard), BF), pltpu.HBM((2, tokens, shard), BF)),
-        in_specs=[whole(sq.shape)] * 3 + [whole((tokens, 1))] + [act] * 3, out_specs=(act, whole((2, tokens, shard))),
-    )(here, sel_f, sel_s, sel_c, scale, fwd, saved, cot)
+        in_specs=[whole((3, *sq)), whole(sq)] + [act] * 3, out_specs=(act, whole((2, tokens, shard))),
+    )(here, sel, scale, fwd, saved, cot)
     parcel = lax.all_to_all(parcel.reshape(experts, PAD, shard), "y", 0, 0, tiled=True)
     rows = experts * 3 * CAP
     fan = call(
@@ -361,7 +374,6 @@
                 pl.BlockSpec((1, shard, w), lambda j, s: (at(j, s), 0, lane + 1)),
                 pl.BlockSpec((1, w, shard), lambda j, s: (at(j, s), row, 0))]
 
-    far_first = lambda j, s: (s[0] + 1 + j) % 2
     straight = lambda j, s: j
 
     def sems(n):
@@ -401,15 +413,21 @@
     )(here, ret)
     ret = lax.all_to_all(ret.reshape(experts, 2 * CAP, shard), "y", 0, 0, tiled=True)
 
-    send, keep = call(
-        shared_post_body, (pltpu.HBM((2, tokens, shard), BF), pltpu.HBM((2, tokens, shard), F32)), grid=(2,),
-        in_specs=[whole(z_shape)] * 2 + weight_specs(fs, 0, (shard + fe) // fs, far_first),
-        out_specs=(whole((2, tokens, shard)),) * 2,
-        scratch=[pltpu.VMEM((tokens, 2 * fs), BF)] * 3,
+    hid_shape = (tokens, 2 * fs)
+    row0 = (shard + fe) // fs
+    send, *hidden = call(
+        shared_send_body, (pltpu.HBM((2, tokens, shard), BF),) + (pltpu.HBM(hid_shape, BF),) * 3,
+        in_specs=[whole(z_shape)] * 2 + weight_specs(fs, 0, row0, lambda j, s: 1 - s[0]),
+        out_specs=(whole((2, tokens, shard)),) + (whole(hid_shape),) * 3,
     )(here, z_s, z_s2, *shared_w2)
+    hidden = [pltpu.with_memory_space_constraint(h, pltpu.HBM) for h in hidden]
+    keep = call(
+        shared_keep_body, shape_of(F32, 2, tokens, shard),
+        in_specs=[whole(hid_shape)] * 3 + weight_specs(fs, 0, row0, lambda j, s: s[0]),
+        out_specs=whole((2, tokens, shard)),
+    )(here, *hidden, *shared_w2)
     far = swapped(send, "xl")
 
-    keep = pltpu.with_memory_space_constraint(keep, pltpu.HBM)
     out, grad = call(
         merge_body, (shape_of(BF, tokens, shard),) * 2,
         in_specs=[whole((8 * experts, shard)), whole(keep.shape), whole(far.shape)] + [whole(tall.shape)] * 3,

time: 118 us -> 119 us (level)
  local copies, waits for them, and re-layouts: 0.01 us -> 1.75 us
    all_to_all x1, waiting for transfers between devices: 6.38 us -> 3.03 us  [local(): lax.all_to_all(ret.reshape(experts, 2 * CAP, shard), 'y', 0, 0, tiled=True)]
    unnamed x6 -> x10, local copies, waits for them, and re-layouts: 0.01 us -> 1.75 us
    ppermute x2, waiting for transfers between devices: 3.41 us -> 4.92 us  [shifted(): lax.ppermute(block, axis, [((i - distance) % n, i) for i in range(n)])]
    all_to_all x1, waiting for transfers between devices: 0.01 us -> 1.24 us  [local(): lax.all_to_all(ret.reshape(4, n_e // 2, shard), ('xh', 'xl'), 0, 0, tiled...]
    pallas_call x3 -> x4, Pallas kernels: 11.3 us -> 12.4 us  [the longest x1 4.5 us: local(): call(prep_first_body, made, in_specs=[hbm] * 10, out_specs=(hbm,) * 3, sc...]
  transfers between devices with their start and end apart: 11 -> 11, of which waited for: 5 -> 6; matrix products, arithmetic and copies ran while one was open for 0% -> 0% of each run, Pallas kernels for 21% -> 21%
where the time goes in v4:
time: 119 us; the launch traced here: 118 us
  starting transfers between devices  52.3 us (44%)
  Pallas kernels  31.8 us (27%)
  waiting for transfers between devices  16.5 us (14%)
  blocking collectives  14.8 us (12%)
  local copies, waits for them, and re-layouts  1.75 us (1%)
    ppermute x6, starting transfers between devices, swapped(): return lax.ppermute(block, axis, [(0, 1), (1, 0)])  27.9 us
    all_to_all x1, blocking collectives, local(): lax.all_to_all(fan, ('xh', 'xl'), 0, 0, tiled=True)  14.8 us
    ppermute x6, waiting for transfers between devices, swapped(): return lax.ppermute(block, axis, [(0, 1), (1, 0)])  7.33 us
    ppermute x2, starting transfers between devices, shifted(): lax.ppermute(block, axis, [((i - distance) % n, i) for i in range(n)])  7.24 us
    all_to_all x1, starting transfers between devices, local(): lax.all_to_all(parcel.reshape(experts, PAD, shard), 'y', 0, 0, tiled=True)  6.83 us
    all_to_all x1, starting transfers between devices, local(): lax.all_to_all(ret.reshape(experts, 2 * CAP, shard), 'y', 0, 0, tiled=True)  6.82 us
    ppermute x2, waiting for transfers between devices, shifted(): lax.ppermute(block, axis, [((i - distance) % n, i) for i in range(n)])  4.92 us
    pallas_call x1, Pallas kernels, local(): call(prep_first_body, made, in_specs=[hbm] * 10, out_specs=(hbm,) * 3, sc...  4.5 us
  transfers between devices with their start and end apart: 11, of which 6 were waited for; matrix products, arithmetic and copies ran while one was open for 0% of the time, Pallas kernels for 21%

profile of v4, /device:TPU:1, one launch (start us, length us, event | category | flops | bytes accessed | tf_op | source)
XLA Modules:
  0.0 118.0 jit_solution(1273493301473523884)
XLA Ops:
  0.7 4.5 %shard_map.140 = (bf16[2,1280,896]{2,1,0:T(8,128)(2,1)}, bf16[3,128,128]{2,1,0:T(8,128)(2,1)}, f32[128,128]{1,0:T(8,128)}) custom-call(s32[3]{0:T(128)S(1)} %pad_add_fusion.s, bf16[4,896,256]{2,1,0:T(8,128)(2,1)} %bitcast.38, bf16[4,896,256]{2,1,0:T(8,128)(2,1)} %bitcast.43, bf16[4,896,128]{2,1,0:T(8,128)(2,1)} %bitcast.53, bf16[4,896,128]{2,1,0:T(8,128)(2,1)} %bitcast.57, ...), custom_call_target="tpu_custom_call" | custom-call | tf_op jit(solution)/shard_map/pallas_call | solution.py:341
  5.3 0.7 shard_map.141
  6.0 12.4 %collective-permute-start.2 = (bf16[2,1280,896]{2,1,0:T(8,128)(2,1)}, bf16[2,1280,896]{2,1,0:T(8,128)(2,1)}, u32[]{:S(2)}, u32[]{:S(2)}) collective-permute-start(bf16[2,1280,896]{2,1,0:T(8,128)(2,1)} %get-tuple-element.25), channel_id=1, source_target_pairs={{0,1},{1,0},{2,3},{3,2},{4,5},{5,4},{6,7},{7,6},{8,9},{9,8},{10,11... | collective-permute-start | bytes 13762568 | tf_op jit(solution)/shard_map/ppermute | solution.py:45
  18.4 1.9 %collective-permute-start = (bf16[128,896]{1,0:T(8,128)(2,1)S(1)}, bf16[128,896]{1,0:T(8,128)(2,1)S(1)}, u32[]{:S(2)}, u32[]{:S(2)}) collective-permute-start(bf16[128,896]{1,0:T(8,128)(2,1)S(1)} %bitcast.80), channel_id=1, source_target_pairs={{704,0},{0,64},{64,128},{128,192},{192,256},{256,320},{320,384},{3... | collective-permute-start | bytes 688136 | tf_op jit(solution)/shard_map/ppermute | solution.py:41
  20.3 5.3 %collective-permute-start.1 = (bf16[128,896]{1,0:T(8,128)(2,1)S(1)}, bf16[128,896]{1,0:T(8,128)(2,1)S(1)}, u32[]{:S(2)}, u32[]{:S(2)}) collective-permute-start(bf16[128,896]{1,0:T(8,128)(2,1)S(1)} %bitcast.81), channel_id=1, source_target_pairs={{64,0},{128,64},{192,128},{256,192},{320,256},{384,320},{448,384},... | collective-permute-start | bytes 688136 | tf_op jit(solution)/shard_map/ppermute | solution.py:41
  25.7 4.0 %collective-permute-done.fwd = bf16[128,896]{1,0:T(8,128)(2,1)S(1)} collective-permute-done((bf16[128,896]{1,0:T(8,128)(2,1)S(1)}, bf16[128,896]{1,0:T(8,128)(2,1)S(1)}, u32[]{:S(2)}, u32[]{:S(2)}) %collective-permute-start) | collective-permute-done | bytes 229408 | tf_op jit(solution)/shard_map/ppermute | solution.py:41
  29.7 0.9 collective-permute-done.1.cot
  30.6 0.9 copy-done.1
  31.5 0.8 copy-done.2
  32.3 1.7 %shard_map.142 = (bf16[128,896]{1,0:T(8,128)(2,1)}, bf16[2,128,896]{2,1,0:T(8,128)(2,1)}) custom-call(s32[3]{0:T(128)S(1)} %pad_add_fusion.s, bf16[3,128,128]{2,1,0:T(8,128)(2,1)S(1)} %copy-done.1, f32[128,128]{1,0:T(8,128)S(1)} %copy-done.2, bf16[128,896]{1,0:T(8,128)(2,1)S(1)} %collective-permute-done.fwd, bf16[128,896]{1,0:T(8,128)(2,1)S(1)} %bitcast.34, ...), custom_call_target="tpu_custom_call" | custom-call | tf_op jit(solution)/shard_map/pallas_call | solution.py:353
  34.0 3.1 %collective-permute-start.4 = (bf16[2,128,896]{2,1,0:T(8,128)(2,1)}, bf16[2,128,896]{2,1,0:T(8,128)(2,1)S(1)}, u32[]{:S(2)}, u32[]{:S(2)}) collective-permute-start(bf16[2,128,896]{2,1,0:T(8,128)(2,1)} %get-tuple-element.26), channel_id=1, source_target_pairs={{0,2},{2,0},{1,3},{3,1},{4,6},{6,4},{5,7},{7,5},{8,10},{10,8},{9,1... | collective-permute-start | bytes 1376264 | tf_op jit(solution)/shard_map/ppermute | solution.py:45
  37.1 2.2 %collective-permute-start.5 = (bf16[128,896]{1,0:T(8,128)(2,1)S(1)}, bf16[128,896]{1,0:T(8,128)(2,1)S(1)}, u32[]{:S(2)}, u32[]{:S(2)}) collective-permute-start(bf16[128,896]{1,0:T(8,128)(2,1)S(1)} %bitcast.35), channel_id=1, source_target_pairs={{0,2},{2,0},{1,3},{3,1},{4,6},{6,4},{5,7},{7,5},{8,10},{10,8},{9,1... | collective-permute-start | bytes 688136 | tf_op jit(solution)/shard_map/ppermute | solution.py:45
  39.3 6.8 %all-to-all-start = ((bf16[8,16,896]{2,1,0:T(8,128)(2,1)}), bf16[8,16,896]{2,1,0:T(8,128)(2,1)S(1)}, u32[]{:S(2)}, u32[]{:S(2)}) async-start(bf16[8,16,896]{2,1,0:T(8,128)(2,1)} %bitcast.67), calls=%async_computation | async-start | bytes 458752 | tf_op jit(solution)/shard_map/all_to_all | solution.py:357
  46.2 6.1 %collective-permute-done.5.far_s = bf16[128,896]{1,0:T(8,128)(2,1)S(1)} collective-permute-done((bf16[128,896]{1,0:T(8,128)(2,1)S(1)}, bf16[128,896]{1,0:T(8,128)(2,1)S(1)}, u32[]{:S(2)}, u32[]{:S(2)}) %collective-permute-start.5) | collective-permute-done | bytes 229408 | tf_op jit(solution)/shard_map/ppermute | solution.py:45
  52.2 4.3 %shard_map.147.mine = f32[640,512]{1,0:T(8,128)S(1)} custom-call(s32[3]{0:T(128)S(1)} %pad_add_fusion.s, bf16[128,896]{1,0:T(8,128)(2,1)S(1)} %collective-permute-done.fwd, bf16[128,896]{1,0:T(8,128)(2,1)S(1)} %bitcast.36, bf16[128,896]{1,0:T(8,128)(2,1)S(1)} %collective-permute-done.1.cot, bf16[2,128,896]{2,1,0:T(8,128)(2,1)S(1)} %collective-permute-done.4.far, ...), custom_call_target="tpu_custom_call" | custom-call | tf_op jit(solution)/shard_map/pallas_call | solution.py:387
  56.5 3.6 %collective-permute-start.6 = (f32[640,512]{1,0:T(8,128)S(1)}, f32[640,512]{1,0:T(8,128)S(1)}, u32[]{:S(2)}, u32[]{:S(2)}) collective-permute-start(f32[640,512]{1,0:T(8,128)S(1)} %shard_map.147.mine), channel_id=1, source_target_pairs={{0,1},{1,0},{2,3},{3,2},{4,5},{5,4},{6,7},{7,6},{8,9},{9,8},{10,11... | collective-permute-start | bytes 3932168 | tf_op jit(solution)/shard_map/ppermute | solution.py:45
  60.2 1.6 %shard_map.143 = bf16[4,96,896]{2,1,0:T(8,128)(2,1)} custom-call(s32[3]{0:T(128)S(1)} %pad_add_fusion.s, bf16[128,896]{1,0:T(8,128)(2,1)S(1)} %bitcast.33), custom_call_target="tpu_custom_call" | custom-call | tf_op jit(solution)/shard_map/pallas_call | solution.py:359
  61.8 14.8 %all_to_all.20 = bf16[4,96,896]{2,1,0:T(8,128)(2,1)S(1)} all-to-all(bf16[4,96,896]{2,1,0:T(8,128)(2,1)} %shard_map.143), channel_id=1, replica_groups=mesh['pipe'=12,'y'=8,'xh'=2,'xl'=2,'core'=2] {'xh','xl'}, dimensions={0} | all-to-all | bytes 1376256 | tf_op jit(solution)/shard_map/all_to_all | solution.py:363
  76.6 3.3 %shard_map.144.mine = f32[320,256]{1,0:T(8,128)S(1)} custom-call(s32[3]{0:T(128)S(1)} %pad_add_fusion.s, bf16[2,2,96,896]{3,2,1,0:T(8,128)(2,1)S(1)} %bitcast.32, bf16[4,896,128]{2,1,0:T(8,128)(2,1)} %bitcast.55, bf16[4,896,128]{2,1,0:T(8,128)(2,1)} %bitcast.59, bf16[128,3584]{1,0:T(8,128)(2,1)} %bitcast.63, ...), custom_call_target="tpu_custom_call" | custom-call | tf_op jit(solution)/shard_map/pallas_call | solution.py:396
  79.9 3.3 %collective-permute-start.3 = (f32[320,256]{1,0:T(8,128)S(1)}, f32[320,256]{1,0:T(8,128)S(1)}, u32[]{:S(2)}, u32[]{:S(2)}) collective-permute-start(f32[320,256]{1,0:T(8,128)S(1)} %shard_map.144.mine), channel_id=1, source_target_pairs={{0,1},{1,0},{2,3},{3,2},{4,5},{5,4},{6,7},{7,6},{8,9},{9,8},{10,11... | collective-permute-start | bytes 983048 | tf_op jit(solution)/shard_map/ppermute | solution.py:45
  83.3 1.2 %collective-permute-done.3.other = f32[320,256]{1,0:T(8,128)S(1)} collective-permute-done((f32[320,256]{1,0:T(8,128)S(1)}, f32[320,256]{1,0:T(8,128)S(1)}, u32[]{:S(2)}, u32[]{:S(2)}) %collective-permute-start.3) | collective-permute-done | bytes 327712 | tf_op jit(solution)/shard_map/ppermute | solution.py:45
  84.5 4.2 %shard_map.145 = bf16[2,2,64,896]{3,2,1,0:T(8,128)(2,1)} custom-call(s32[3]{0:T(128)S(1)} %pad_add_fusion.s, f32[320,256]{1,0:T(8,128)S(1)} %shard_map.144.mine, f32[320,256]{1,0:T(8,128)S(1)} %collective-permute-done.3.other, bf16[4,896,128]{2,1,0:T(8,128)(2,1)} %bitcast.56, bf16[4,896,128]{2,1,0:T(8,128)(2,1)} %bitcast.60, bf16[128,3584]{1,0:T(8,128)(2,1)} %bitcast.64, ...), custom_call_target="tpu_custom_call" | custom-call | tf_op jit(solution)/shard_map/pallas_call | solution.py:403
  88.7 3.5 %all-to-all-start.2 = ((bf16[4,64,896]{2,1,0:T(8,128)(2,1)}), bf16[4,64,896]{2,1,0:T(8,128)(2,1)S(1)}, u32[]{:S(2)}, u32[]{:S(2)}) async-start(bf16[4,64,896]{2,1,0:T(8,128)(2,1)} %bitcast.65), calls=%async_computation.2 | async-start | bytes 917504 | tf_op jit(solution)/shard_map/all_to_all | solution.py:409
  92.2 3.9 %shard_map.148 = (bf16[2,128,896]{2,1,0:T(8,128)(2,1)}, bf16[128,512]{1,0:T(8,128)(2,1)}, bf16[128,512]{1,0:T(8,128)(2,1)}, bf16[128,512]{1,0:T(8,128)(2,1)}) custom-call(s32[3]{0:T(128)S(1)} %pad_add_fusion.s, f32[640,512]{1,0:T(8,128)S(1)} %shard_map.147.mine, f32[640,512]{1,0:T(8,128)S(1)} %collective-permute-done.6.other, bf16[4,896,256]{2,1,0:T(8,128)(2,1)} %bitcast.41, ...), custom_call_target="tpu_custom_call" | custom-call | tf_op jit(solution)/shard_map/pallas_call | solution.py:418
  96.1 3.3 %collective-permute-start.7 = (bf16[2,128,896]{2,1,0:T(8,128)(2,1)}, bf16[2,128,896]{2,1,0:T(8,128)(2,1)S(1)}, u32[]{:S(2)}, u32[]{:S(2)}) collective-permute-start(bf16[2,128,896]{2,1,0:T(8,128)(2,1)} %get-tuple-element.30), channel_id=1, source_target_pairs={{0,2},{2,0},{1,3},{3,1},{4,6},{6,4},{5,7},{7,5},{8,10},{10,8},{9,1... | collective-permute-start | bytes 1376264 | tf_op jit(solution)/shard_map/ppermute | solution.py:45
  99.4 1.2 %all-to-all-done.2.parts = bf16[4,64,896]{2,1,0:T(8,128)(2,1)S(1)} async-done(((bf16[4,64,896]{2,1,0:T(8,128)(2,1)}), bf16[4,64,896]{2,1,0:T(8,128)(2,1)S(1)}, u32[]{:S(2)}, u32[]{:S(2)}) %all-to-all-start.2) | async-done | bytes 458784 | tf_op jit(solution)/shard_map/all_to_all | solution.py:409
  100.6 1.2 %shard_map.146 = bf16[64,896]{1,0:T(8,128)(2,1)} custom-call(s32[3]{0:T(128)S(1)} %pad_add_fusion.s, bf16[4,64,896]{2,1,0:T(8,128)(2,1)S(1)} %all-to-all-done.2.parts), custom_call_target="tpu_custom_call" | custom-call | tf_op jit(solution)/shard_map/pallas_call | solution.py:410
  101.8 6.8 %all-to-all-start.3 = ((bf16[8,8,896]{2,1,0:T(8,128)(2,1)}), bf16[8,8,896]{2,1,0:T(8,128)(2,1)S(1)}, u32[]{:S(2)}, u32[]{:S(2)}) async-start(bf16[8,8,896]{2,1,0:T(8,128)(2,1)} %bitcast.66), calls=%async_computation.3 | async-start | bytes 229376 | tf_op jit(solution)/shard_map/all_to_all | solution.py:414
  108.7 1.5 %shard_map.150 = (bf16[128,64]{1,0:T(8,128)(2,1)S(1)}, bf16[128,64]{1,0:T(8,128)(2,1)S(1)}, bf16[128,64]{1,0:T(8,128)(2,1)S(1)}) custom-call(s32[3]{0:T(128)S(1)} %pad_add_fusion.s, s32[2,8,128]{2,1,0:T(8,128)} %bitcast.70, s32[2,8,128]{2,1,0:T(8,128)} %bitcast.73, s32[2,8,128]{2,1,0:T(8,128)} %bitcast.76, s32[2,8,128]{2,1,0:T(8,128)} %bitcast.79), custom_call_target="tpu_custom_call" | custom-call | tf_op jit(solution)/shard_map/pallas_call | solution.py:348
  110.1 3.3 %shard_map.149.keep = f32[2,128,896]{2,1,0:T(8,128)S(1)} custom-call(s32[3]{0:T(128)S(1)} %pad_add_fusion.s, bf16[128,512]{1,0:T(8,128)(2,1)} %get-tuple-element.27.hid, bf16[128,512]{1,0:T(8,128)(2,1)} %get-tuple-element.28.gg, bf16[128,512]{1,0:T(8,128)(2,1)} %get-tuple-element.29.gu, bf16[4,896,256]{2,1,0:T(8,128)(2,1)} %bitcast.42, ...), custom_call_target="tpu_custom_call" | custom-call | tf_op jit(solution)/shard_map/pallas_call | solution.py:424
  113.4 3.0 %all-to-all-done.3 = bf16[8,8,896]{2,1,0:T(8,128)(2,1)S(1)} async-done(((bf16[8,8,896]{2,1,0:T(8,128)(2,1)}), bf16[8,8,896]{2,1,0:T(8,128)(2,1)S(1)}, u32[]{:S(2)}, u32[]{:S(2)}) %all-to-all-start.3) | async-done | bytes 114720 | tf_op jit(solution)/shard_map/all_to_all | solution.py:414
  116.4 1.6 %shard_map.151 = (bf16[128,896]{1,0:T(8,128)(2,1)}, bf16[128,896]{1,0:T(8,128)(2,1)}) custom-call(s32[3]{0:T(128)S(1)} %pad_add_fusion.s, bf16[64,896]{1,0:T(8,128)(2,1)S(1)} %bitcast.37, f32[2,128,896]{2,1,0:T(8,128)S(1)} %shard_map.149.keep, bf16[2,128,896]{2,1,0:T(8,128)(2,1)S(1)} %collective-permute-done.7.far, ...), custom_call_target="tpu_custom_call" | custom-call | tf_op jit(solution)/shard_map/pallas_call | solution.py:431
  (14 shorter events, 0.1 us)
Async XLA Ops:
  5.2 13.2 %copy-start.3 = (bf16[1,128,896]{2,1,0:T(8,128)(2,1)S(1)}, bf16[1,128,896]{2,1,0:T(8,128)(2,1)}, u32[]{:S(2)}) copy-start(bf16[1,128,896]{2,1,0:T(8,128)(2,1)} %param.13) | copy-start | bytes 688132
  5.2 15.1 %copy-start.4 = (bf16[1,128,896]{2,1,0:T(8,128)(2,1)S(1)}, bf16[1,128,896]{2,1,0:T(8,128)(2,1)}, u32[]{:S(2)}) copy-start(bf16[1,128,896]{2,1,0:T(8,128)(2,1)} %param.14) | copy-start | bytes 688132
  5.2 25.4 %copy-start = (bf16[1,128,896]{2,1,0:T(8,128)(2,1)S(1)}, bf16[1,128,896]{2,1,0:T(8,128)(2,1)}, u32[]{:S(2)}) copy-start(bf16[1,128,896]{2,1,0:T(8,128)(2,1)} %param.15) | copy-start | bytes 688132
  6.0 46.2 %collective-permute-start.2 = (bf16[2,1280,896]{2,1,0:T(8,128)(2,1)}, bf16[2,1280,896]{2,1,0:T(8,128)(2,1)}, u32[]{:S(2)}, u32[]{:S(2)}) collective-permute-start(bf16[2,1280,896]{2,1,0:T(8,128)(2,1)} %get-tuple-element.25), channel_id=1, source_target_pairs={{0,1},{1,0},{2,3},{3,2},{4,5},{5,4},{6,7},{7,6},{8,9},{9,8},{10,11... | collective-permute-start | bytes 13762568 | tf_op jit(solution)/shard_map/ppermute | solution.py:45
  18.4 11.3 %collective-permute-start = (bf16[128,896]{1,0:T(8,128)(2,1)S(1)}, bf16[128,896]{1,0:T(8,128)(2,1)S(1)}, u32[]{:S(2)}, u32[]{:S(2)}) collective-permute-start(bf16[128,896]{1,0:T(8,128)(2,1)S(1)} %bitcast.80), channel_id=1, source_target_pairs={{704,0},{0,64},{64,128},{128,192},{192,256},{256,320},{320,384},{3... | collective-permute-start | bytes 688136 | tf_op jit(solution)/shard_map/ppermute | solution.py:41
  20.3 10.3 %collective-permute-start.1 = (bf16[128,896]{1,0:T(8,128)(2,1)S(1)}, bf16[128,896]{1,0:T(8,128)(2,1)S(1)}, u32[]{:S(2)}, u32[]{:S(2)}) collective-permute-start(bf16[128,896]{1,0:T(8,128)(2,1)S(1)} %bitcast.81), channel_id=1, source_target_pairs={{64,0},{128,64},{192,128},{256,192},{320,256},{384,320},{448,384},... | collective-permute-start | bytes 688136 | tf_op jit(solution)/shard_map/ppermute | solution.py:41
  30.6 0.9 copy-start.1
  31.5 0.8 copy-start.2
  34.0 18.2 %collective-permute-start.4 = (bf16[2,128,896]{2,1,0:T(8,128)(2,1)}, bf16[2,128,896]{2,1,0:T(8,128)(2,1)S(1)}, u32[]{:S(2)}, u32[]{:S(2)}) collective-permute-start(bf16[2,128,896]{2,1,0:T(8,128)(2,1)} %get-tuple-element.26), channel_id=1, source_target_pairs={{0,2},{2,0},{1,3},{3,1},{4,6},{6,4},{5,7},{7,5},{8,10},{10,8},{9,1... | collective-permute-start | bytes 1376264 | tf_op jit(solution)/shard_map/ppermute | solution.py:45
  37.1 15.1 %collective-permute-start.5 = (bf16[128,896]{1,0:T(8,128)(2,1)S(1)}, bf16[128,896]{1,0:T(8,128)(2,1)S(1)}, u32[]{:S(2)}, u32[]{:S(2)}) collective-permute-start(bf16[128,896]{1,0:T(8,128)(2,1)S(1)} %bitcast.35), channel_id=1, source_target_pairs={{0,2},{2,0},{1,3},{3,1},{4,6},{6,4},{5,7},{7,5},{8,10},{10,8},{9,1... | collective-permute-start | bytes 688136 | tf_op jit(solution)/shard_map/ppermute | solution.py:45
  39.3 20.9 %all-to-all-start = ((bf16[8,16,896]{2,1,0:T(8,128)(2,1)}), bf16[8,16,896]{2,1,0:T(8,128)(2,1)S(1)}, u32[]{:S(2)}, u32[]{:S(2)}) async-start(bf16[8,16,896]{2,1,0:T(8,128)(2,1)} %bitcast.67), calls=%async_computation | async-start | bytes 458752 | tf_op jit(solution)/shard_map/all_to_all | solution.py:357
  56.5 35.6 %collective-permute-start.6 = (f32[640,512]{1,0:T(8,128)S(1)}, f32[640,512]{1,0:T(8,128)S(1)}, u32[]{:S(2)}, u32[]{:S(2)}) collective-permute-start(f32[640,512]{1,0:T(8,128)S(1)} %shard_map.147.mine), channel_id=1, source_target_pairs={{0,1},{1,0},{2,3},{3,2},{4,5},{5,4},{6,7},{7,6},{8,9},{9,8},{10,11... | collective-permute-start | bytes 3932168 | tf_op jit(solution)/shard_map/ppermute | solution.py:45
  79.9 4.6 %collective-permute-start.3 = (f32[320,256]{1,0:T(8,128)S(1)}, f32[320,256]{1,0:T(8,128)S(1)}, u32[]{:S(2)}, u32[]{:S(2)}) collective-permute-start(f32[320,256]{1,0:T(8,128)S(1)} %shard_map.144.mine), channel_id=1, source_target_pairs={{0,1},{1,0},{2,3},{3,2},{4,5},{5,4},{6,7},{7,6},{8,9},{9,8},{10,11... | collective-permute-start | bytes 983048 | tf_op jit(solution)/shard_map/ppermute | solution.py:45
  88.7 11.9 %all-to-all-start.2 = ((bf16[4,64,896]{2,1,0:T(8,128)(2,1)}), bf16[4,64,896]{2,1,0:T(8,128)(2,1)S(1)}, u32[]{:S(2)}, u32[]{:S(2)}) async-start(bf16[4,64,896]{2,1,0:T(8,128)(2,1)} %bitcast.65), calls=%async_computation.2 | async-start | bytes 917504 | tf_op jit(solution)/shard_map/all_to_all | solution.py:409
  96.1 20.4 %collective-permute-start.7 = (bf16[2,128,896]{2,1,0:T(8,128)(2,1)}, bf16[2,128,896]{2,1,0:T(8,128)(2,1)S(1)}, u32[]{:S(2)}, u32[]{:S(2)}) collective-permute-start(bf16[2,128,896]{2,1,0:T(8,128)(2,1)} %get-tuple-element.30), channel_id=1, source_target_pairs={{0,2},{2,0},{1,3},{3,1},{4,6},{6,4},{5,7},{7,5},{8,10},{10,8},{9,1... | collective-permute-start | bytes 1376264 | tf_op jit(solution)/shard_map/ppermute | solution.py:45
  101.8 14.6 %all-to-all-start.3 = ((bf16[8,8,896]{2,1,0:T(8,128)(2,1)}), bf16[8,8,896]{2,1,0:T(8,128)(2,1)S(1)}, u32[]{:S(2)}, u32[]{:S(2)}) async-start(bf16[8,8,896]{2,1,0:T(8,128)(2,1)} %bitcast.66), calls=%async_computation.3 | async-start | bytes 229376 | tf_op jit(solution)/shard_map/all_to_all | solution.py:414

commit v5 on v4

--- a/solution.py
+++ b/solution.py
@@ -262,7 +262,6 @@
     j = pl.program_id(0)
     n = hid.shape[0]
     m = n // 2
-    w = gate.shape[2]
 
     @pl.when(j == 0)
     def _():
@@ -279,11 +278,11 @@
         gg[...] = jnp.where(back, dh * b * (sg * (1.0 + a * (1.0 - sg))), 0.0).astype(BF)
         gu[...] = jnp.where(back, dh * (a * sg), 0.0).astype(BF)
 
-    rows = (
-        dot(hid[:, :w], down[...]) + dot(hid[:, w:], down_o[0])
-        + contract_last(gg[:, :w], gate[0]) + contract_last(gg[:, w:], gate_o[0])
-        + contract_last(gu[:, :w], up[0]) + contract_last(gu[:, w:], up_o[0])
-    ).astype(BF)
+    g = jnp.concatenate([gate[0], gate_o[0]], axis=1)
+    u = jnp.concatenate([up[0], up_o[0]], axis=1)
+    d = jnp.concatenate([down[...], down_o[0]], axis=0)
+    both = jnp.concatenate([gg[...], gu[...]], axis=1)
+    rows = (dot(hid[...], d) + contract_last(both, jnp.concatenate([g, u], axis=1))).astype(BF)
     out[0, 0] = rows[:m]
     out[1, 0] = rows[m:]
 
@@ -349,6 +348,7 @@
         adders_body, (tall, tall, tall), in_specs=[tab] * 4, out_specs=(whole(tall.shape),) * 3,
     )(here, *plan)
 
+    sel, scale = [pltpu.with_memory_space_constraint(v, pltpu.HBM) for v in (sel, scale)]
     act = whole((tokens, shard))
     parcel, pair = call(
         parcel_body, (pltpu.HBM((tokens, shard), BF), pltpu.HBM((2, tokens, shard), BF)),

time: 119 us -> 118 us (level)
  local copies, waits for them, and re-layouts: 1.75 us -> 0.02 us
    unnamed x10 -> x6, local copies, waits for them, and re-layouts: 1.75 us -> 0.02 us
  transfers between devices with their start and end apart: 11 -> 11, of which waited for: 6 -> 6; matrix products, arithmetic and copies ran while one was open for 0% -> 0% of each run, Pallas kernels for 21% -> 22%
where the time goes in v5:
time: 118 us; the launch traced here: 117 us
  starting transfers between devices  52.3 us (44%)
  Pallas kernels  32.5 us (28%)
  waiting for transfers between devices  16.5 us (14%)
  blocking collectives  14.8 us (13%)
    ppermute x6, starting transfers between devices, swapped(): return lax.ppermute(block, axis, [(0, 1), (1, 0)])  28 us
    all_to_all x1, blocking collectives, local(): lax.all_to_all(fan, ('xh', 'xl'), 0, 0, tiled=True)  14.8 us
    ppermute x6, waiting for transfers between devices, swapped(): return lax.ppermute(block, axis, [(0, 1), (1, 0)])  7.32 us
    ppermute x2, starting transfers between devices, shifted(): lax.ppermute(block, axis, [((i - distance) % n, i) for i in range(n)])  7.24 us
    all_to_all x1, starting transfers between devices, local(): lax.all_to_all(parcel.reshape(experts, PAD, shard), 'y', 0, 0, tiled=True)  6.84 us
    all_to_all x1, starting transfers between devices, local(): lax.all_to_all(ret.reshape(experts, 2 * CAP, shard), 'y', 0, 0, tiled=True)  6.82 us
    ppermute x2, waiting for transfers between devices, shifted(): lax.ppermute(block, axis, [((i - distance) % n, i) for i in range(n)])  4.92 us
    pallas_call x1, Pallas kernels, local(): call(prep_first_body, made, in_specs=[hbm] * 10, out_specs=(hbm,) * 3, sc...  4.49 us
  transfers between devices with their start and end apart: 11, of which 6 were waited for; matrix products, arithmetic and copies ran while one was open for 0% of the time, Pallas kernels for 22%

profile of v5, /device:TPU:1, one launch (start us, length us, event | category | flops | bytes accessed | tf_op | source)
XLA Modules:
  0.0 117.1 jit_solution(8773523262180383071)
XLA Ops:
  0.6 0.1 pad_add_fusion.s
  0.7 4.5 %shard_map.140 = (bf16[2,1280,896]{2,1,0:T(8,128)(2,1)}, bf16[3,128,128]{2,1,0:T(8,128)(2,1)}, f32[128,128]{1,0:T(8,128)}) custom-call(s32[3]{0:T(128)S(1)} %pad_add_fusion.s, bf16[4,896,256]{2,1,0:T(8,128)(2,1)} %bitcast.38, bf16[4,896,256]{2,1,0:T(8,128)(2,1)} %bitcast.43, bf16[4,896,128]{2,1,0:T(8,128)(2,1)} %bitcast.53, bf16[4,896,128]{2,1,0:T(8,128)(2,1)} %bitcast.57, ...), custom_call_target="tpu_custom_call" | custom-call | tf_op jit(solution)/shard_map/pallas_call | solution.py:340
  5.2 0.0 copy-start.1
  5.2 0.7 shard_map.141
  6.0 12.4 %collective-permute-start.2 = (bf16[2,1280,896]{2,1,0:T(8,128)(2,1)}, bf16[2,1280,896]{2,1,0:T(8,128)(2,1)}, u32[]{:S(2)}, u32[]{:S(2)}) collective-permute-start(bf16[2,1280,896]{2,1,0:T(8,128)(2,1)} %get-tuple-element.25), channel_id=1, source_target_pairs={{0,1},{1,0},{2,3},{3,2},{4,5},{5,4},{6,7},{7,6},{8,9},{9,8},{10,11... | collective-permute-start | bytes 13762568 | tf_op jit(solution)/shard_map/ppermute | solution.py:45
  18.4 1.9 %collective-permute-start = (bf16[128,896]{1,0:T(8,128)(2,1)S(1)}, bf16[128,896]{1,0:T(8,128)(2,1)S(1)}, u32[]{:S(2)}, u32[]{:S(2)}) collective-permute-start(bf16[128,896]{1,0:T(8,128)(2,1)S(1)} %bitcast.80), channel_id=1, source_target_pairs={{704,0},{0,64},{64,128},{128,192},{192,256},{256,320},{320,384},{3... | collective-permute-start | bytes 688136 | tf_op jit(solution)/shard_map/ppermute | solution.py:41
  20.3 5.3 %collective-permute-start.1 = (bf16[128,896]{1,0:T(8,128)(2,1)S(1)}, bf16[128,896]{1,0:T(8,128)(2,1)S(1)}, u32[]{:S(2)}, u32[]{:S(2)}) collective-permute-start(bf16[128,896]{1,0:T(8,128)(2,1)S(1)} %bitcast.81), channel_id=1, source_target_pairs={{64,0},{128,64},{192,128},{256,192},{320,256},{384,320},{448,384},... | collective-permute-start | bytes 688136 | tf_op jit(solution)/shard_map/ppermute | solution.py:41
  25.7 4.0 %collective-permute-done.fwd = bf16[128,896]{1,0:T(8,128)(2,1)S(1)} collective-permute-done((bf16[128,896]{1,0:T(8,128)(2,1)S(1)}, bf16[128,896]{1,0:T(8,128)(2,1)S(1)}, u32[]{:S(2)}, u32[]{:S(2)}) %collective-permute-start) | collective-permute-done | bytes 229408 | tf_op jit(solution)/shard_map/ppermute | solution.py:41
  29.7 0.9 collective-permute-done.1.cot
  30.6 2.6 %shard_map.142 = (bf16[128,896]{1,0:T(8,128)(2,1)}, bf16[2,128,896]{2,1,0:T(8,128)(2,1)}) custom-call(s32[3]{0:T(128)S(1)} %pad_add_fusion.s, bf16[3,128,128]{2,1,0:T(8,128)(2,1)} %get-tuple-element.22.sel, f32[128,128]{1,0:T(8,128)} %get-tuple-element.23.scale, bf16[128,896]{1,0:T(8,128)(2,1)S(1)} %collective-permute-done.fwd, ...), custom_call_target="tpu_custom_call" | custom-call | tf_op jit(solution)/shard_map/pallas_call | solution.py:353
  33.2 3.1 %collective-permute-start.4 = (bf16[2,128,896]{2,1,0:T(8,128)(2,1)}, bf16[2,128,896]{2,1,0:T(8,128)(2,1)S(1)}, u32[]{:S(2)}, u32[]{:S(2)}) collective-permute-start(bf16[2,128,896]{2,1,0:T(8,128)(2,1)} %get-tuple-element.26), channel_id=1, source_target_pairs={{0,2},{2,0},{1,3},{3,1},{4,6},{6,4},{5,7},{7,5},{8,10},{10,8},{9,1... | collective-permute-start | bytes 1376264 | tf_op jit(solution)/shard_map/ppermute | solution.py:45
  36.3 2.2 %collective-permute-start.5 = (bf16[128,896]{1,0:T(8,128)(2,1)S(1)}, bf16[128,896]{1,0:T(8,128)(2,1)S(1)}, u32[]{:S(2)}, u32[]{:S(2)}) collective-permute-start(bf16[128,896]{1,0:T(8,128)(2,1)S(1)} %bitcast.35), channel_id=1, source_target_pairs={{0,2},{2,0},{1,3},{3,1},{4,6},{6,4},{5,7},{7,5},{8,10},{10,8},{9,1... | collective-permute-start | bytes 688136 | tf_op jit(solution)/shard_map/ppermute | solution.py:45
  38.5 6.8 %all-to-all-start = ((bf16[8,16,896]{2,1,0:T(8,128)(2,1)}), bf16[8,16,896]{2,1,0:T(8,128)(2,1)S(1)}, u32[]{:S(2)}, u32[]{:S(2)}) async-start(bf16[8,16,896]{2,1,0:T(8,128)(2,1)} %bitcast.67), calls=%async_computation | async-start | bytes 458752 | tf_op jit(solution)/shard_map/all_to_all | solution.py:357
  45.3 6.1 %collective-permute-done.5.far_s = bf16[128,896]{1,0:T(8,128)(2,1)S(1)} collective-permute-done((bf16[128,896]{1,0:T(8,128)(2,1)S(1)}, bf16[128,896]{1,0:T(8,128)(2,1)S(1)}, u32[]{:S(2)}, u32[]{:S(2)}) %collective-permute-start.5) | collective-permute-done | bytes 229408 | tf_op jit(solution)/shard_map/ppermute | solution.py:45
  51.4 4.3 %shard_map.147.mine = f32[640,512]{1,0:T(8,128)S(1)} custom-call(s32[3]{0:T(128)S(1)} %pad_add_fusion.s, bf16[128,896]{1,0:T(8,128)(2,1)S(1)} %collective-permute-done.fwd, bf16[128,896]{1,0:T(8,128)(2,1)S(1)} %bitcast.36, bf16[128,896]{1,0:T(8,128)(2,1)S(1)} %collective-permute-done.1.cot, bf16[2,128,896]{2,1,0:T(8,128)(2,1)S(1)} %collective-permute-done.4.far, ...), custom_call_target="tpu_custom_call" | custom-call | tf_op jit(solution)/shard_map/pallas_call | solution.py:387
  55.7 3.6 %collective-permute-start.6 = (f32[640,512]{1,0:T(8,128)S(1)}, f32[640,512]{1,0:T(8,128)S(1)}, u32[]{:S(2)}, u32[]{:S(2)}) collective-permute-start(f32[640,512]{1,0:T(8,128)S(1)} %shard_map.147.mine), channel_id=1, source_target_pairs={{0,1},{1,0},{2,3},{3,2},{4,5},{5,4},{6,7},{7,6},{8,9},{9,8},{10,11... | collective-permute-start | bytes 3932168 | tf_op jit(solution)/shard_map/ppermute | solution.py:45
  59.3 1.6 %shard_map.143 = bf16[4,96,896]{2,1,0:T(8,128)(2,1)} custom-call(s32[3]{0:T(128)S(1)} %pad_add_fusion.s, bf16[128,896]{1,0:T(8,128)(2,1)S(1)} %bitcast.33), custom_call_target="tpu_custom_call" | custom-call | tf_op jit(solution)/shard_map/pallas_call | solution.py:359
  61.0 14.8 %all_to_all.20 = bf16[4,96,896]{2,1,0:T(8,128)(2,1)S(1)} all-to-all(bf16[4,96,896]{2,1,0:T(8,128)(2,1)} %shard_map.143), channel_id=1, replica_groups=mesh['pipe'=12,'y'=8,'xh'=2,'xl'=2,'core'=2] {'xh','xl'}, dimensions={0} | all-to-all | bytes 1376256 | tf_op jit(solution)/shard_map/all_to_all | solution.py:363
  75.8 3.3 %shard_map.144.mine = f32[320,256]{1,0:T(8,128)S(1)} custom-call(s32[3]{0:T(128)S(1)} %pad_add_fusion.s, bf16[2,2,96,896]{3,2,1,0:T(8,128)(2,1)S(1)} %bitcast.32, bf16[4,896,128]{2,1,0:T(8,128)(2,1)} %bitcast.55, bf16[4,896,128]{2,1,0:T(8,128)(2,1)} %bitcast.59, bf16[128,3584]{1,0:T(8,128)(2,1)} %bitcast.63, ...), custom_call_target="tpu_custom_call" | custom-call | tf_op jit(solution)/shard_map/pallas_call | solution.py:396
  79.1 3.3 %collective-permute-start.3 = (f32[320,256]{1,0:T(8,128)S(1)}, f32[320,256]{1,0:T(8,128)S(1)}, u32[]{:S(2)}, u32[]{:S(2)}) collective-permute-start(f32[320,256]{1,0:T(8,128)S(1)} %shard_map.144.mine), channel_id=1, source_target_pairs={{0,1},{1,0},{2,3},{3,2},{4,5},{5,4},{6,7},{7,6},{8,9},{9,8},{10,11... | collective-permute-start | bytes 983048 | tf_op jit(solution)/shard_map/ppermute | solution.py:45
  82.4 1.2 %collective-permute-done.3.other = f32[320,256]{1,0:T(8,128)S(1)} collective-permute-done((f32[320,256]{1,0:T(8,128)S(1)}, f32[320,256]{1,0:T(8,128)S(1)}, u32[]{:S(2)}, u32[]{:S(2)}) %collective-permute-start.3) | collective-permute-done | bytes 327712 | tf_op jit(solution)/shard_map/ppermute | solution.py:45
  83.7 4.0 %shard_map.145 = bf16[2,2,64,896]{3,2,1,0:T(8,128)(2,1)} custom-call(s32[3]{0:T(128)S(1)} %pad_add_fusion.s, f32[320,256]{1,0:T(8,128)S(1)} %shard_map.144.mine, f32[320,256]{1,0:T(8,128)S(1)} %collective-permute-done.3.other, bf16[4,896,128]{2,1,0:T(8,128)(2,1)} %bitcast.56, bf16[4,896,128]{2,1,0:T(8,128)(2,1)} %bitcast.60, bf16[128,3584]{1,0:T(8,128)(2,1)} %bitcast.64, ...), custom_call_target="tpu_custom_call" | custom-call | tf_op jit(solution)/shard_map/pallas_call | solution.py:403
  87.7 3.5 %all-to-all-start.2 = ((bf16[4,64,896]{2,1,0:T(8,128)(2,1)}), bf16[4,64,896]{2,1,0:T(8,128)(2,1)S(1)}, u32[]{:S(2)}, u32[]{:S(2)}) async-start(bf16[4,64,896]{2,1,0:T(8,128)(2,1)} %bitcast.65), calls=%async_computation.2 | async-start | bytes 917504 | tf_op jit(solution)/shard_map/all_to_all | solution.py:409
  91.2 3.9 %shard_map.148 = (bf16[2,128,896]{2,1,0:T(8,128)(2,1)}, bf16[128,512]{1,0:T(8,128)(2,1)}, bf16[128,512]{1,0:T(8,128)(2,1)}, bf16[128,512]{1,0:T(8,128)(2,1)}) custom-call(s32[3]{0:T(128)S(1)} %pad_add_fusion.s, f32[640,512]{1,0:T(8,128)S(1)} %shard_map.147.mine, f32[640,512]{1,0:T(8,128)S(1)} %collective-permute-done.6.other, bf16[4,896,256]{2,1,0:T(8,128)(2,1)} %bitcast.41, ...), custom_call_target="tpu_custom_call" | custom-call | tf_op jit(solution)/shard_map/pallas_call | solution.py:418
  95.1 3.3 %collective-permute-start.7 = (bf16[2,128,896]{2,1,0:T(8,128)(2,1)}, bf16[2,128,896]{2,1,0:T(8,128)(2,1)S(1)}, u32[]{:S(2)}, u32[]{:S(2)}) collective-permute-start(bf16[2,128,896]{2,1,0:T(8,128)(2,1)} %get-tuple-element.30), channel_id=1, source_target_pairs={{0,2},{2,0},{1,3},{3,1},{4,6},{6,4},{5,7},{7,5},{8,10},{10,8},{9,1... | collective-permute-start | bytes 1376264 | tf_op jit(solution)/shard_map/ppermute | solution.py:45
  98.4 1.2 %all-to-all-done.2.parts = bf16[4,64,896]{2,1,0:T(8,128)(2,1)S(1)} async-done(((bf16[4,64,896]{2,1,0:T(8,128)(2,1)}), bf16[4,64,896]{2,1,0:T(8,128)(2,1)S(1)}, u32[]{:S(2)}, u32[]{:S(2)}) %all-to-all-start.2) | async-done | bytes 458784 | tf_op jit(solution)/shard_map/all_to_all | solution.py:409
  99.6 1.2 %shard_map.146 = bf16[64,896]{1,0:T(8,128)(2,1)} custom-call(s32[3]{0:T(128)S(1)} %pad_add_fusion.s, bf16[4,64,896]{2,1,0:T(8,128)(2,1)S(1)} %all-to-all-done.2.parts), custom_call_target="tpu_custom_call" | custom-call | tf_op jit(solution)/shard_map/pallas_call | solution.py:410
  100.9 6.8 %all-to-all-start.3 = ((bf16[8,8,896]{2,1,0:T(8,128)(2,1)}), bf16[8,8,896]{2,1,0:T(8,128)(2,1)S(1)}, u32[]{:S(2)}, u32[]{:S(2)}) async-start(bf16[8,8,896]{2,1,0:T(8,128)(2,1)} %bitcast.66), calls=%async_computation.3 | async-start | bytes 229376 | tf_op jit(solution)/shard_map/all_to_all | solution.py:414
  107.7 1.5 %shard_map.150 = (bf16[128,64]{1,0:T(8,128)(2,1)S(1)}, bf16[128,64]{1,0:T(8,128)(2,1)S(1)}, bf16[128,64]{1,0:T(8,128)(2,1)S(1)}) custom-call(s32[3]{0:T(128)S(1)} %pad_add_fusion.s, s32[2,8,128]{2,1,0:T(8,128)} %bitcast.70, s32[2,8,128]{2,1,0:T(8,128)} %bitcast.73, s32[2,8,128]{2,1,0:T(8,128)} %bitcast.76, s32[2,8,128]{2,1,0:T(8,128)} %bitcast.79), custom_call_target="tpu_custom_call" | custom-call | tf_op jit(solution)/shard_map/pallas_call | solution.py:347
  109.2 3.3 %shard_map.149.keep = f32[2,128,896]{2,1,0:T(8,128)S(1)} custom-call(s32[3]{0:T(128)S(1)} %pad_add_fusion.s, bf16[128,512]{1,0:T(8,128)(2,1)} %get-tuple-element.27.hid, bf16[128,512]{1,0:T(8,128)(2,1)} %get-tuple-element.28.gg, bf16[128,512]{1,0:T(8,128)(2,1)} %get-tuple-element.29.gu, bf16[4,896,256]{2,1,0:T(8,128)(2,1)} %bitcast.42, ...), custom_call_target="tpu_custom_call" | custom-call | tf_op jit(solution)/shard_map/pallas_call | solution.py:424
  112.5 3.0 %all-to-all-done.3 = bf16[8,8,896]{2,1,0:T(8,128)(2,1)S(1)} async-done(((bf16[8,8,896]{2,1,0:T(8,128)(2,1)}), bf16[8,8,896]{2,1,0:T(8,128)(2,1)S(1)}, u32[]{:S(2)}, u32[]{:S(2)}) %all-to-all-start.3) | async-done | bytes 114720 | tf_op jit(solution)/shard_map/all_to_all | solution.py:414
  115.5 1.6 %shard_map.151 = (bf16[128,896]{1,0:T(8,128)(2,1)}, bf16[128,896]{1,0:T(8,128)(2,1)}) custom-call(s32[3]{0:T(128)S(1)} %pad_add_fusion.s, bf16[64,896]{1,0:T(8,128)(2,1)S(1)} %bitcast.37, f32[2,128,896]{2,1,0:T(8,128)S(1)} %shard_map.149.keep, bf16[2,128,896]{2,1,0:T(8,128)(2,1)S(1)} %collective-permute-done.7.far, ...), custom_call_target="tpu_custom_call" | custom-call | tf_op jit(solution)/shard_map/pallas_call | solution.py:431
  (10 shorter events, 0.0 us)
Async XLA Ops:
  5.2 13.2 %copy-start.1 = (bf16[1,128,896]{2,1,0:T(8,128)(2,1)S(1)}, bf16[1,128,896]{2,1,0:T(8,128)(2,1)}, u32[]{:S(2)}) copy-start(bf16[1,128,896]{2,1,0:T(8,128)(2,1)} %param.13) | copy-start | bytes 688132
  5.2 15.1 %copy-start.2 = (bf16[1,128,896]{2,1,0:T(8,128)(2,1)S(1)}, bf16[1,128,896]{2,1,0:T(8,128)(2,1)}, u32[]{:S(2)}) copy-start(bf16[1,128,896]{2,1,0:T(8,128)(2,1)} %param.14) | copy-start | bytes 688132
  5.2 25.4 %copy-start = (bf16[1,128,896]{2,1,0:T(8,128)(2,1)S(1)}, bf16[1,128,896]{2,1,0:T(8,128)(2,1)}, u32[]{:S(2)}) copy-start(bf16[1,128,896]{2,1,0:T(8,128)(2,1)} %param.15) | copy-start | bytes 688132
  6.0 45.4 %collective-permute-start.2 = (bf16[2,1280,896]{2,1,0:T(8,128)(2,1)}, bf16[2,1280,896]{2,1,0:T(8,128)(2,1)}, u32[]{:S(2)}, u32[]{:S(2)}) collective-permute-start(bf16[2,1280,896]{2,1,0:T(8,128)(2,1)} %get-tuple-element.25), channel_id=1, source_target_pairs={{0,1},{1,0},{2,3},{3,2},{4,5},{5,4},{6,7},{7,6},{8,9},{9,8},{10,11... | collective-permute-start | bytes 13762568 | tf_op jit(solution)/shard_map/ppermute | solution.py:45
  18.4 11.3 %collective-permute-start = (bf16[128,896]{1,0:T(8,128)(2,1)S(1)}, bf16[128,896]{1,0:T(8,128)(2,1)S(1)}, u32[]{:S(2)}, u32[]{:S(2)}) collective-permute-start(bf16[128,896]{1,0:T(8,128)(2,1)S(1)} %bitcast.80), channel_id=1, source_target_pairs={{704,0},{0,64},{64,128},{128,192},{192,256},{256,320},{320,384},{3... | collective-permute-start | bytes 688136 | tf_op jit(solution)/shard_map/ppermute | solution.py:41
  20.3 10.3 %collective-permute-start.1 = (bf16[128,896]{1,0:T(8,128)(2,1)S(1)}, bf16[128,896]{1,0:T(8,128)(2,1)S(1)}, u32[]{:S(2)}, u32[]{:S(2)}) collective-permute-start(bf16[128,896]{1,0:T(8,128)(2,1)S(1)} %bitcast.81), channel_id=1, source_target_pairs={{64,0},{128,64},{192,128},{256,192},{320,256},{384,320},{448,384},... | collective-permute-start | bytes 688136 | tf_op jit(solution)/shard_map/ppermute | solution.py:41
  33.2 18.2 %collective-permute-start.4 = (bf16[2,128,896]{2,1,0:T(8,128)(2,1)}, bf16[2,128,896]{2,1,0:T(8,128)(2,1)S(1)}, u32[]{:S(2)}, u32[]{:S(2)}) collective-permute-start(bf16[2,128,896]{2,1,0:T(8,128)(2,1)} %get-tuple-element.26), channel_id=1, source_target_pairs={{0,2},{2,0},{1,3},{3,1},{4,6},{6,4},{5,7},{7,5},{8,10},{10,8},{9,1... | collective-permute-start | bytes 1376264 | tf_op jit(solution)/shard_map/ppermute | solution.py:45
  36.3 15.1 %collective-permute-start.5 = (bf16[128,896]{1,0:T(8,128)(2,1)S(1)}, bf16[128,896]{1,0:T(8,128)(2,1)S(1)}, u32[]{:S(2)}, u32[]{:S(2)}) collective-permute-start(bf16[128,896]{1,0:T(8,128)(2,1)S(1)} %bitcast.35), channel_id=1, source_target_pairs={{0,2},{2,0},{1,3},{3,1},{4,6},{6,4},{5,7},{7,5},{8,10},{10,8},{9,1... | collective-permute-start | bytes 688136 | tf_op jit(solution)/shard_map/ppermute | solution.py:45
  38.5 20.9 %all-to-all-start = ((bf16[8,16,896]{2,1,0:T(8,128)(2,1)}), bf16[8,16,896]{2,1,0:T(8,128)(2,1)S(1)}, u32[]{:S(2)}, u32[]{:S(2)}) async-start(bf16[8,16,896]{2,1,0:T(8,128)(2,1)} %bitcast.67), calls=%async_computation | async-start | bytes 458752 | tf_op jit(solution)/shard_map/all_to_all | solution.py:357
  55.7 35.5 %collective-permute-start.6 = (f32[640,512]{1,0:T(8,128)S(1)}, f32[640,512]{1,0:T(8,128)S(1)}, u32[]{:S(2)}, u32[]{:S(2)}) collective-permute-start(f32[640,512]{1,0:T(8,128)S(1)} %shard_map.147.mine), channel_id=1, source_target_pairs={{0,1},{1,0},{2,3},{3,2},{4,5},{5,4},{6,7},{7,6},{8,9},{9,8},{10,11... | collective-permute-start | bytes 3932168 | tf_op jit(solution)/shard_map/ppermute | solution.py:45
  79.1 4.6 %collective-permute-start.3 = (f32[320,256]{1,0:T(8,128)S(1)}, f32[320,256]{1,0:T(8,128)S(1)}, u32[]{:S(2)}, u32[]{:S(2)}) collective-permute-start(f32[320,256]{1,0:T(8,128)S(1)} %shard_map.144.mine), channel_id=1, source_target_pairs={{0,1},{1,0},{2,3},{3,2},{4,5},{5,4},{6,7},{7,6},{8,9},{9,8},{10,11... | collective-permute-start | bytes 983048 | tf_op jit(solution)/shard_map/ppermute | solution.py:45
  87.7 11.9 %all-to-all-start.2 = ((bf16[4,64,896]{2,1,0:T(8,128)(2,1)}), bf16[4,64,896]{2,1,0:T(8,128)(2,1)S(1)}, u32[]{:S(2)}, u32[]{:S(2)}) async-start(bf16[4,64,896]{2,1,0:T(8,128)(2,1)} %bitcast.65), calls=%async_computation.2 | async-start | bytes 917504 | tf_op jit(solution)/shard_map/all_to_all | solution.py:409
  95.1 20.4 %collective-permute-start.7 = (bf16[2,128,896]{2,1,0:T(8,128)(2,1)}, bf16[2,128,896]{2,1,0:T(8,128)(2,1)S(1)}, u32[]{:S(2)}, u32[]{:S(2)}) collective-permute-start(bf16[2,128,896]{2,1,0:T(8,128)(2,1)} %get-tuple-element.30), channel_id=1, source_target_pairs={{0,2},{2,0},{1,3},{3,1},{4,6},{6,4},{5,7},{7,5},{8,10},{10,8},{9,1... | collective-permute-start | bytes 1376264 | tf_op jit(solution)/shard_map/ppermute | solution.py:45
  100.9 14.6 %all-to-all-start.3 = ((bf16[8,8,896]{2,1,0:T(8,128)(2,1)}), bf16[8,8,896]{2,1,0:T(8,128)(2,1)S(1)}, u32[]{:S(2)}, u32[]{:S(2)}) async-start(bf16[8,8,896]{2,1,0:T(8,128)(2,1)} %bitcast.66), calls=%async_computation.3 | async-start | bytes 229376 | tf_op jit(solution)/shard_map/all_to_all | solution.py:414
